TPU v7x, 256 devices: a whole 4x4x8 slice. The times are simulated.
256 devices in a mesh: row: 16 (over x, y), col: 8 (over z), depth: 2 (over core).
Axes of the slice: x: 4, y: 4, z: 8, core: 2. Of those that a mesh axis runs over, the one named last changes fastest.
Arguments:
- halves: bfloat16 [2, 8192, 16384], P(None, 'row', ('col', 'depth')), may hold values from -6 to 6
- spectrum: float32 [2, 16384], P(None, ('col', 'depth')), as said below
- wanted: int32 [4096], P('col'), may hold values from 0 to 32766, as said below
- fraction: float32 [4096], P('col'), may hold values from 0.05 to 0.95
Outputs:
- eigvec: float32 [2, 8192, 4096], P(None, 'row', ('col', 'depth'))
Inputs may be any that keep to these rules, and one draw needn't show every extreme that they name: Read in the order spectrum[0,0], spectrum[1,0], spectrum[0,1], spectrum[1,1], ... the values rise strictly, each by more than 0.05 over the one before. `wanted`: distinct positions in that merged order of the 32768 eigenvalues.
All inputs are finite; a program needn't handle non-finite values.
Results may differ from a plain program's by a relative error of at most 0.0029.
Values may be sent and summed in bfloat16 or wider, within the bound.
No kernel may reach another device: no remote copies, remote signals or barrier semaphores. Data moves between devices by JAX's collectives and lax.ppermute only.
A program may use at most 128 MiB of HBM per device.

v0:
```python
import functools

import jax
import jax.numpy as jnp
from jax import lax
from jax.experimental import pallas as pl
from jax.experimental.pallas import tpu as pltpu
from jax.sharding import Mesh
from jax.sharding import PartitionSpec as P


ROW = ("row_0", "row_1")
LANES = 128
PIECE = 64
F32 = jnp.float32
BF16 = jnp.bfloat16


def look_up(core, col, blocks_ref, low_ref, shift_ref, *, step, value_rows, columns):
    count = blocks_ref.shape[0]
    table = blocks_ref[:, :value_rows, :].reshape(count * value_rows, LANES)
    high = table.astype(BF16)
    rest = table - high.astype(F32)
    middle = rest.astype(BF16)
    small = (rest - middle.astype(F32)).astype(BF16)
    split = jnp.concatenate([high, middle, small], axis=1)
    per_block = value_rows * LANES
    half = per_block // 2

    roots = blocks_ref[2 * step, value_rows : value_rows + 8, :]
    swapped = jnp.concatenate([roots[2:4], roots[0:2], roots[6:8], roots[4:6]], axis=0)
    roots = jnp.where(core == 0, roots, swapped)
    wanted = roots[:4].astype(jnp.int32)
    rows = []
    for position in (wanted, wanted + 1):
        owner = lax.shift_right_logical(position, per_block.bit_length() - 1)
        ahead = lax.shift_right_logical(owner, 1) - col
        ahead = jnp.where(core == 0, ahead, -ahead) & (count // 2 - 1)
        order = ahead * 2 + ((owner & 1) ^ core)
        inside = position & (per_block - 1)
        index = (inside & 1) * half + lax.shift_right_logical(inside, 1)
        rows += [order * value_rows + lax.shift_right_logical(index, 7), index & (LANES - 1)]
    rows = jnp.concatenate([r.astype(F32) for r in rows] + [roots[4:], jnp.zeros((LANES - 20, LANES), F32)], axis=0)
    spots = jnp.transpose(rows)
    row_ids = lax.broadcasted_iota(jnp.int32, (LANES, count * value_rows), 1).astype(F32)
    lane_ids = lax.broadcasted_iota(jnp.int32, (LANES, LANES), 1).astype(F32)
    for tile in range(columns // LANES):
        picks = [jnp.where(row_ids == spots[:, k + tile : k + tile + 1], 1.0, 0.0).astype(BF16) for k in (0, 8)]
        got = jnp.dot(jnp.concatenate(picks, axis=0), split, preferred_element_type=F32)
        got = (got[:, :LANES] + got[:, LANES : 2 * LANES]) + got[:, 2 * LANES :]
        lower, upper = (
            jnp.sum(jnp.where(lane_ids == spots[:, k + tile : k + tile + 1], got[at : at + LANES], 0.0), axis=1, keepdims=True)
            for k, at in ((4, 0), (12, LANES))
        )
        shift = spots[:, 16 + tile : 17 + tile] * (upper - lower)
        at = slice(tile * LANES, (tile + 1) * LANES)
        low_ref[at, :] = jnp.broadcast_to(lower, (LANES, LANES))
        shift_ref[at, :] = jnp.broadcast_to(shift, (LANES, LANES))


def multiply(which_ref, where_ref, blocks_ref, own_ref, other_ref, *refs, step, sends, tall):
    out_ref, norm_ref = refs[0], refs[1] if len(refs) > 7 else None
    low_ref, shift_ref, block_ref, square_ref, halves_ref, sems = refs[-6:]
    unit = pl.program_id(0)
    units = halves_ref.shape[0]
    columns = low_ref.shape[0]
    rows, width = halves_ref.shape[2:]
    tiles = width // LANES
    value_rows = 2 * tiles
    half = which_ref[unit]
    last = jnp.where(half == 0, blocks_ref.shape[0] - 1, 0)

    def load(u, source):
        ref = (own_ref, other_ref)[source]
        return pltpu.make_async_copy(ref.at[which_ref[u]], halves_ref.at[u, source], sems.at[u, source])

    @pl.when(unit == 0)
    def _():
        for u in range(units):
            for source in range(2):
                load(u, source).start()
        look_up(
            where_ref[0], where_ref[1], blocks_ref, low_ref, shift_ref, step=step, value_rows=value_rows, columns=columns
        )

    values = [[blocks_ref[s, pl.ds(half * tiles + t, 1), :] for t in range(tiles)] for s in range(2)]
    seams = [[blocks_ref[last, value_rows + 8 + s * tiles + t, :][None] for t in range(tiles)] for s in range(2)]
    for part in range(columns // 256):
        for piece in range(256 // PIECE):
            start = part * 256 + piece * PIECE
            low = low_ref[start : start + PIECE, :]
            shift = shift_ref[start : start + PIECE, :]
            square = jnp.zeros((PIECE, LANES), F32)
            for source in range(2):
                for tile in range(tiles):
                    cauchy = seams[source][tile] / ((values[source][tile] - low) - shift)
                    square = square + cauchy * cauchy
                    block_ref[
                        start : start + PIECE, source * width + tile * LANES : source * width + (tile + 1) * LANES
                    ] = cauchy.astype(BF16)
            square_ref[start : start + PIECE, :] = square
        if part == 0:
            for source in range(2):
                load(unit, source).wait()
        at = slice(part * 256, (part + 1) * 256)
        nt = (((1,), (1,)), ((), ()))
        product = lax.dot_general(halves_ref[unit, 0], block_ref[at, :width], nt, preferred_element_type=F32)
        product = product + lax.dot_general(halves_ref[unit, 1], block_ref[at, width:], nt, preferred_element_type=F32)
        norm = jnp.sum(jnp.transpose(square_ref[at, :]), axis=0, keepdims=True)
        if sends:
            out_ref[:rows, at] = product.astype(BF16)
        else:
            out_ref[0, :, at] = product
        if tall:
            put_norm(out_ref, rows, at, norm)
        else:
            norm_ref[:, at] = jnp.where(unit == 0, 0.0, norm_ref[:, at]) + jnp.broadcast_to(norm, (8, 256))


def put_norm(out_ref, rows, at, norm):
    high = norm.astype(BF16).astype(F32)
    row = lax.broadcasted_iota(jnp.int32, (16, norm.shape[1]), 0)
    both = jnp.where(row == 0, high, jnp.where(row == 1, norm - high, 0.0))
    out_ref[rows : rows + 16, at] = both.astype(BF16)


def products(which, where, blocks, own, other, step, columns, sends=False, tall=False):
    n = which.shape[0]
    rows, width = own.shape[1:]
    if sends:
        height = rows + 16 if tall else rows
        out_shape = [jax.ShapeDtypeStruct((height, columns), BF16)]
        out_specs = [pl.BlockSpec((height, columns), lambda u, w: (0, 0))]
    else:
        out_shape = [jax.ShapeDtypeStruct((n, rows, columns), F32)]
        out_specs = [pl.BlockSpec((1, rows, columns), lambda u, w: (u, 0, 0))]
    if not tall:
        out_shape.append(jax.ShapeDtypeStruct((8, columns), F32))
        out_specs.append(pl.BlockSpec((8, columns), lambda u, w: (0, 0)))
    return pl.pallas_call(
        functools.partial(multiply, step=step, sends=sends, tall=tall),
        out_shape=out_shape,
        grid_spec=pltpu.PrefetchScalarGridSpec(
            num_scalar_prefetch=1,
            grid=(n,),
            in_specs=[
                pl.BlockSpec(memory_space=pltpu.SMEM),
                pl.BlockSpec(blocks.shape, lambda u, w: (0, 0, 0)),
                pl.BlockSpec(memory_space=pltpu.HBM),
                pl.BlockSpec(memory_space=pltpu.HBM),
            ],
            out_specs=out_specs,
            scratch_shapes=[
                pltpu.VMEM((columns, LANES), F32),
                pltpu.VMEM((columns, LANES), F32),
                pltpu.VMEM((columns, 2 * width), BF16),
                pltpu.VMEM((columns, LANES), F32),
                pltpu.VMEM((n, 2, rows, width), BF16),
                pltpu.SemaphoreType.DMA((n, 2)),
            ],
        ),
        compiler_params=pltpu.CompilerParams(vmem_limit_bytes=52 << 20),
        cost_estimate=pl.CostEstimate(
            flops=n * rows * columns * width * 4, bytes_accessed=n * 6 << 20, transcendentals=n * columns * width * 2
        ),
        name="products",
    )(which, where, blocks, own, other)


def add_on(got_ref, product_ref, norm_ref, *out_refs):
    rows = product_ref.shape[1]
    each = product_ref.shape[2] // len(out_refs)
    for i, out_ref in enumerate(out_refs):
        at = slice(i * each, (i + 1) * each)
        out_ref[:rows, :] = (got_ref[:rows, at].astype(F32) + product_ref[0, :, at]).astype(BF16)
        if out_ref.shape[0] > rows:
            norm = jnp.sum(got_ref[rows:, at].astype(F32), axis=0, keepdims=True) + norm_ref[:1, at]
            put_norm(out_ref, rows, slice(None), norm)


def added(got, product, norm, at, pieces):
    rows, columns = product.shape[1:]
    each = columns // pieces
    tall = got.shape[0]
    outs = [jax.ShapeDtypeStruct((tall, each), BF16)] * pieces
    return pl.pallas_call(
        add_on,
        out_shape=outs,
        grid=(1,),
        in_specs=[
            pl.BlockSpec((tall, columns), lambda i: (0, 0)),
            pl.BlockSpec((1, rows, columns), lambda i: (at, 0, 0)),
            pl.BlockSpec((8, columns), lambda i: (0, 0)),
        ],
        out_specs=[pl.BlockSpec((tall, each), lambda i: (0, 0))] * pieces,
        compiler_params=pltpu.CompilerParams(vmem_limit_bytes=8 << 20),
        cost_estimate=pl.CostEstimate(flops=rows * columns * 1000, bytes_accessed=2 << 20, transcendentals=0),
        name="add_on",
    )(got, product, norm)


def finish(which_ref, a_ref, b_ref, c_ref, d_ref, product_ref, norm_ref, out_ref):
    rows = product_ref.shape[1]
    squares = norm_ref[:1, :]
    for ref in (a_ref, c_ref):
        squares = squares + jnp.sum(ref[rows:, :].astype(F32), axis=0, keepdims=True)
    norm = jnp.sqrt(squares)
    for unit, (one, two) in enumerate(((a_ref, d_ref), (b_ref, c_ref))):

        @pl.when(pl.program_id(0) == unit)
        def _():
            total = product_ref[0] + one[:rows, :].astype(F32) + two[:rows, :].astype(F32)
            out_ref[0] = total / norm


def finished(which, first, second, first_across, second_across, product, norm):
    n, rows, columns = product.shape
    whole = [pl.BlockSpec(x.shape, lambda u, w: (0, 0)) for x in (first, second, first_across, second_across)]
    return pl.pallas_call(
        finish,
        out_shape=jax.ShapeDtypeStruct(product.shape, F32),
        grid_spec=pltpu.PrefetchScalarGridSpec(
            num_scalar_prefetch=1,
            grid=(n,),
            in_specs=whole
            + [pl.BlockSpec((1, rows, columns), lambda u, w: (w[u], 0, 0)), pl.BlockSpec(norm.shape, lambda u, w: (0, 0))],
            out_specs=pl.BlockSpec((1, rows, columns), lambda u, w: (w[u], 0, 0)),
        ),
        cost_estimate=pl.CostEstimate(flops=product.size * 100, bytes_accessed=4 << 20, transcendentals=0),
        compiler_params=pltpu.CompilerParams(vmem_limit_bytes=8 << 20),
        name="finish",
    )(which, first, second, first_across, second_across, product, norm)


def body(halves, spectrum, wanted, fraction):
    rows, _ = halves.shape[1:]
    ncols = lax.axis_size("col")
    ndepth = lax.axis_size("depth")
    nrows = lax.axis_size(ROW)
    core = lax.axis_index("depth").astype(jnp.int32)
    col = lax.axis_index("col").astype(jnp.int32)
    place = lax.axis_index(ROW)
    columns = wanted.shape[0]
    reach = ncols // 2

    def along(core, col, by):
        return (col + (by if core == 0 else -by)) % ncols

    pairs = []
    for r in range(nrows):
        for k in range(ncols):
            for c in range(ndepth):
                source = along(c, k, r // 2) * ndepth + (c ^ (r & 1))
                pairs.append((r * ncols * ndepth + source, r * ncols * ndepth + k * ndepth + c))
    theirs = [lax.ppermute(x, ROW + ("col", "depth"), pairs) for x in (spectrum, wanted, fraction)]
    other = lax.ppermute(halves, "depth", [(0, 1), (1, 0)])
    last = place == nrows - 1
    seam = [jnp.where(last, h[0, rows - 1], h[1, 0]) for h in (halves, other)]
    parcel = jnp.concatenate([x.astype(F32).reshape(-1, LANES) for x in theirs + seam], axis=0)
    blocks = lax.all_to_all(jnp.broadcast_to(parcel[None], (nrows,) + parcel.shape), ROW, 0, 0, tiled=True)

    straight = [(k * ndepth + c, along(c, k, 1) * ndepth + c) for k in range(ncols) for c in range(ndepth)]
    across = [(k * ndepth + c, along(c, k, 1) * ndepth + 1 - c) for k in range(ncols) for c in range(ndepth)]
    ring = ("col", "depth")
    where = jnp.stack([core, col])
    both = jnp.stack([1 - core, core])
    multiplied = functools.partial(products, where=where, blocks=blocks, own=halves, other=other)

    (a,) = multiplied(both[1:], step=reach, columns=columns, sends=True, tall=True)
    a = lax.ppermute(a, ring, straight)
    b, norm = multiplied(both[:1], step=reach - 1, columns=columns, sends=True)
    b = lax.ppermute(b, ring, straight)
    product, more = multiplied(both[1:], step=reach - 1, columns=columns)
    (a,) = added(a, product, norm + more, 0, 1)
    for step in range(reach - 2, 0, -1):
        a = lax.ppermute(a, ring, straight)
        product, norm = multiplied(both[:1], step=step, columns=columns)
        pieces = 1 if step > 1 else 2
        b, *b_across = added(b, product, norm, 0, pieces)
        b = lax.ppermute(b, ring, straight)
        b_across = [lax.ppermute(x, ring, across) for x in b_across]
        product, more = multiplied(both[1:], step=step, columns=columns)
        a, *a_across = added(a, product, norm + more, 0, pieces)
    a = lax.ppermute(a, ring, straight)
    a_across = [lax.ppermute(x, ring, across) for x in a_across]
    product, norm = multiplied(jnp.arange(2, dtype=jnp.int32), step=0, columns=columns // ndepth)
    return finished(both[::-1], a, b, a_across[0], b_across[0], product, norm)


def solution(mesh):
    split = Mesh(
        mesh.devices.reshape(4, 4, mesh.shape["col"], mesh.shape["depth"]), ("row_0", "row_1", "col", "depth")
    )
    in_specs = (P(None, ROW, ("col", "depth")), P(None, ("col", "depth")), P("col"), P("col"))
    out_specs = P(None, ROW, ("col", "depth"))
    return jax.shard_map(body, mesh=split, in_specs=in_specs, out_specs=out_specs, check_vma=False)
```

profile of v0, /device:TPU:1, one launch (start us, length us, event | category | flops | bytes accessed | tf_op | source)
XLA Modules:
  0.0 95.0 jit_solution(4411626705464697615)
XLA Ops:
  0.0 3.2 %collective-permute-start.3 = (bf16[2,512,1024]{2,1,0:T(8,128)(2,1)}, bf16[2,512,1024]{2,1,0:T(8,128)(2,1)S(1)}, u32[]{:S(2)}, u32[]{:S(2)}) collective-permute-start(bf16[2,512,1024]{2,1,0:T(8,128)(2,1)} %own_ref.15), channel_id=1, source_target_pairs={{0,1},{1,0},{2,3},{3,2},{4,5},{5,4},{6,7},{7,6},{8,9},{9,8},{10,11... | collective-permute-start | bytes 6291464 | tf_op jit(solution)/shard_map/ppermute | solution.py:256
  3.2 1.3 %collective-permute-start = (f32[2,1024]{1,0:T(2,128)}, f32[2,1024]{1,0:T(2,128)S(1)}, u32[]{:S(2)}, u32[]{:S(2)}) collective-permute-start(f32[2,1024]{1,0:T(2,128)} %param.5), channel_id=1, source_target_pairs={{0,0},{1,1},{2,2},{3,3},{4,4},{5,5},{6,6},{7,7},{8,8},{9,9},{10,10... | collective-permute-start | bytes 24584 | tf_op jit(solution)/shard_map/ppermute | solution.py:255
  4.5 1.3 %collective-permute-start.1 = (s32[512]{0:T(512)}, s32[512]{0:T(512)S(1)}, u32[]{:S(2)}, u32[]{:S(2)}) collective-permute-start(s32[512]{0:T(512)} %param.6), channel_id=1, source_target_pairs={{0,0},{1,1},{2,2},{3,3},{4,4},{5,5},{6,6},{7,7},{8,8},{9,9},{10,10... | collective-permute-start | bytes 6152 | tf_op jit(solution)/shard_map/ppermute | solution.py:255
  5.9 1.3 %collective-permute-start.2 = (f32[512]{0:T(512)}, f32[512]{0:T(512)S(1)}, u32[]{:S(2)}, u32[]{:S(2)}) collective-permute-start(f32[512]{0:T(512)} %param.7), channel_id=1, source_target_pairs={{0,0},{1,1},{2,2},{3,3},{4,4},{5,5},{6,6},{7,7},{8,8},{9,9},{10,10... | collective-permute-start | bytes 6152 | tf_op jit(solution)/shard_map/ppermute | solution.py:255
  7.2 0.7 fusion
  7.9 0.0 collective-permute-done.1
  8.0 0.0 collective-permute-done
  8.0 0.0 collective-permute-done.3.other_ref
  8.0 0.0 collective-permute-done.2
  8.1 0.9 broadcast_in_dim.2
  8.9 18.2 %all-to-all-start = ((f32[16,40,128]{2,1,0:T(8,128)}), f32[16,40,128]{2,1,0:T(8,128)S(1)}, u32[]{:S(2)}, u32[]{:S(2)}) async-start(f32[16,40,128]{2,1,0:T(8,128)} %broadcast_in_dim.2), calls=%async_computation | async-start | bytes 655360 | tf_op jit(solution)/shard_map/all_to_all | solution.py:260
  27.2 0.1 pad_add_fusion.1.where_ref
  27.3 7.6 %all-to-all-done.blocks_ref = f32[16,40,128]{2,1,0:T(8,128)S(1)} async-done(((f32[16,40,128]{2,1,0:T(8,128)}), f32[16,40,128]{2,1,0:T(8,128)S(1)}, u32[]{:S(2)}, u32[]{:S(2)}) %all-to-all-start) | async-done | bytes 327712 | tf_op jit(solution)/shard_map/all_to_all | solution.py:260
  34.9 0.0 copy-done
  34.9 3.6 %products.8 = bf16[528,512]{1,0:T(8,128)(2,1)S(1)} custom-call(s32[1]{0:T(128)} %bitcast.1.which_ref, s32[2]{0:T(128)S(1)} %pad_add_fusion.1.where_ref, f32[16,40,128]{2,1,0:T(8,128)S(1)} %all-to-all-done.blocks_ref, bf16[2,512,1024]{2,1,0:T(8,128)(2,1)} %own_ref.15, bf16[2,512,1024]{2,1,0:T(8,128)(2,1)} %copy-done), custom_call_target="tpu_custom_call" | custom-call | flops 1073741824 | bytes 6291456 | tf_op jit(solution)/shard_map/products/pallas_call | solution.py:140
  38.5 5.0 %collective-permute-start.4 = (bf16[528,512]{1,0:T(8,128)(2,1)S(1)}, bf16[528,512]{1,0:T(8,128)(2,1)S(1)}, u32[]{:S(2)}, u32[]{:S(2)}) collective-permute-start(bf16[528,512]{1,0:T(8,128)(2,1)S(1)} %products.8), channel_id=1, source_target_pairs={{0,2},{1,15},{2,4},{3,1},{4,6},{5,3},{6,8},{7,5},{8,10},{9,7},{10,... | collective-permute-start | bytes 1622024 | tf_op jit(solution)/shard_map/ppermute | solution.py:270
  43.5 3.6 %products.9 = (f32[1,512,512]{2,1,0:T(8,128)S(1)}, f32[8,512]{1,0:T(8,128)S(1)}) custom-call(s32[1]{0:T(128)} %bitcast.1.which_ref, s32[2]{0:T(128)S(1)} %pad_add_fusion.1.where_ref, f32[16,40,128]{2,1,0:T(8,128)S(1)} %all-to-all-done.blocks_ref, bf16[2,512,1024]{2,1,0:T(8,128)(2,1)} %own_ref.15, bf16[2,512,1024]{2,1,0:T(8,128)(2,1)} %copy-done), custom_call_target="tpu_custom_call" | custom-call | flops 1073741824 | bytes 6291456 | tf_op jit(solution)/shard_map/products/pallas_call | solution.py:140
  47.1 3.6 %products.10 = (bf16[512,512]{1,0:T(8,128)(2,1)S(1)}, f32[8,512]{1,0:T(8,128)S(1)}) custom-call(s32[1]{0:T(128)} %bitcast.which_ref, s32[2]{0:T(128)S(1)} %pad_add_fusion.1.where_ref, f32[16,40,128]{2,1,0:T(8,128)S(1)} %all-to-all-done.blocks_ref, bf16[2,512,1024]{2,1,0:T(8,128)(2,1)} %own_ref.15, bf16[2,512,1024]{2,1,0:T(8,128)(2,1)} %copy-done), custom_call_target="tpu_custom_call" | custom-call | flops 1073741824 | bytes 6291456 | tf_op jit(solution)/shard_map/products/pallas_call | solution.py:140
  50.7 0.0 collective-permute-done.4.got_ref
  50.8 0.1 add_on.5
  50.9 2.2 %collective-permute-start.5 = (bf16[528,512]{1,0:T(8,128)(2,1)S(1)}, bf16[528,512]{1,0:T(8,128)(2,1)S(1)}, u32[]{:S(2)}, u32[]{:S(2)}) collective-permute-start(bf16[528,512]{1,0:T(8,128)(2,1)S(1)} %add_on.5), channel_id=1, source_target_pairs={{0,2},{1,15},{2,4},{3,1},{4,6},{5,3},{6,8},{7,5},{8,10},{9,7},{10,... | collective-permute-start | bytes 1622024 | tf_op jit(solution)/shard_map/ppermute | solution.py:276
  53.1 0.3 collective-permute-start.8
  53.4 3.6 %products.11 = (f32[1,512,512]{2,1,0:T(8,128)S(1)}, f32[8,512]{1,0:T(8,128)S(1)}) custom-call(s32[1]{0:T(128)} %bitcast.1.which_ref, s32[2]{0:T(128)S(1)} %pad_add_fusion.1.where_ref, f32[16,40,128]{2,1,0:T(8,128)S(1)} %all-to-all-done.blocks_ref, bf16[2,512,1024]{2,1,0:T(8,128)(2,1)} %own_ref.15, bf16[2,512,1024]{2,1,0:T(8,128)(2,1)} %copy-done), custom_call_target="tpu_custom_call" | custom-call | flops 1073741824 | bytes 6291456 | tf_op jit(solution)/shard_map/products/pallas_call | solution.py:140
  57.0 3.6 %products.12 = (f32[1,512,512]{2,1,0:T(8,128)S(1)}, f32[8,512]{1,0:T(8,128)S(1)}) custom-call(s32[1]{0:T(128)} %bitcast.which_ref, s32[2]{0:T(128)S(1)} %pad_add_fusion.1.where_ref, f32[16,40,128]{2,1,0:T(8,128)S(1)} %all-to-all-done.blocks_ref, bf16[2,512,1024]{2,1,0:T(8,128)(2,1)} %own_ref.15, bf16[2,512,1024]{2,1,0:T(8,128)(2,1)} %copy-done), custom_call_target="tpu_custom_call" | custom-call | flops 1073741824 | bytes 6291456 | tf_op jit(solution)/shard_map/products/pallas_call | solution.py:140
  60.6 0.0 collective-permute-done.5.got_ref
  60.7 0.1 add_on.6
  60.8 2.0 %collective-permute-start.6 = (bf16[528,512]{1,0:T(8,128)(2,1)S(1)}, bf16[528,512]{1,0:T(8,128)(2,1)S(1)}, u32[]{:S(2)}, u32[]{:S(2)}) collective-permute-start(bf16[528,512]{1,0:T(8,128)(2,1)S(1)} %add_on.6), channel_id=1, source_target_pairs={{0,2},{1,15},{2,4},{3,1},{4,6},{5,3},{6,8},{7,5},{8,10},{9,7},{10,... | collective-permute-start | bytes 1622024 | tf_op jit(solution)/shard_map/ppermute | solution.py:276
  62.7 2.4 %collective-permute-done.8.got_ref = bf16[512,512]{1,0:T(8,128)(2,1)S(1)} collective-permute-done((bf16[512,512]{1,0:T(8,128)(2,1)S(1)}, bf16[512,512]{1,0:T(8,128)(2,1)S(1)}, u32[]{:S(2)}, u32[]{:S(2)}) %collective-permute-start.8) | collective-permute-done | bytes 524320 | tf_op jit(solution)/shard_map/ppermute | solution.py:272
  65.1 0.1 add_on.8
  65.2 3.1 %collective-permute-start.9 = (bf16[512,512]{1,0:T(8,128)(2,1)S(1)}, bf16[512,512]{1,0:T(8,128)(2,1)S(1)}, u32[]{:S(2)}, u32[]{:S(2)}) collective-permute-start(bf16[512,512]{1,0:T(8,128)(2,1)S(1)} %add_on.8), channel_id=1, source_target_pairs={{0,2},{1,15},{2,4},{3,1},{4,6},{5,3},{6,8},{7,5},{8,10},{9,7},{10,... | collective-permute-start | bytes 1572872 | tf_op jit(solution)/shard_map/ppermute | solution.py:280
  68.3 3.6 %products.13 = (f32[1,512,512]{2,1,0:T(8,128)S(1)}, f32[8,512]{1,0:T(8,128)S(1)}) custom-call(s32[1]{0:T(128)} %bitcast.1.which_ref, s32[2]{0:T(128)S(1)} %pad_add_fusion.1.where_ref, f32[16,40,128]{2,1,0:T(8,128)S(1)} %all-to-all-done.blocks_ref, bf16[2,512,1024]{2,1,0:T(8,128)(2,1)} %own_ref.15, bf16[2,512,1024]{2,1,0:T(8,128)(2,1)} %copy-done), custom_call_target="tpu_custom_call" | custom-call | flops 1073741824 | bytes 6291456 | tf_op jit(solution)/shard_map/products/pallas_call | solution.py:140
  72.0 3.6 %products.14 = (f32[1,512,512]{2,1,0:T(8,128)S(1)}, f32[8,512]{1,0:T(8,128)S(1)}) custom-call(s32[1]{0:T(128)} %bitcast.which_ref, s32[2]{0:T(128)S(1)} %pad_add_fusion.1.where_ref, f32[16,40,128]{2,1,0:T(8,128)S(1)} %all-to-all-done.blocks_ref, bf16[2,512,1024]{2,1,0:T(8,128)(2,1)} %own_ref.15, bf16[2,512,1024]{2,1,0:T(8,128)(2,1)} %copy-done), custom_call_target="tpu_custom_call" | custom-call | flops 1073741824 | bytes 6291456 | tf_op jit(solution)/shard_map/products/pallas_call | solution.py:140
  75.6 0.0 collective-permute-done.6.got_ref
  75.6 0.1 add_on.7
  75.7 0.3 collective-permute-start.7
  76.0 4.7 %collective-permute-start.11 = (bf16[528,256]{1,0:T(8,128)(2,1)S(1)}, bf16[528,256]{1,0:T(8,128)(2,1)S(1)}, u32[]{:S(2)}, u32[]{:S(2)}) collective-permute-start(bf16[528,256]{1,0:T(8,128)(2,1)S(1)} %get-tuple-element.37), channel_id=1, source_target_pairs={{0,3},{1,14},{2,5},{3,0},{4,7},{5,2},{6,9},{7,4},{8,11},{9,6},{10,... | collective-permute-start | bytes 811016 | tf_op jit(solution)/shard_map/ppermute | solution.py:285
  80.8 0.0 collective-permute-done.9.got_ref
  80.8 0.1 add_on.9
  80.9 1.7 %collective-permute-start.10 = (bf16[512,256]{1,0:T(8,128)(2,1)S(1)}, bf16[512,256]{1,0:T(8,128)(2,1)S(1)}, u32[]{:S(2)}, u32[]{:S(2)}) collective-permute-start(bf16[512,256]{1,0:T(8,128)(2,1)S(1)} %get-tuple-element.36), channel_id=1, source_target_pairs={{0,2},{1,15},{2,4},{3,1},{4,6},{5,3},{6,8},{7,5},{8,10},{9,7},{10,... | collective-permute-start | bytes 786440 | tf_op jit(solution)/shard_map/ppermute | solution.py:280
  82.6 1.8 %collective-permute-start.12 = (bf16[512,256]{1,0:T(8,128)(2,1)S(1)}, bf16[512,256]{1,0:T(8,128)(2,1)S(1)}, u32[]{:S(2)}, u32[]{:S(2)}) collective-permute-start(bf16[512,256]{1,0:T(8,128)(2,1)S(1)} %get-tuple-element.38), channel_id=1, source_target_pairs={{0,3},{1,14},{2,5},{3,0},{4,7},{5,2},{6,9},{7,4},{8,11},{9,6},{10,... | collective-permute-start | bytes 786440 | tf_op jit(solution)/shard_map/ppermute | solution.py:281
  84.4 0.1 pad_add_fusion
  84.5 0.1 rev.3.which_ref
  84.6 4.7 %products.15 = (f32[2,512,256]{2,1,0:T(8,128)S(1)}, f32[8,256]{1,0:T(8,128)S(1)}) custom-call(s32[2]{0:T(128)S(1)} %iota.3.which_ref, s32[2]{0:T(128)S(1)} %pad_add_fusion.1.where_ref, f32[16,40,128]{2,1,0:T(8,128)S(1)} %all-to-all-done.blocks_ref, bf16[2,512,1024]{2,1,0:T(8,128)(2,1)} %own_ref.15, bf16[2,512,1024]{2,1,0:T(8,128)(2,1)} %copy-done), custom_call_target="tpu_custom_call" | custom-call | flops 1073741824 | bytes 12582912 | tf_op jit(solution)/shard_map/products/pallas_call | solution.py:140
  89.3 0.0 collective-permute-done.10.b_ref
  89.3 4.0 %collective-permute-done.12.d_ref = bf16[512,256]{1,0:T(8,128)(2,1)S(1)} collective-permute-done((bf16[512,256]{1,0:T(8,128)(2,1)S(1)}, bf16[512,256]{1,0:T(8,128)(2,1)S(1)}, u32[]{:S(2)}, u32[]{:S(2)}) %collective-permute-start.12) | collective-permute-done | bytes 262176 | tf_op jit(solution)/shard_map/ppermute | solution.py:281
  93.3 0.0 collective-permute-done.7.a_ref
  93.3 0.0 collective-permute-done.11.c_ref
  93.3 1.7 %finish.1 = f32[2,512,256]{2,1,0:T(8,128)} custom-call(s32[2]{0:T(128)S(1)} %rev.3.which_ref, bf16[528,256]{1,0:T(8,128)(2,1)S(1)} %collective-permute-done.7.a_ref, bf16[512,256]{1,0:T(8,128)(2,1)S(1)} %collective-permute-done.10.b_ref, bf16[528,256]{1,0:T(8,128)(2,1)S(1)} %collective-permute-done.11.c_ref, ...), custom_call_target="tpu_custom_call" | custom-call | flops 26214400 | bytes 4194304 | tf_op jit(solution)/shard_map/finish/pallas_call | solution.py:219
  (9 shorter events, 0.1 us)
Async XLA Ops:
  0.0 8.0 %collective-permute-start.3 = (bf16[2,512,1024]{2,1,0:T(8,128)(2,1)}, bf16[2,512,1024]{2,1,0:T(8,128)(2,1)S(1)}, u32[]{:S(2)}, u32[]{:S(2)}) collective-permute-start(bf16[2,512,1024]{2,1,0:T(8,128)(2,1)} %own_ref.15), channel_id=1, source_target_pairs={{0,1},{1,0},{2,3},{3,2},{4,5},{5,4},{6,7},{7,6},{8,9},{9,8},{10,11... | collective-permute-start | bytes 6291464 | tf_op jit(solution)/shard_map/ppermute | solution.py:256
  3.2 4.8 %collective-permute-start = (f32[2,1024]{1,0:T(2,128)}, f32[2,1024]{1,0:T(2,128)S(1)}, u32[]{:S(2)}, u32[]{:S(2)}) collective-permute-start(f32[2,1024]{1,0:T(2,128)} %param.5), channel_id=1, source_target_pairs={{0,0},{1,1},{2,2},{3,3},{4,4},{5,5},{6,6},{7,7},{8,8},{9,9},{10,10... | collective-permute-start | bytes 24584 | tf_op jit(solution)/shard_map/ppermute | solution.py:255
  4.5 3.4 %collective-permute-start.1 = (s32[512]{0:T(512)}, s32[512]{0:T(512)S(1)}, u32[]{:S(2)}, u32[]{:S(2)}) collective-permute-start(s32[512]{0:T(512)} %param.6), channel_id=1, source_target_pairs={{0,0},{1,1},{2,2},{3,3},{4,4},{5,5},{6,6},{7,7},{8,8},{9,9},{10,10... | collective-permute-start | bytes 6152 | tf_op jit(solution)/shard_map/ppermute | solution.py:255
  5.9 2.2 %collective-permute-start.2 = (f32[512]{0:T(512)}, f32[512]{0:T(512)S(1)}, u32[]{:S(2)}, u32[]{:S(2)}) collective-permute-start(f32[512]{0:T(512)} %param.7), channel_id=1, source_target_pairs={{0,0},{1,1},{2,2},{3,3},{4,4},{5,5},{6,6},{7,7},{8,8},{9,9},{10,10... | collective-permute-start | bytes 6152 | tf_op jit(solution)/shard_map/ppermute | solution.py:255
  8.0 26.9 %copy-start = (bf16[2,512,1024]{2,1,0:T(8,128)(2,1)}, bf16[2,512,1024]{2,1,0:T(8,128)(2,1)S(1)}, u32[]{:S(2)}) copy-start(bf16[2,512,1024]{2,1,0:T(8,128)(2,1)S(1)} %collective-permute-done.3.other_ref) | copy-start | bytes 6291460
  8.9 25.9 %all-to-all-start = ((f32[16,40,128]{2,1,0:T(8,128)}), f32[16,40,128]{2,1,0:T(8,128)S(1)}, u32[]{:S(2)}, u32[]{:S(2)}) async-start(f32[16,40,128]{2,1,0:T(8,128)} %broadcast_in_dim.2), calls=%async_computation | async-start | bytes 655360 | tf_op jit(solution)/shard_map/all_to_all | solution.py:260
  38.5 12.3 %collective-permute-start.4 = (bf16[528,512]{1,0:T(8,128)(2,1)S(1)}, bf16[528,512]{1,0:T(8,128)(2,1)S(1)}, u32[]{:S(2)}, u32[]{:S(2)}) collective-permute-start(bf16[528,512]{1,0:T(8,128)(2,1)S(1)} %products.8), channel_id=1, source_target_pairs={{0,2},{1,15},{2,4},{3,1},{4,6},{5,3},{6,8},{7,5},{8,10},{9,7},{10,... | collective-permute-start | bytes 1622024 | tf_op jit(solution)/shard_map/ppermute | solution.py:270
  50.9 9.7 %collective-permute-start.5 = (bf16[528,512]{1,0:T(8,128)(2,1)S(1)}, bf16[528,512]{1,0:T(8,128)(2,1)S(1)}, u32[]{:S(2)}, u32[]{:S(2)}) collective-permute-start(bf16[528,512]{1,0:T(8,128)(2,1)S(1)} %add_on.5), channel_id=1, source_target_pairs={{0,2},{1,15},{2,4},{3,1},{4,6},{5,3},{6,8},{7,5},{8,10},{9,7},{10,... | collective-permute-start | bytes 1622024 | tf_op jit(solution)/shard_map/ppermute | solution.py:276
  53.1 12.0 %collective-permute-start.8 = (bf16[512,512]{1,0:T(8,128)(2,1)S(1)}, bf16[512,512]{1,0:T(8,128)(2,1)S(1)}, u32[]{:S(2)}, u32[]{:S(2)}) collective-permute-start(bf16[512,512]{1,0:T(8,128)(2,1)S(1)} %get-tuple-element.33), channel_id=1, source_target_pairs={{0,2},{1,15},{2,4},{3,1},{4,6},{5,3},{6,8},{7,5},{8,10},{9,7},{10,... | collective-permute-start | bytes 1572872 | tf_op jit(solution)/shard_map/ppermute | solution.py:272
  60.8 14.8 %collective-permute-start.6 = (bf16[528,512]{1,0:T(8,128)(2,1)S(1)}, bf16[528,512]{1,0:T(8,128)(2,1)S(1)}, u32[]{:S(2)}, u32[]{:S(2)}) collective-permute-start(bf16[528,512]{1,0:T(8,128)(2,1)S(1)} %add_on.6), channel_id=1, source_target_pairs={{0,2},{1,15},{2,4},{3,1},{4,6},{5,3},{6,8},{7,5},{8,10},{9,7},{10,... | collective-permute-start | bytes 1622024 | tf_op jit(solution)/shard_map/ppermute | solution.py:276
  65.2 15.6 %collective-permute-start.9 = (bf16[512,512]{1,0:T(8,128)(2,1)S(1)}, bf16[512,512]{1,0:T(8,128)(2,1)S(1)}, u32[]{:S(2)}, u32[]{:S(2)}) collective-permute-start(bf16[512,512]{1,0:T(8,128)(2,1)S(1)} %add_on.8), channel_id=1, source_target_pairs={{0,2},{1,15},{2,4},{3,1},{4,6},{5,3},{6,8},{7,5},{8,10},{9,7},{10,... | collective-permute-start | bytes 1572872 | tf_op jit(solution)/shard_map/ppermute | solution.py:280
  75.7 17.6 %collective-permute-start.7 = (bf16[528,256]{1,0:T(8,128)(2,1)S(1)}, bf16[528,256]{1,0:T(8,128)(2,1)S(1)}, u32[]{:S(2)}, u32[]{:S(2)}) collective-permute-start(bf16[528,256]{1,0:T(8,128)(2,1)S(1)} %get-tuple-element.32), channel_id=1, source_target_pairs={{0,2},{1,15},{2,4},{3,1},{4,6},{5,3},{6,8},{7,5},{8,10},{9,7},{10,... | collective-permute-start | bytes 811016 | tf_op jit(solution)/shard_map/ppermute | solution.py:284
  76.0 17.3 %collective-permute-start.11 = (bf16[528,256]{1,0:T(8,128)(2,1)S(1)}, bf16[528,256]{1,0:T(8,128)(2,1)S(1)}, u32[]{:S(2)}, u32[]{:S(2)}) collective-permute-start(bf16[528,256]{1,0:T(8,128)(2,1)S(1)} %get-tuple-element.37), channel_id=1, source_target_pairs={{0,3},{1,14},{2,5},{3,0},{4,7},{5,2},{6,9},{7,4},{8,11},{9,6},{10,... | collective-permute-start | bytes 811016 | tf_op jit(solution)/shard_map/ppermute | solution.py:285
  80.9 8.4 %collective-permute-start.10 = (bf16[512,256]{1,0:T(8,128)(2,1)S(1)}, bf16[512,256]{1,0:T(8,128)(2,1)S(1)}, u32[]{:S(2)}, u32[]{:S(2)}) collective-permute-start(bf16[512,256]{1,0:T(8,128)(2,1)S(1)} %get-tuple-element.36), channel_id=1, source_target_pairs={{0,2},{1,15},{2,4},{3,1},{4,6},{5,3},{6,8},{7,5},{8,10},{9,7},{10,... | collective-permute-start | bytes 786440 | tf_op jit(solution)/shard_map/ppermute | solution.py:280
  82.6 10.7 %collective-permute-start.12 = (bf16[512,256]{1,0:T(8,128)(2,1)S(1)}, bf16[512,256]{1,0:T(8,128)(2,1)S(1)}, u32[]{:S(2)}, u32[]{:S(2)}) collective-permute-start(bf16[512,256]{1,0:T(8,128)(2,1)S(1)} %get-tuple-element.38), channel_id=1, source_target_pairs={{0,3},{1,14},{2,5},{3,0},{4,7},{5,2},{6,9},{7,4},{8,11},{9,6},{10,... | collective-permute-start | bytes 786440 | tf_op jit(solution)/shard_map/ppermute | solution.py:281
where the time goes:
time: 95.4 us; the launch traced here: 95 us
  starting transfers between devices  46.7 us (49%)
  Pallas kernels  32.1 us (34%)
  waiting for transfers between devices  14 us (15%)
  local copies, waits for them, and re-layouts  0.99 us (1%)
    pallas_call x8, Pallas kernels, products(): pl.pallas_call(functools.partial(multiply, step=step, sends=sends, tall=t...  29.9 us
    all_to_all x1, starting transfers between devices, body(): lax.all_to_all(jnp.broadcast_to(parcel[None], (nrows,) + parcel.shape), R...  18.2 us
    ppermute x4, starting transfers between devices, body(): a = lax.ppermute(a, ring, straight)  9.54 us
    all_to_all x1, waiting for transfers between devices, body(): lax.all_to_all(jnp.broadcast_to(parcel[None], (nrows,) + parcel.shape), R...  7.61 us
    ppermute x3, starting transfers between devices, body(): b = lax.ppermute(b, ring, straight)  5.14 us
    ppermute x1, starting transfers between devices, body(): a_across = [lax.ppermute(x, ring, across) for x in a_across]  4.74 us
    ppermute x1, waiting for transfers between devices, body(): b_across = [lax.ppermute(x, ring, across) for x in b_across]  4.04 us
    ppermute x3, starting transfers between devices, body(): lax.ppermute(x, ROW + ('col', 'depth'), pairs)  4 us
  transfers between devices with their start and end apart: 14, of which 3 were waited for; matrix products, arithmetic and copies ran while one was open for 1% of the time, Pallas kernels for 28%

commit v1 on v0

v1 whole, which is shorter than its diff:
```python
import functools

import jax
import jax.numpy as jnp
from jax import lax
from jax.experimental import pallas as pl
from jax.experimental.pallas import tpu as pltpu
from jax.sharding import Mesh
from jax.sharding import PartitionSpec as P


ROW = ("row_0", "row_1")
LANES = 128
PIECE = 64
F32 = jnp.float32
BF16 = jnp.bfloat16


def heading(step):
    core = lax.axis_index("depth").astype(jnp.int32)
    col = lax.axis_index("col").astype(jnp.int32)
    ncols = lax.axis_size("col")
    target = lax.rem(col + jnp.where(core == 0, step, ncols - step), ncols)
    return core, col, target


def look_up(core, target, blocks_ref, low_ref, shift_ref, *, value_rows, first, count):
    places = blocks_ref.shape[0]
    table = blocks_ref[:, :value_rows, :].reshape(places * value_rows, LANES)
    high = table.astype(BF16)
    rest = table - high.astype(F32)
    middle = rest.astype(BF16)
    small = (rest - middle.astype(F32)).astype(BF16)
    split = jnp.concatenate([high, middle, small], axis=1)
    per_block = value_rows * LANES
    half = per_block // 2

    roots = blocks_ref[2 * target, value_rows : value_rows + 8, :]
    swapped = jnp.concatenate([roots[2:4], roots[0:2], roots[6:8], roots[4:6]], axis=0)
    roots = jnp.where(core == 0, roots, swapped)
    wanted = roots[:4].astype(jnp.int32)
    rows = []
    for position in (wanted, wanted + 1):
        owner = lax.shift_right_logical(position, per_block.bit_length() - 1)
        inside = position & (per_block - 1)
        index = (inside & 1) * half + lax.shift_right_logical(inside, 1)
        rows += [owner * value_rows + lax.shift_right_logical(index, 7), index & (LANES - 1)]
    rows = jnp.concatenate([r.astype(F32) for r in rows] + [roots[4:], jnp.zeros((LANES - 20, LANES), F32)], axis=0)
    spots = jnp.transpose(rows)
    row_ids = lax.broadcasted_iota(jnp.int32, (LANES, places * value_rows), 1).astype(F32)
    lane_ids = lax.broadcasted_iota(jnp.int32, (LANES, LANES), 1).astype(F32)
    for tile in range(first, first + count):
        picks = [jnp.where(row_ids == spots[:, k + tile : k + tile + 1], 1.0, 0.0).astype(BF16) for k in (0, 8)]
        got = jnp.dot(jnp.concatenate(picks, axis=0), split, preferred_element_type=F32)
        got = (got[:, :LANES] + got[:, LANES : 2 * LANES]) + got[:, 2 * LANES :]
        lower, upper = (
            jnp.sum(jnp.where(lane_ids == spots[:, k + tile : k + tile + 1], got[at : at + LANES], 0.0), axis=1, keepdims=True)
            for k, at in ((4, 0), (12, LANES))
        )
        shift = spots[:, 16 + tile : 17 + tile] * (upper - lower)
        at = slice((tile - first) * LANES, (tile - first + 1) * LANES)
        low_ref[at, :] = jnp.broadcast_to(lower, (LANES, LANES))
        shift_ref[at, :] = jnp.broadcast_to(shift, (LANES, LANES))


def multiply(blocks_ref, seam_ref, own_ref, other_ref, *refs, step, which, first, sends, tall):
    out_ref, norm_ref = refs[0], None if tall else refs[1]
    low_ref, shift_ref, block_ref, square_ref, halves_ref, sems = refs[-6:]
    columns = low_ref.shape[0]
    rows, width = halves_ref.shape[2:]
    tiles = width // LANES
    value_rows = 2 * tiles
    core, col, target = heading(step)
    halves = [core if w == "first" else 1 - core if w == "second" else w for w in which]
    loads = [
        [
            pltpu.make_async_copy(ref.at[half], halves_ref.at[u, source], sems.at[u, source])
            for source, ref in enumerate((own_ref, other_ref))
        ]
        for u, half in enumerate(halves)
    ]
    for pair in loads:
        for load in pair:
            load.start()
    look_up(core, target, blocks_ref, low_ref, shift_ref, value_rows=value_rows, first=first, count=columns // LANES)
    here = [2 * col + core, 2 * col + 1 - core]
    for u, half in enumerate(halves):
        values = [[blocks_ref[s, pl.ds(half * tiles + t, 1), :] for t in range(tiles)] for s in here]
        rows_of = seam_ref[jnp.where(half == 0, seam_ref.shape[0] - 1, 0)].astype(F32)
        seams = [[rows_of[s * tiles + t : s * tiles + t + 1] for t in range(tiles)] for s in range(2)]
        for part in range(columns // 256):
            for piece in range(256 // PIECE):
                start = part * 256 + piece * PIECE
                low = low_ref[start : start + PIECE, :]
                shift = shift_ref[start : start + PIECE, :]
                square = jnp.zeros((PIECE, LANES), F32)
                for source in range(2):
                    for tile in range(tiles):
                        cauchy = seams[source][tile] / ((values[source][tile] - low) - shift)
                        square = square + cauchy * cauchy
                        block_ref[
                            start : start + PIECE, source * width + tile * LANES : source * width + (tile + 1) * LANES
                        ] = cauchy.astype(BF16)
                square_ref[start : start + PIECE, :] = square
            if part == 0:
                for load in loads[u]:
                    load.wait()
            at = slice(part * 256, (part + 1) * 256)
            nt = (((1,), (1,)), ((), ()))
            product = lax.dot_general(halves_ref[u, 0], block_ref[at, :width], nt, preferred_element_type=F32)
            product = product + lax.dot_general(halves_ref[u, 1], block_ref[at, width:], nt, preferred_element_type=F32)
            norm = jnp.sum(jnp.transpose(square_ref[at, :]), axis=0, keepdims=True)
            if sends:
                out_ref[:rows, at] = product.astype(BF16)
            else:
                out_ref[u, :, at] = product
            if tall:
                put_norm(out_ref, rows, at, norm)
            elif u == 0:
                norm_ref[:, at] = jnp.broadcast_to(norm, (8, 256))
            else:
                norm_ref[:, at] += jnp.broadcast_to(norm, (8, 256))


def put_norm(out_ref, rows, at, norm):
    high = norm.astype(BF16).astype(F32)
    row = lax.broadcasted_iota(jnp.int32, (16, norm.shape[1]), 0)
    both = jnp.where(row == 0, high, jnp.where(row == 1, norm - high, 0.0))
    out_ref[rows : rows + 16, at] = both.astype(BF16)


VMEM = pl.BlockSpec(memory_space=pltpu.VMEM)
HBM = pl.BlockSpec(memory_space=pl.ANY)


def products(which, blocks, seam, own, other, step, columns, first=0, sends=False, tall=False):
    n = len(which)
    rows, width = own.shape[1:]
    if sends:
        out_shape = [jax.ShapeDtypeStruct((rows + 16 if tall else rows, columns), BF16)]
    else:
        out_shape = [jax.ShapeDtypeStruct((n, rows, columns), F32)]
    if not tall:
        out_shape.append(jax.ShapeDtypeStruct((8, columns), F32))
    return pl.pallas_call(
        functools.partial(multiply, step=step, which=which, first=first, sends=sends, tall=tall),
        out_shape=out_shape,
        in_specs=[VMEM, VMEM, HBM, HBM],
        out_specs=[VMEM] * len(out_shape),
        scratch_shapes=[
            pltpu.VMEM((columns, LANES), F32),
            pltpu.VMEM((columns, LANES), F32),
            pltpu.VMEM((columns, 2 * width), BF16),
            pltpu.VMEM((columns, LANES), F32),
            pltpu.VMEM((n, 2, rows, width), BF16),
            pltpu.SemaphoreType.DMA((n, 2)),
        ],
        compiler_params=pltpu.CompilerParams(vmem_limit_bytes=52 << 20),
        cost_estimate=pl.CostEstimate(
            flops=n * rows * columns * width * 4, bytes_accessed=n * 6 << 20, transcendentals=n * columns * width * 2
        ),
        name="products",
    )(blocks, seam, own, other)


def add_on(got_ref, product_ref, norm_ref, *out_refs):
    rows = product_ref.shape[1]
    each = product_ref.shape[2] // len(out_refs)
    for i, out_ref in enumerate(out_refs):
        at = slice(i * each, (i + 1) * each)
        out_ref[:rows, :] = (got_ref[:rows, at].astype(F32) + product_ref[0, :, at]).astype(BF16)
        if out_ref.shape[0] > rows:
            norm = jnp.sum(got_ref[rows:, at].astype(F32), axis=0, keepdims=True) + norm_ref[:1, at]
            put_norm(out_ref, rows, slice(None), norm)


def added(got, product, norm, pieces):
    rows, columns = product.shape[1:]
    return pl.pallas_call(
        add_on,
        out_shape=[jax.ShapeDtypeStruct((got.shape[0], columns // pieces), BF16)] * pieces,
        in_specs=[VMEM] * 3,
        out_specs=[VMEM] * pieces,
        compiler_params=pltpu.CompilerParams(vmem_limit_bytes=8 << 20),
        cost_estimate=pl.CostEstimate(flops=rows * columns * 1000, bytes_accessed=2 << 20, transcendentals=0),
        name="add_on",
    )(got, product, norm)


def finish(a_ref, b_ref, c_ref, d_ref, product_ref, norm_ref, out_ref, held_ref, sems):
    rows = product_ref.shape[1]
    step = rows // 2
    squares = norm_ref[:1, :]
    for ref in (a_ref, c_ref):
        squares = squares + jnp.sum(ref[rows:, :].astype(F32), axis=0, keepdims=True)
    norm = jnp.sqrt(squares)
    core = lax.axis_index("depth").astype(jnp.int32)
    stores = []
    for half, one, two in ((core, a_ref, d_ref), (1 - core, b_ref, c_ref)):
        for start in range(0, rows, step):
            at = pl.ds(start, step)
            total = product_ref[half, at] + one[at, :].astype(F32) + two[at, :].astype(F32)
            held_ref[len(stores)] = total / norm
            store = pltpu.make_async_copy(held_ref.at[len(stores)], out_ref.at[half, at], sems.at[len(stores)])
            store.start()
            stores.append(store)
    for store in stores:
        store.wait()


def finished(first, second, first_across, second_across, product, norm):
    _, rows, columns = product.shape
    return pl.pallas_call(
        finish,
        out_shape=jax.ShapeDtypeStruct(product.shape, F32),
        in_specs=[VMEM] * 6,
        out_specs=HBM,
        scratch_shapes=[pltpu.VMEM((4, rows // 2, columns), F32), pltpu.SemaphoreType.DMA((4,))],
        cost_estimate=pl.CostEstimate(flops=product.size * 100, bytes_accessed=4 << 20, transcendentals=0),
        compiler_params=pltpu.CompilerParams(vmem_limit_bytes=8 << 20),
        name="finish",
    )(first, second, first_across, second_across, product, norm)


def pack(spectrum_ref, wanted_ref, fraction_ref, out_ref):
    rows = []
    for half in range(2):
        for start in range(0, spectrum_ref.shape[1], LANES):
            rows.append(spectrum_ref[half : half + 1, start : start + LANES])
    for ref in (wanted_ref, fraction_ref):
        for start in range(0, ref.shape[1], LANES):
            rows.append(ref[:, start : start + LANES].astype(F32))
    out_ref[...] = jnp.broadcast_to(jnp.concatenate(rows, axis=0)[None], out_ref.shape)


def packed(spectrum, wanted, fraction, copies):
    rows = (spectrum.size + wanted.size + fraction.size) // LANES
    return pl.pallas_call(
        pack,
        out_shape=jax.ShapeDtypeStruct((copies, rows, LANES), F32),
        in_specs=[VMEM] * 3,
        out_specs=VMEM,
        compiler_params=pltpu.CompilerParams(vmem_limit_bytes=4 << 20),
        cost_estimate=pl.CostEstimate(flops=1000, bytes_accessed=400000, transcendentals=0),
        name="pack",
    )(spectrum, wanted.reshape(1, -1), fraction.reshape(1, -1))


def body(halves, spectrum, wanted, fraction):
    rows = halves.shape[1]
    ncols = lax.axis_size("col")
    ndepth = lax.axis_size("depth")
    nrows = lax.axis_size(ROW)
    columns = wanted.shape[0]
    reach = ncols // 2
    ring = ("col", "depth")

    def along(core, col, by):
        return (col + (by if core == 0 else -by)) % ncols

    straight = [(k * ndepth + c, along(c, k, 1) * ndepth + c) for k in range(ncols) for c in range(ndepth)]
    across = [(k * ndepth + c, along(c, k, 1) * ndepth + 1 - c) for k in range(ncols) for c in range(ndepth)]

    other = lax.ppermute(halves, "depth", [(0, 1), (1, 0)])
    blocks = lax.all_to_all(packed(spectrum, wanted, fraction, ncols * ndepth), ring, 0, 0, tiled=True)
    last = lax.axis_index(ROW) == nrows - 1
    seam = [jnp.where(last, h[0, rows - 1], h[1, 0]).reshape(-1, LANES) for h in (halves, other)]
    seam = jnp.concatenate(seam, axis=0)
    seam = lax.all_to_all(jnp.broadcast_to(seam[None], (nrows,) + seam.shape), ROW, 0, 0, tiled=True)

    multiplied = functools.partial(products, blocks=blocks, seam=seam, own=halves, other=other, columns=columns)
    (a,) = multiplied(("first",), step=reach, sends=True, tall=True)
    a = lax.ppermute(a, ring, straight)
    b, norm = multiplied(("second",), step=reach - 1, sends=True)
    b = lax.ppermute(b, ring, straight)
    product, more = multiplied(("first",), step=reach - 1)
    (a,) = added(a, product, norm + more, 1)
    for step in range(reach - 2, 0, -1):
        a = lax.ppermute(a, ring, straight)
        product, norm = multiplied(("second",), step=step)
        pieces = 1 if step > 1 else 2
        b, *b_across = added(b, product, norm, pieces)
        b = lax.ppermute(b, ring, straight)
        b_across = [lax.ppermute(x, ring, across) for x in b_across]
        product, more = multiplied(("first",), step=step)
        a, *a_across = added(a, product, norm + more, pieces)
    a = lax.ppermute(a, ring, straight)
    a_across = [lax.ppermute(x, ring, across) for x in a_across]
    product, norm = multiplied((0, 1), step=0, columns=columns // ndepth)
    return finished(a, b, a_across[0], b_across[0], product, norm)


def solution(mesh):
    split = Mesh(
        mesh.devices.reshape(4, 4, mesh.shape["col"], mesh.shape["depth"]), ("row_0", "row_1", "col", "depth")
    )
    in_specs = (P(None, ROW, ("col", "depth")), P(None, ("col", "depth")), P("col"), P("col"))
    out_specs = P(None, ROW, ("col", "depth"))
    return jax.shard_map(body, mesh=split, in_specs=in_specs, out_specs=out_specs, check_vma=False)
```

time: 95.4 us -> 91.5 us (0.959)
  starting transfers between devices: 46.7 us -> 26.6 us
  blocking collectives: 0 us -> 13.1 us
  waiting for transfers between devices: 14 us -> 20.2 us
  Pallas kernels: 32.1 us -> 27.8 us
  local copies, waits for them, and re-layouts: 0.99 us -> 2.07 us
    all_to_all x0 -> x1, blocking collectives: none -> 13.1 us  [body(): lax.all_to_all(jnp.broadcast_to(seam[None], (nrows,) + seam.shape), ROW,...]
    all_to_all x1, starting transfers between devices: 18.2 us -> 6.88 us  [body(): lax.all_to_all(packed(spectrum, wanted, fraction, ncols * ndepth), ring,...]
    ppermute x4, starting transfers between devices: 9.54 us -> 3.31 us  [body(): a = lax.ppermute(a, ring, straight)]
    ppermute x3 -> x0, starting transfers between devices: 4 us -> none  [body(): lax.ppermute(x, ROW + ('col', 'depth'), pairs)]
    pallas_call x13 -> x14, Pallas kernels: 30.5 us -> 26.8 us  [the longest x8 25.5 us: products(): pl.pallas_call(functools.partial(multiply, step=step, which=which, first=...]
    ppermute x4, waiting for transfers between devices: 0.01 us -> 3.51 us  [body(): a = lax.ppermute(a, ring, straight)]
    unnamed x2 -> x8, local copies, waits for them, and re-layouts: 0.01 us -> 2.06 us
    all_to_all x1, waiting for transfers between devices: 7.61 us -> 9.38 us  [body(): lax.all_to_all(packed(spectrum, wanted, fraction, ncols * ndepth), ring,...]
  transfers between devices with their start and end apart: 14 -> 11, of which waited for: 3 -> 5; matrix products, arithmetic and copies ran while one was open for 1% -> 1% of each run, Pallas kernels for 28% -> 26%
where the time goes in v1:
time: 91.5 us; the launch traced here: 90.9 us
  Pallas kernels  27.8 us (30%)
  starting transfers between devices  26.6 us (29%)
  waiting for transfers between devices  20.2 us (22%)
  blocking collectives  13.1 us (14%)
  local copies, waits for them, and re-layouts  2.07 us (2%)
    pallas_call x8, Pallas kernels, products(): pl.pallas_call(functools.partial(multiply, step=step, which=which, first=...  25.5 us
    all_to_all x1, blocking collectives, body(): lax.all_to_all(jnp.broadcast_to(seam[None], (nrows,) + seam.shape), ROW,...  13.1 us
    all_to_all x1, waiting for transfers between devices, body(): lax.all_to_all(packed(spectrum, wanted, fraction, ncols * ndepth), ring,...  9.38 us
    all_to_all x1, starting transfers between devices, body(): lax.all_to_all(packed(spectrum, wanted, fraction, ncols * ndepth), ring,...  6.88 us
    ppermute x1, starting transfers between devices, body(): a_across = [lax.ppermute(x, ring, across) for x in a_across]  6.4 us
    ppermute x3, starting transfers between devices, body(): b = lax.ppermute(b, ring, straight)  3.9 us
    ppermute x1, waiting for transfers between devices, body(): b_across = [lax.ppermute(x, ring, across) for x in b_across]  3.68 us
    ppermute x3, waiting for transfers between devices, body(): b = lax.ppermute(b, ring, straight)  3.6 us
  transfers between devices with their start and end apart: 11, of which 5 were waited for; matrix products, arithmetic and copies ran while one was open for 1% of the time, Pallas kernels for 26%

profile of v1, /device:TPU:1, one launch (start us, length us, event | category | flops | bytes accessed | tf_op | source)
XLA Modules:
  0.0 90.9 jit_solution(6336471370336133302)
XLA Ops:
  0.0 3.2 %collective-permute-start = (bf16[2,512,1024]{2,1,0:T(8,128)(2,1)}, bf16[2,512,1024]{2,1,0:T(8,128)(2,1)S(1)}, u32[]{:S(2)}, u32[]{:S(2)}) collective-permute-start(bf16[2,512,1024]{2,1,0:T(8,128)(2,1)} %own_ref.15), channel_id=1, source_target_pairs={{0,1},{1,0},{2,3},{3,2},{4,5},{5,4},{6,7},{7,6},{8,9},{9,8},{10,11... | collective-permute-start | bytes 6291464 | tf_op jit(solution)/shard_map/ppermute | solution.py:264
  3.2 0.0 copy-start
  3.2 0.7 copy-done
  3.9 0.0 copy-start.1
  3.9 0.7 copy-done.1
  4.6 0.0 copy-start.2
  4.6 0.7 copy-done.2
  5.3 0.7 pack.1
  6.0 6.9 %all-to-all-start = ((f32[16,24,128]{2,1,0:T(8,128)}), f32[16,24,128]{2,1,0:T(8,128)S(1)}, u32[]{:S(2)}, u32[]{:S(2)}) async-start(f32[16,24,128]{2,1,0:T(8,128)} %pack.1), calls=%async_computation | async-start | bytes 393216 | tf_op jit(solution)/shard_map/all_to_all | solution.py:265
  12.8 0.8 fusion
  13.6 0.0 collective-permute-done.other_ref
  13.6 0.0 copy-start.3
  13.7 9.4 %all-to-all-done.blocks_ref = f32[16,24,128]{2,1,0:T(8,128)S(1)} async-done(((f32[16,24,128]{2,1,0:T(8,128)}), f32[16,24,128]{2,1,0:T(8,128)S(1)}, u32[]{:S(2)}, u32[]{:S(2)}) %all-to-all-start) | async-done | bytes 196640 | tf_op jit(solution)/shard_map/all_to_all | solution.py:265
  23.1 13.1 %all_to_all.10.seam_ref = bf16[16,16,128]{2,1,0:T(8,128)(2,1)S(1)} all-to-all(bf16[16,16,128]{2,1,0:T(8,128)(2,1)S(1)} %broadcast_in_dim.2), channel_id=1, replica_groups=mesh['row_0'=4,'row_1'=4,'col'=8,'depth'=2] {'row_0','row_1'}, dimensions={0} | all-to-all | bytes 131072 | tf_op jit(solution)/shard_map/all_to_all | solution.py:269
  36.2 0.0 copy-done.3
  36.2 3.1 %products.8 = bf16[528,512]{1,0:T(8,128)(2,1)S(1)} custom-call(f32[16,24,128]{2,1,0:T(8,128)S(1)} %all-to-all-done.blocks_ref, bf16[16,16,128]{2,1,0:T(8,128)(2,1)S(1)} %all_to_all.10.seam_ref, bf16[2,512,1024]{2,1,0:T(8,128)(2,1)} %own_ref.15, bf16[2,512,1024]{2,1,0:T(8,128)(2,1)} %copy-done.3), custom_call_target="tpu_custom_call" | custom-call | flops 1073741824 | bytes 6291456 | tf_op jit(solution)/shard_map/products/pallas_call | solution.py:145
  39.2 0.1 collective-permute-start.1
  39.3 3.0 %products.10 = (bf16[512,512]{1,0:T(8,128)(2,1)S(1)}, f32[8,512]{1,0:T(8,128)S(1)}) custom-call(f32[16,24,128]{2,1,0:T(8,128)S(1)} %all-to-all-done.blocks_ref, bf16[16,16,128]{2,1,0:T(8,128)(2,1)S(1)} %all_to_all.10.seam_ref, bf16[2,512,1024]{2,1,0:T(8,128)(2,1)} %own_ref.15, bf16[2,512,1024]{2,1,0:T(8,128)(2,1)} %copy-done.3), custom_call_target="tpu_custom_call" | custom-call | flops 1073741824 | bytes 6291456 | tf_op jit(solution)/shard_map/products/pallas_call | solution.py:145
  42.4 3.1 %products.9 = (f32[1,512,512]{2,1,0:T(8,128)S(1)}, f32[8,512]{1,0:T(8,128)S(1)}) custom-call(f32[16,24,128]{2,1,0:T(8,128)S(1)} %all-to-all-done.blocks_ref, bf16[16,16,128]{2,1,0:T(8,128)(2,1)S(1)} %all_to_all.10.seam_ref, bf16[2,512,1024]{2,1,0:T(8,128)(2,1)} %own_ref.15, bf16[2,512,1024]{2,1,0:T(8,128)(2,1)} %copy-done.3), custom_call_target="tpu_custom_call" | custom-call | flops 1073741824 | bytes 6291456 | tf_op jit(solution)/shard_map/products/pallas_call | solution.py:145
  45.5 2.3 %collective-permute-done.1.got_ref = bf16[528,512]{1,0:T(8,128)(2,1)S(1)} collective-permute-done((bf16[528,512]{1,0:T(8,128)(2,1)S(1)}, bf16[528,512]{1,0:T(8,128)(2,1)S(1)}, u32[]{:S(2)}, u32[]{:S(2)}) %collective-permute-start.1) | collective-permute-done | bytes 540704 | tf_op jit(solution)/shard_map/ppermute | solution.py:273
  47.8 0.1 add_on.5
  47.9 1.0 %collective-permute-start.2 = (bf16[528,512]{1,0:T(8,128)(2,1)S(1)}, bf16[528,512]{1,0:T(8,128)(2,1)S(1)}, u32[]{:S(2)}, u32[]{:S(2)}) collective-permute-start(bf16[528,512]{1,0:T(8,128)(2,1)S(1)} %add_on.5), channel_id=1, source_target_pairs={{0,2},{1,15},{2,4},{3,1},{4,6},{5,3},{6,8},{7,5},{8,10},{9,7},{10,... | collective-permute-start | bytes 1622024 | tf_op jit(solution)/shard_map/ppermute | solution.py:279
  48.9 0.3 collective-permute-start.5
  49.2 3.0 %products.12 = (f32[1,512,512]{2,1,0:T(8,128)S(1)}, f32[8,512]{1,0:T(8,128)S(1)}) custom-call(f32[16,24,128]{2,1,0:T(8,128)S(1)} %all-to-all-done.blocks_ref, bf16[16,16,128]{2,1,0:T(8,128)(2,1)S(1)} %all_to_all.10.seam_ref, bf16[2,512,1024]{2,1,0:T(8,128)(2,1)} %own_ref.15, bf16[2,512,1024]{2,1,0:T(8,128)(2,1)} %copy-done.3), custom_call_target="tpu_custom_call" | custom-call | flops 1073741824 | bytes 6291456 | tf_op jit(solution)/shard_map/products/pallas_call | solution.py:145
  52.2 3.1 %products.11 = (f32[1,512,512]{2,1,0:T(8,128)S(1)}, f32[8,512]{1,0:T(8,128)S(1)}) custom-call(f32[16,24,128]{2,1,0:T(8,128)S(1)} %all-to-all-done.blocks_ref, bf16[16,16,128]{2,1,0:T(8,128)(2,1)S(1)} %all_to_all.10.seam_ref, bf16[2,512,1024]{2,1,0:T(8,128)(2,1)} %own_ref.15, bf16[2,512,1024]{2,1,0:T(8,128)(2,1)} %copy-done.3), custom_call_target="tpu_custom_call" | custom-call | flops 1073741824 | bytes 6291456 | tf_op jit(solution)/shard_map/products/pallas_call | solution.py:145
  55.3 1.2 %collective-permute-done.2.got_ref = bf16[528,512]{1,0:T(8,128)(2,1)S(1)} collective-permute-done((bf16[528,512]{1,0:T(8,128)(2,1)S(1)}, bf16[528,512]{1,0:T(8,128)(2,1)S(1)}, u32[]{:S(2)}, u32[]{:S(2)}) %collective-permute-start.2) | collective-permute-done | bytes 540704 | tf_op jit(solution)/shard_map/ppermute | solution.py:279
  56.5 0.1 add_on.6
  56.6 1.9 %collective-permute-start.3 = (bf16[528,512]{1,0:T(8,128)(2,1)S(1)}, bf16[528,512]{1,0:T(8,128)(2,1)S(1)}, u32[]{:S(2)}, u32[]{:S(2)}) collective-permute-start(bf16[528,512]{1,0:T(8,128)(2,1)S(1)} %add_on.6), channel_id=1, source_target_pairs={{0,2},{1,15},{2,4},{3,1},{4,6},{5,3},{6,8},{7,5},{8,10},{9,7},{10,... | collective-permute-start | bytes 1622024 | tf_op jit(solution)/shard_map/ppermute | solution.py:279
  58.5 3.6 %collective-permute-done.5.got_ref = bf16[512,512]{1,0:T(8,128)(2,1)S(1)} collective-permute-done((bf16[512,512]{1,0:T(8,128)(2,1)S(1)}, bf16[512,512]{1,0:T(8,128)(2,1)S(1)}, u32[]{:S(2)}, u32[]{:S(2)}) %collective-permute-start.5) | collective-permute-done | bytes 524320 | tf_op jit(solution)/shard_map/ppermute | solution.py:275
  62.1 0.1 add_on.8
  62.2 1.9 %collective-permute-start.6 = (bf16[512,512]{1,0:T(8,128)(2,1)S(1)}, bf16[512,512]{1,0:T(8,128)(2,1)S(1)}, u32[]{:S(2)}, u32[]{:S(2)}) collective-permute-start(bf16[512,512]{1,0:T(8,128)(2,1)S(1)} %add_on.8), channel_id=1, source_target_pairs={{0,2},{1,15},{2,4},{3,1},{4,6},{5,3},{6,8},{7,5},{8,10},{9,7},{10,... | collective-permute-start | bytes 1572872 | tf_op jit(solution)/shard_map/ppermute | solution.py:283
  64.1 3.0 %products.14 = (f32[1,512,512]{2,1,0:T(8,128)S(1)}, f32[8,512]{1,0:T(8,128)S(1)}) custom-call(f32[16,24,128]{2,1,0:T(8,128)S(1)} %all-to-all-done.blocks_ref, bf16[16,16,128]{2,1,0:T(8,128)(2,1)S(1)} %all_to_all.10.seam_ref, bf16[2,512,1024]{2,1,0:T(8,128)(2,1)} %own_ref.15, bf16[2,512,1024]{2,1,0:T(8,128)(2,1)} %copy-done.3), custom_call_target="tpu_custom_call" | custom-call | flops 1073741824 | bytes 6291456 | tf_op jit(solution)/shard_map/products/pallas_call | solution.py:145
  67.2 3.1 %products.13 = (f32[1,512,512]{2,1,0:T(8,128)S(1)}, f32[8,512]{1,0:T(8,128)S(1)}) custom-call(f32[16,24,128]{2,1,0:T(8,128)S(1)} %all-to-all-done.blocks_ref, bf16[16,16,128]{2,1,0:T(8,128)(2,1)S(1)} %all_to_all.10.seam_ref, bf16[2,512,1024]{2,1,0:T(8,128)(2,1)} %own_ref.15, bf16[2,512,1024]{2,1,0:T(8,128)(2,1)} %copy-done.3), custom_call_target="tpu_custom_call" | custom-call | flops 1073741824 | bytes 6291456 | tf_op jit(solution)/shard_map/products/pallas_call | solution.py:145
  70.3 0.0 collective-permute-done.3.got_ref
  70.3 0.1 add_on.7
  70.4 0.3 collective-permute-start.4
  70.7 6.4 %collective-permute-start.8 = (bf16[528,256]{1,0:T(8,128)(2,1)S(1)}, bf16[528,256]{1,0:T(8,128)(2,1)S(1)}, u32[]{:S(2)}, u32[]{:S(2)}) collective-permute-start(bf16[528,256]{1,0:T(8,128)(2,1)S(1)} %get-tuple-element.37), channel_id=1, source_target_pairs={{0,3},{1,14},{2,5},{3,0},{4,7},{5,2},{6,9},{7,4},{8,11},{9,6},{10,... | collective-permute-start | bytes 811016 | tf_op jit(solution)/shard_map/ppermute | solution.py:288
  77.1 0.0 collective-permute-done.6.got_ref
  77.1 0.1 add_on.9
  77.2 1.7 %collective-permute-start.7 = (bf16[512,256]{1,0:T(8,128)(2,1)S(1)}, bf16[512,256]{1,0:T(8,128)(2,1)S(1)}, u32[]{:S(2)}, u32[]{:S(2)}) collective-permute-start(bf16[512,256]{1,0:T(8,128)(2,1)S(1)} %get-tuple-element.36), channel_id=1, source_target_pairs={{0,2},{1,15},{2,4},{3,1},{4,6},{5,3},{6,8},{7,5},{8,10},{9,7},{10,... | collective-permute-start | bytes 786440 | tf_op jit(solution)/shard_map/ppermute | solution.py:283
  78.9 2.9 %collective-permute-start.9 = (bf16[512,256]{1,0:T(8,128)(2,1)S(1)}, bf16[512,256]{1,0:T(8,128)(2,1)S(1)}, u32[]{:S(2)}, u32[]{:S(2)}) collective-permute-start(bf16[512,256]{1,0:T(8,128)(2,1)S(1)} %get-tuple-element.38), channel_id=1, source_target_pairs={{0,3},{1,14},{2,5},{3,0},{4,7},{5,2},{6,9},{7,4},{8,11},{9,6},{10,... | collective-permute-start | bytes 786440 | tf_op jit(solution)/shard_map/ppermute | solution.py:284
  81.9 4.1 %products.15 = (f32[2,512,256]{2,1,0:T(8,128)S(1)}, f32[8,256]{1,0:T(8,128)S(1)}) custom-call(f32[16,24,128]{2,1,0:T(8,128)S(1)} %all-to-all-done.blocks_ref, bf16[16,16,128]{2,1,0:T(8,128)(2,1)S(1)} %all_to_all.10.seam_ref, bf16[2,512,1024]{2,1,0:T(8,128)(2,1)} %own_ref.15, bf16[2,512,1024]{2,1,0:T(8,128)(2,1)} %copy-done.3), custom_call_target="tpu_custom_call" | custom-call | flops 1073741824 | bytes 12582912 | tf_op jit(solution)/shard_map/products/pallas_call | solution.py:145
  86.0 0.0 collective-permute-done.7.b_ref
  86.0 3.7 %collective-permute-done.9.d_ref = bf16[512,256]{1,0:T(8,128)(2,1)S(1)} collective-permute-done((bf16[512,256]{1,0:T(8,128)(2,1)S(1)}, bf16[512,256]{1,0:T(8,128)(2,1)S(1)}, u32[]{:S(2)}, u32[]{:S(2)}) %collective-permute-start.9) | collective-permute-done | bytes 262176 | tf_op jit(solution)/shard_map/ppermute | solution.py:284
  89.7 0.0 collective-permute-done.4.a_ref
  89.7 0.0 collective-permute-done.8.c_ref
  89.7 1.1 %finish.1 = f32[2,512,256]{2,1,0:T(8,128)} custom-call(bf16[528,256]{1,0:T(8,128)(2,1)S(1)} %collective-permute-done.4.a_ref, bf16[512,256]{1,0:T(8,128)(2,1)S(1)} %collective-permute-done.7.b_ref, bf16[528,256]{1,0:T(8,128)(2,1)S(1)} %collective-permute-done.8.c_ref, bf16[512,256]{1,0:T(8,128)(2,1)S(1)} %collective-permute-done.9.d_ref, ...), custom_call_target="tpu_custom_call" | custom-call | flops 26214400 | bytes 4194304 | tf_op jit(solution)/shard_map/finish/pallas_call | solution.py:213
  (6 shorter events, 0.1 us)
Async XLA Ops:
  0.0 13.6 %collective-permute-start = (bf16[2,512,1024]{2,1,0:T(8,128)(2,1)}, bf16[2,512,1024]{2,1,0:T(8,128)(2,1)S(1)}, u32[]{:S(2)}, u32[]{:S(2)}) collective-permute-start(bf16[2,512,1024]{2,1,0:T(8,128)(2,1)} %own_ref.15), channel_id=1, source_target_pairs={{0,1},{1,0},{2,3},{3,2},{4,5},{5,4},{6,7},{7,6},{8,9},{9,8},{10,11... | collective-permute-start | bytes 6291464 | tf_op jit(solution)/shard_map/ppermute | solution.py:264
  3.2 0.7 copy-start
  3.9 0.7 copy-start.1
  4.6 0.7 copy-start.2
  6.0 17.1 %all-to-all-start = ((f32[16,24,128]{2,1,0:T(8,128)}), f32[16,24,128]{2,1,0:T(8,128)S(1)}, u32[]{:S(2)}, u32[]{:S(2)}) async-start(f32[16,24,128]{2,1,0:T(8,128)} %pack.1), calls=%async_computation | async-start | bytes 393216 | tf_op jit(solution)/shard_map/all_to_all | solution.py:265
  13.6 22.5 %copy-start.3 = (bf16[2,512,1024]{2,1,0:T(8,128)(2,1)}, bf16[2,512,1024]{2,1,0:T(8,128)(2,1)S(1)}, u32[]{:S(2)}) copy-start(bf16[2,512,1024]{2,1,0:T(8,128)(2,1)S(1)} %collective-permute-done.other_ref) | copy-start | bytes 6291460
  39.2 8.6 %collective-permute-start.1 = (bf16[528,512]{1,0:T(8,128)(2,1)S(1)}, bf16[528,512]{1,0:T(8,128)(2,1)S(1)}, u32[]{:S(2)}, u32[]{:S(2)}) collective-permute-start(bf16[528,512]{1,0:T(8,128)(2,1)S(1)} %products.8), channel_id=1, source_target_pairs={{0,2},{1,15},{2,4},{3,1},{4,6},{5,3},{6,8},{7,5},{8,10},{9,7},{10,... | collective-permute-start | bytes 1622024 | tf_op jit(solution)/shard_map/ppermute | solution.py:273
  47.9 8.6 %collective-permute-start.2 = (bf16[528,512]{1,0:T(8,128)(2,1)S(1)}, bf16[528,512]{1,0:T(8,128)(2,1)S(1)}, u32[]{:S(2)}, u32[]{:S(2)}) collective-permute-start(bf16[528,512]{1,0:T(8,128)(2,1)S(1)} %add_on.5), channel_id=1, source_target_pairs={{0,2},{1,15},{2,4},{3,1},{4,6},{5,3},{6,8},{7,5},{8,10},{9,7},{10,... | collective-permute-start | bytes 1622024 | tf_op jit(solution)/shard_map/ppermute | solution.py:279
  48.9 13.2 %collective-permute-start.5 = (bf16[512,512]{1,0:T(8,128)(2,1)S(1)}, bf16[512,512]{1,0:T(8,128)(2,1)S(1)}, u32[]{:S(2)}, u32[]{:S(2)}) collective-permute-start(bf16[512,512]{1,0:T(8,128)(2,1)S(1)} %get-tuple-element.33), channel_id=1, source_target_pairs={{0,2},{1,15},{2,4},{3,1},{4,6},{5,3},{6,8},{7,5},{8,10},{9,7},{10,... | collective-permute-start | bytes 1572872 | tf_op jit(solution)/shard_map/ppermute | solution.py:275
  56.6 13.7 %collective-permute-start.3 = (bf16[528,512]{1,0:T(8,128)(2,1)S(1)}, bf16[528,512]{1,0:T(8,128)(2,1)S(1)}, u32[]{:S(2)}, u32[]{:S(2)}) collective-permute-start(bf16[528,512]{1,0:T(8,128)(2,1)S(1)} %add_on.6), channel_id=1, source_target_pairs={{0,2},{1,15},{2,4},{3,1},{4,6},{5,3},{6,8},{7,5},{8,10},{9,7},{10,... | collective-permute-start | bytes 1622024 | tf_op jit(solution)/shard_map/ppermute | solution.py:279
  62.2 14.9 %collective-permute-start.6 = (bf16[512,512]{1,0:T(8,128)(2,1)S(1)}, bf16[512,512]{1,0:T(8,128)(2,1)S(1)}, u32[]{:S(2)}, u32[]{:S(2)}) collective-permute-start(bf16[512,512]{1,0:T(8,128)(2,1)S(1)} %add_on.8), channel_id=1, source_target_pairs={{0,2},{1,15},{2,4},{3,1},{4,6},{5,3},{6,8},{7,5},{8,10},{9,7},{10,... | collective-permute-start | bytes 1572872 | tf_op jit(solution)/shard_map/ppermute | solution.py:283
  70.4 19.3 %collective-permute-start.4 = (bf16[528,256]{1,0:T(8,128)(2,1)S(1)}, bf16[528,256]{1,0:T(8,128)(2,1)S(1)}, u32[]{:S(2)}, u32[]{:S(2)}) collective-permute-start(bf16[528,256]{1,0:T(8,128)(2,1)S(1)} %get-tuple-element.32), channel_id=1, source_target_pairs={{0,2},{1,15},{2,4},{3,1},{4,6},{5,3},{6,8},{7,5},{8,10},{9,7},{10,... | collective-permute-start | bytes 811016 | tf_op jit(solution)/shard_map/ppermute | solution.py:287
  70.7 19.0 %collective-permute-start.8 = (bf16[528,256]{1,0:T(8,128)(2,1)S(1)}, bf16[528,256]{1,0:T(8,128)(2,1)S(1)}, u32[]{:S(2)}, u32[]{:S(2)}) collective-permute-start(bf16[528,256]{1,0:T(8,128)(2,1)S(1)} %get-tuple-element.37), channel_id=1, source_target_pairs={{0,3},{1,14},{2,5},{3,0},{4,7},{5,2},{6,9},{7,4},{8,11},{9,6},{10,... | collective-permute-start | bytes 811016 | tf_op jit(solution)/shard_map/ppermute | solution.py:288
  77.2 8.8 %collective-permute-start.7 = (bf16[512,256]{1,0:T(8,128)(2,1)S(1)}, bf16[512,256]{1,0:T(8,128)(2,1)S(1)}, u32[]{:S(2)}, u32[]{:S(2)}) collective-permute-start(bf16[512,256]{1,0:T(8,128)(2,1)S(1)} %get-tuple-element.36), channel_id=1, source_target_pairs={{0,2},{1,15},{2,4},{3,1},{4,6},{5,3},{6,8},{7,5},{8,10},{9,7},{10,... | collective-permute-start | bytes 786440 | tf_op jit(solution)/shard_map/ppermute | solution.py:283
  78.9 10.8 %collective-permute-start.9 = (bf16[512,256]{1,0:T(8,128)(2,1)S(1)}, bf16[512,256]{1,0:T(8,128)(2,1)S(1)}, u32[]{:S(2)}, u32[]{:S(2)}) collective-permute-start(bf16[512,256]{1,0:T(8,128)(2,1)S(1)} %get-tuple-element.38), channel_id=1, source_target_pairs={{0,3},{1,14},{2,5},{3,0},{4,7},{5,2},{6,9},{7,4},{8,11},{9,6},{10,... | collective-permute-start | bytes 786440 | tf_op jit(solution)/shard_map/ppermute | solution.py:284

commit v2 on v1

--- a/solution.py
+++ b/solution.py
@@ -16,15 +16,7 @@
 BF16 = jnp.bfloat16
 
 
-def heading(step):
-    core = lax.axis_index("depth").astype(jnp.int32)
-    col = lax.axis_index("col").astype(jnp.int32)
-    ncols = lax.axis_size("col")
-    target = lax.rem(col + jnp.where(core == 0, step, ncols - step), ncols)
-    return core, col, target
-
-
-def look_up(core, target, blocks_ref, low_ref, shift_ref, *, value_rows, first, count):
+def look_up(core, col, blocks_ref, low_ref, shift_ref, *, step, value_rows, first, count):
     places = blocks_ref.shape[0]
     table = blocks_ref[:, :value_rows, :].reshape(places * value_rows, LANES)
     high = table.astype(BF16)
@@ -35,13 +27,16 @@
     per_block = value_rows * LANES
     half = per_block // 2
 
-    roots = blocks_ref[2 * target, value_rows : value_rows + 8, :]
+    roots = blocks_ref[2 * step, value_rows : value_rows + 8, :]
     swapped = jnp.concatenate([roots[2:4], roots[0:2], roots[6:8], roots[4:6]], axis=0)
     roots = jnp.where(core == 0, roots, swapped)
     wanted = roots[:4].astype(jnp.int32)
     rows = []
     for position in (wanted, wanted + 1):
         owner = lax.shift_right_logical(position, per_block.bit_length() - 1)
+        ahead = lax.shift_right_logical(owner, 1) - col
+        ahead = jnp.where(core == 0, ahead, -ahead) & (places // 2 - 1)
+        owner = ahead * 2 + ((owner & 1) ^ core)
         inside = position & (per_block - 1)
         index = (inside & 1) * half + lax.shift_right_logical(inside, 1)
         rows += [owner * value_rows + lax.shift_right_logical(index, 7), index & (LANES - 1)]
@@ -63,14 +58,15 @@
         shift_ref[at, :] = jnp.broadcast_to(shift, (LANES, LANES))
 
 
-def multiply(blocks_ref, seam_ref, own_ref, other_ref, *refs, step, which, first, sends, tall):
+def multiply(blocks_ref, own_ref, other_ref, *refs, step, which, first, sends, tall):
     out_ref, norm_ref = refs[0], None if tall else refs[1]
     low_ref, shift_ref, block_ref, square_ref, halves_ref, sems = refs[-6:]
     columns = low_ref.shape[0]
     rows, width = halves_ref.shape[2:]
     tiles = width // LANES
     value_rows = 2 * tiles
-    core, col, target = heading(step)
+    core = lax.axis_index("depth").astype(jnp.int32)
+    col = lax.axis_index("col").astype(jnp.int32)
     halves = [core if w == "first" else 1 - core if w == "second" else w for w in which]
     loads = [
         [
@@ -82,12 +78,13 @@
     for pair in loads:
         for load in pair:
             load.start()
-    look_up(core, target, blocks_ref, low_ref, shift_ref, value_rows=value_rows, first=first, count=columns // LANES)
-    here = [2 * col + core, 2 * col + 1 - core]
+    look_up(
+        core, col, blocks_ref, low_ref, shift_ref, step=step, value_rows=value_rows, first=first, count=columns // LANES
+    )
     for u, half in enumerate(halves):
-        values = [[blocks_ref[s, pl.ds(half * tiles + t, 1), :] for t in range(tiles)] for s in here]
-        rows_of = seam_ref[jnp.where(half == 0, seam_ref.shape[0] - 1, 0)].astype(F32)
-        seams = [[rows_of[s * tiles + t : s * tiles + t + 1] for t in range(tiles)] for s in range(2)]
+        values = [[blocks_ref[s, pl.ds(half * tiles + t, 1), :] for t in range(tiles)] for s in range(2)]
+        edge = blocks_ref[jnp.where(half == 0, blocks_ref.shape[0] - 1, 0), value_rows + 8 :, :]
+        seams = [[edge[s * tiles + t : s * tiles + t + 1] for t in range(tiles)] for s in range(2)]
         for part in range(columns // 256):
             for piece in range(256 // PIECE):
                 start = part * 256 + piece * PIECE
@@ -133,7 +130,7 @@
 HBM = pl.BlockSpec(memory_space=pl.ANY)
 
 
-def products(which, blocks, seam, own, other, step, columns, first=0, sends=False, tall=False):
+def products(which, blocks, own, other, step, columns, first=0, sends=False, tall=False):
     n = len(which)
     rows, width = own.shape[1:]
     if sends:
@@ -145,7 +142,7 @@
     return pl.pallas_call(
         functools.partial(multiply, step=step, which=which, first=first, sends=sends, tall=tall),
         out_shape=out_shape,
-        in_specs=[VMEM, VMEM, HBM, HBM],
+        in_specs=[VMEM, HBM, HBM],
         out_specs=[VMEM] * len(out_shape),
         scratch_shapes=[
             pltpu.VMEM((columns, LANES), F32),
@@ -160,31 +157,35 @@
             flops=n * rows * columns * width * 4, bytes_accessed=n * 6 << 20, transcendentals=n * columns * width * 2
         ),
         name="products",
-    )(blocks, seam, own, other)
-
-
-def add_on(got_ref, product_ref, norm_ref, *out_refs):
+    )(blocks, own, other)
+
+
+def add_on(*refs, pieces):
+    got_refs, (product_ref, norm_ref), out_refs = refs[: -pieces - 2], refs[-pieces - 2 : -pieces], refs[-pieces:]
     rows = product_ref.shape[1]
-    each = product_ref.shape[2] // len(out_refs)
-    for i, out_ref in enumerate(out_refs):
+    runs = max(len(got_refs), pieces)
+    each = product_ref.shape[2] // runs
+    for i in range(runs):
         at = slice(i * each, (i + 1) * each)
-        out_ref[:rows, :] = (got_ref[:rows, at].astype(F32) + product_ref[0, :, at]).astype(BF16)
+        got_ref, got_at = (got_refs[0], at) if len(got_refs) == 1 else (got_refs[i], slice(None))
+        out_ref, out_at = (out_refs[0], at) if pieces == 1 else (out_refs[i], slice(None))
+        out_ref[:rows, out_at] = (got_ref[:rows, got_at].astype(F32) + product_ref[0, :, at]).astype(BF16)
         if out_ref.shape[0] > rows:
-            norm = jnp.sum(got_ref[rows:, at].astype(F32), axis=0, keepdims=True) + norm_ref[:1, at]
-            put_norm(out_ref, rows, slice(None), norm)
+            norm = jnp.sum(got_ref[rows:, got_at].astype(F32), axis=0, keepdims=True) + norm_ref[:1, at]
+            put_norm(out_ref, rows, out_at, norm)
 
 
 def added(got, product, norm, pieces):
     rows, columns = product.shape[1:]
     return pl.pallas_call(
-        add_on,
-        out_shape=[jax.ShapeDtypeStruct((got.shape[0], columns // pieces), BF16)] * pieces,
-        in_specs=[VMEM] * 3,
+        functools.partial(add_on, pieces=pieces),
+        out_shape=[jax.ShapeDtypeStruct((got[0].shape[0], columns // pieces), BF16)] * pieces,
+        in_specs=[VMEM] * (len(got) + 2),
         out_specs=[VMEM] * pieces,
         compiler_params=pltpu.CompilerParams(vmem_limit_bytes=8 << 20),
         cost_estimate=pl.CostEstimate(flops=rows * columns * 1000, bytes_accessed=2 << 20, transcendentals=0),
         name="add_on",
-    )(got, product, norm)
+    )(*got, product, norm)
 
 
 def finish(a_ref, b_ref, c_ref, d_ref, product_ref, norm_ref, out_ref, held_ref, sems):
@@ -222,28 +223,37 @@
     )(first, second, first_across, second_across, product, norm)
 
 
-def pack(spectrum_ref, wanted_ref, fraction_ref, out_ref):
+def pack(spectrum_ref, wanted_ref, fraction_ref, out_ref, held_ref, wanted_held, fraction_held, sems):
+    loads = []
+    for i, (ref, held) in enumerate(((spectrum_ref, held_ref), (wanted_ref, wanted_held), (fraction_ref, fraction_held))):
+        loads.append(pltpu.make_async_copy(ref, held, sems.at[i]))
+    for load in loads:
+        load.start()
+    for load in loads:
+        load.wait()
     rows = []
     for half in range(2):
-        for start in range(0, spectrum_ref.shape[1], LANES):
-            rows.append(spectrum_ref[half : half + 1, start : start + LANES])
-    for ref in (wanted_ref, fraction_ref):
+        for start in range(0, held_ref.shape[1], LANES):
+            rows.append(held_ref[half : half + 1, start : start + LANES])
+    for ref in (wanted_held, fraction_held):
         for start in range(0, ref.shape[1], LANES):
             rows.append(ref[:, start : start + LANES].astype(F32))
-    out_ref[...] = jnp.broadcast_to(jnp.concatenate(rows, axis=0)[None], out_ref.shape)
-
-
-def packed(spectrum, wanted, fraction, copies):
-    rows = (spectrum.size + wanted.size + fraction.size) // LANES
+    out_ref[...] = jnp.concatenate(rows, axis=0)
+
+
+def packed(spectrum, wanted, fraction):
+    arrays = (spectrum, wanted.reshape(1, -1), fraction.reshape(1, -1))
+    rows = sum(x.size for x in arrays) // LANES
     return pl.pallas_call(
         pack,
-        out_shape=jax.ShapeDtypeStruct((copies, rows, LANES), F32),
-        in_specs=[VMEM] * 3,
+        out_shape=jax.ShapeDtypeStruct((rows, LANES), F32),
+        in_specs=[HBM] * 3,
         out_specs=VMEM,
-        compiler_params=pltpu.CompilerParams(vmem_limit_bytes=4 << 20),
+        scratch_shapes=[pltpu.VMEM(x.shape, x.dtype) for x in arrays] + [pltpu.SemaphoreType.DMA((3,))],
+        compiler_params=pltpu.CompilerParams(vmem_limit_bytes=62 << 20),
         cost_estimate=pl.CostEstimate(flops=1000, bytes_accessed=400000, transcendentals=0),
         name="pack",
-    )(spectrum, wanted.reshape(1, -1), fraction.reshape(1, -1))
+    )(*arrays)
 
 
 def body(halves, spectrum, wanted, fraction):
@@ -262,28 +272,36 @@
     across = [(k * ndepth + c, along(c, k, 1) * ndepth + 1 - c) for k in range(ncols) for c in range(ndepth)]
 
     other = lax.ppermute(halves, "depth", [(0, 1), (1, 0)])
-    blocks = lax.all_to_all(packed(spectrum, wanted, fraction, ncols * ndepth), ring, 0, 0, tiled=True)
+    pairs = []
+    for r in range(nrows):
+        for k in range(ncols):
+            for c in range(ndepth):
+                source = along(c, k, r // 2) * ndepth + (c ^ (r & 1))
+                pairs.append((r * ncols * ndepth + source, r * ncols * ndepth + k * ndepth + c))
+    theirs = lax.ppermute(packed(spectrum, wanted, fraction), ROW + ring, pairs)
     last = lax.axis_index(ROW) == nrows - 1
-    seam = [jnp.where(last, h[0, rows - 1], h[1, 0]).reshape(-1, LANES) for h in (halves, other)]
-    seam = jnp.concatenate(seam, axis=0)
-    seam = lax.all_to_all(jnp.broadcast_to(seam[None], (nrows,) + seam.shape), ROW, 0, 0, tiled=True)
-
-    multiplied = functools.partial(products, blocks=blocks, seam=seam, own=halves, other=other, columns=columns)
-    (a,) = multiplied(("first",), step=reach, sends=True, tall=True)
-    a = lax.ppermute(a, ring, straight)
-    b, norm = multiplied(("second",), step=reach - 1, sends=True)
+    edge = [jnp.where(last, h[0, rows - 1], h[1, 0]).astype(F32).reshape(-1, LANES) for h in (halves, other)]
+    parcel = jnp.concatenate([theirs] + edge, axis=0)
+    blocks = lax.all_to_all(jnp.broadcast_to(parcel[None], (nrows,) + parcel.shape), ROW, 0, 0, tiled=True)
+
+    multiplied = functools.partial(products, blocks=blocks, own=halves, other=other)
+    a = []
+    for first in range(0, columns // LANES, 2):
+        (part,) = multiplied(("first",), step=reach, first=first, columns=2 * LANES, sends=True, tall=True)
+        a.append(lax.ppermute(part, ring, straight))
+    b, norm = multiplied(("second",), step=reach - 1, columns=columns, sends=True)
     b = lax.ppermute(b, ring, straight)
-    product, more = multiplied(("first",), step=reach - 1)
+    product, more = multiplied(("first",), step=reach - 1, columns=columns)
     (a,) = added(a, product, norm + more, 1)
     for step in range(reach - 2, 0, -1):
         a = lax.ppermute(a, ring, straight)
-        product, norm = multiplied(("second",), step=step)
+        product, norm = multiplied(("second",), step=step, columns=columns)
         pieces = 1 if step > 1 else 2
-        b, *b_across = added(b, product, norm, pieces)
+        b, *b_across = added([b], product, norm, pieces)
         b = lax.ppermute(b, ring, straight)
         b_across = [lax.ppermute(x, ring, across) for x in b_across]
-        product, more = multiplied(("first",), step=step)
-        a, *a_across = added(a, product, norm + more, pieces)
+        product, more = multiplied(("first",), step=step, columns=columns)
+        a, *a_across = added([a], product, norm + more, pieces)
     a = lax.ppermute(a, ring, straight)
     a_across = [lax.ppermute(x, ring, across) for x in a_across]
     product, norm = multiplied((0, 1), step=0, columns=columns // ndepth)

time: 91.5 us -> 83.3 us (0.910)
  waiting for transfers between devices: 20.2 us -> 9.83 us
  blocking collectives: 13.1 us -> 19.1 us
  starting transfers between devices: 26.6 us -> 21.5 us
  Pallas kernels: 27.8 us -> 30.1 us
  local copies, waits for them, and re-layouts: 2.07 us -> 0.02 us
    all_to_all x1 -> x0, waiting for transfers between devices: 9.38 us -> none  [body(): lax.all_to_all(packed(spectrum, wanted, fraction, ncols * ndepth), ring,...]
    all_to_all x1 -> x0, starting transfers between devices: 6.88 us -> none  [body(): lax.all_to_all(packed(spectrum, wanted, fraction, ncols * ndepth), ring,...]
    ppermute x0 -> x3, starting transfers between devices: none -> 6.12 us  [the longest x2 4.75 us: body(): a.append(lax.ppermute(part, ring, straight))]
    all_to_all x1, blocking collectives: 13.1 us -> 19.1 us  [body(): lax.all_to_all(jnp.broadcast_to(parcel[None], (nrows,) + parcel.shape), R...]
    ppermute x1, starting transfers between devices: 6.4 us -> 3.98 us  [body(): a_across = [lax.ppermute(x, ring, across) for x in a_across]]
    ppermute x3, waiting for transfers between devices: 3.6 us -> 5.82 us  [body(): b = lax.ppermute(b, ring, straight)]
    ppermute x4 -> x3, waiting for transfers between devices: 3.51 us -> 1.31 us  [body(): a = lax.ppermute(a, ring, straight)]
    unnamed x8 -> x0, local copies, waits for them, and re-layouts: 2.06 us -> none
  transfers between devices with their start and end apart: 11 -> 12, of which waited for: 5 -> 5; matrix products, arithmetic and copies ran while one was open for 1% -> 2% of each run, Pallas kernels for 26% -> 32%
where the time goes in v2:
time: 83.3 us; the launch traced here: 82.4 us
  Pallas kernels  30.1 us (36%)
  starting transfers between devices  21.5 us (26%)
  blocking collectives  19.1 us (23%)
  waiting for transfers between devices  9.83 us (12%)
  other arithmetic  1.51 us (2%)
    pallas_call x9, Pallas kernels, products(): pl.pallas_call(functools.partial(multiply, step=step, which=which, first=...  27.2 us
    all_to_all x1, blocking collectives, body(): lax.all_to_all(jnp.broadcast_to(parcel[None], (nrows,) + parcel.shape), R...  19.1 us
    ppermute x3, waiting for transfers between devices, body(): b = lax.ppermute(b, ring, straight)  5.82 us
    ppermute x2, starting transfers between devices, body(): a.append(lax.ppermute(part, ring, straight))  4.75 us
    ppermute x1, starting transfers between devices, body(): a_across = [lax.ppermute(x, ring, across) for x in a_across]  3.98 us
    ppermute x3, starting transfers between devices, body(): b = lax.ppermute(b, ring, straight)  3.32 us
    ppermute x1, starting transfers between devices, body(): other = lax.ppermute(halves, 'depth', [(0, 1), (1, 0)])  3.2 us
    ppermute x3, starting transfers between devices, body(): a = lax.ppermute(a, ring, straight)  2.61 us
  transfers between devices with their start and end apart: 12, of which 5 were waited for; matrix products, arithmetic and copies ran while one was open for 2% of the time, Pallas kernels for 32%

profile of v2, /device:TPU:1, one launch (start us, length us, event | category | flops | bytes accessed | tf_op | source)
XLA Modules:
  0.0 82.4 jit_solution(542070876526016065)
XLA Ops:
  0.0 3.2 %collective-permute-start.1 = (bf16[2,512,1024]{2,1,0:T(8,128)(2,1)}, bf16[2,512,1024]{2,1,0:T(8,128)(2,1)}, u32[]{:S(2)}, u32[]{:S(2)}) collective-permute-start(bf16[2,512,1024]{2,1,0:T(8,128)(2,1)} %own_ref.17), channel_id=1, source_target_pairs={{0,1},{1,0},{2,3},{3,2},{4,5},{5,4},{6,7},{7,6},{8,9},{9,8},{10,11... | collective-permute-start | bytes 6291464 | tf_op jit(solution)/shard_map/ppermute | solution.py:274
  3.2 1.3 %pack.1 = f32[24,128]{1,0:T(8,128)} custom-call(f32[2,1024]{1,0:T(2,128)} %spectrum_ref.1, s32[1,512]{1,0:T(1,128)} %bitcast.6, f32[1,512]{1,0:T(1,128)} %bitcast.7), custom_call_target="tpu_custom_call" | custom-call | flops 1000 | bytes 400000 | tf_op jit(solution)/shard_map/pack/pallas_call | solution.py:247
  4.6 1.4 %collective-permute-start = (f32[24,128]{1,0:T(8,128)}, f32[24,128]{1,0:T(8,128)S(1)}, u32[]{:S(2)}, u32[]{:S(2)}) collective-permute-start(f32[24,128]{1,0:T(8,128)} %pack.1), channel_id=1, source_target_pairs={{0,0},{1,1},{2,2},{3,3},{4,4},{5,5},{6,6},{7,7},{8,8},{9,9},{10,10... | collective-permute-start | bytes 36872 | tf_op jit(solution)/shard_map/ppermute | solution.py:281
  5.9 0.7 fusion
  6.7 0.7 collective-permute-done.1.other_ref
  7.3 0.7 fusion.1
  8.1 0.0 collective-permute-done
  8.1 19.1 %all_to_all.5.blocks_ref = f32[16,40,128]{2,1,0:T(8,128)S(1)} all-to-all(f32[16,40,128]{2,1,0:T(8,128)S(1)} %broadcast_in_dim.2), channel_id=1, replica_groups=mesh['row_0'=4,'row_1'=4,'col'=8,'depth'=2] {'row_0','row_1'}, dimensions={0} | all-to-all | bytes 655360 | tf_op jit(solution)/shard_map/all_to_all | solution.py:285
  27.2 2.3 %products.10 = bf16[528,256]{1,0:T(8,128)(2,1)S(1)} custom-call(f32[16,40,128]{2,1,0:T(8,128)S(1)} %all_to_all.5.blocks_ref, bf16[2,512,1024]{2,1,0:T(8,128)(2,1)} %own_ref.17, bf16[2,512,1024]{2,1,0:T(8,128)(2,1)} %collective-permute-done.1.other_ref), custom_call_target="tpu_custom_call" | custom-call | flops 536870912 | bytes 6291456 | tf_op jit(solution)/shard_map/products/pallas_call | solution.py:142
  29.6 4.7 %collective-permute-start.3 = (bf16[528,256]{1,0:T(8,128)(2,1)S(1)}, bf16[528,256]{1,0:T(8,128)(2,1)S(1)}, u32[]{:S(2)}, u32[]{:S(2)}) collective-permute-start(bf16[528,256]{1,0:T(8,128)(2,1)S(1)} %products.10), channel_id=1, source_target_pairs={{0,2},{1,15},{2,4},{3,1},{4,6},{5,3},{6,8},{7,5},{8,10},{9,7},{10,... | collective-permute-start | bytes 811016 | tf_op jit(solution)/shard_map/ppermute | solution.py:291
  34.2 2.4 %products.9 = bf16[528,256]{1,0:T(8,128)(2,1)S(1)} custom-call(f32[16,40,128]{2,1,0:T(8,128)S(1)} %all_to_all.5.blocks_ref, bf16[2,512,1024]{2,1,0:T(8,128)(2,1)} %own_ref.17, bf16[2,512,1024]{2,1,0:T(8,128)(2,1)} %collective-permute-done.1.other_ref), custom_call_target="tpu_custom_call" | custom-call | flops 536870912 | bytes 6291456 | tf_op jit(solution)/shard_map/products/pallas_call | solution.py:142
  36.6 0.1 collective-permute-start.2
  36.7 3.0 %products.12 = (bf16[512,512]{1,0:T(8,128)(2,1)S(1)}, f32[8,512]{1,0:T(8,128)S(1)}) custom-call(f32[16,40,128]{2,1,0:T(8,128)S(1)} %all_to_all.5.blocks_ref, bf16[2,512,1024]{2,1,0:T(8,128)(2,1)} %own_ref.17, bf16[2,512,1024]{2,1,0:T(8,128)(2,1)} %collective-permute-done.1.other_ref), custom_call_target="tpu_custom_call" | custom-call | flops 1073741824 | bytes 6291456 | tf_op jit(solution)/shard_map/products/pallas_call | solution.py:142
  39.7 3.1 %products.11 = (f32[1,512,512]{2,1,0:T(8,128)S(1)}, f32[8,512]{1,0:T(8,128)S(1)}) custom-call(f32[16,40,128]{2,1,0:T(8,128)S(1)} %all_to_all.5.blocks_ref, bf16[2,512,1024]{2,1,0:T(8,128)(2,1)} %own_ref.17, bf16[2,512,1024]{2,1,0:T(8,128)(2,1)} %collective-permute-done.1.other_ref), custom_call_target="tpu_custom_call" | custom-call | flops 1073741824 | bytes 6291456 | tf_op jit(solution)/shard_map/products/pallas_call | solution.py:142
  42.8 0.0 collective-permute-done.3.refs_1_
  42.8 0.0 collective-permute-done.2.refs_0_
  42.9 0.1 add_on.5
  43.0 0.8 %collective-permute-start.4 = (bf16[528,512]{1,0:T(8,128)(2,1)S(1)}, bf16[528,512]{1,0:T(8,128)(2,1)S(1)}, u32[]{:S(2)}, u32[]{:S(2)}) collective-permute-start(bf16[528,512]{1,0:T(8,128)(2,1)S(1)} %add_on.5), channel_id=1, source_target_pairs={{0,2},{1,15},{2,4},{3,1},{4,6},{5,3},{6,8},{7,5},{8,10},{9,7},{10,... | collective-permute-start | bytes 1622024 | tf_op jit(solution)/shard_map/ppermute | solution.py:297
  43.8 0.3 collective-permute-start.7
  44.1 3.0 %products.14 = (f32[1,512,512]{2,1,0:T(8,128)S(1)}, f32[8,512]{1,0:T(8,128)S(1)}) custom-call(f32[16,40,128]{2,1,0:T(8,128)S(1)} %all_to_all.5.blocks_ref, bf16[2,512,1024]{2,1,0:T(8,128)(2,1)} %own_ref.17, bf16[2,512,1024]{2,1,0:T(8,128)(2,1)} %collective-permute-done.1.other_ref), custom_call_target="tpu_custom_call" | custom-call | flops 1073741824 | bytes 6291456 | tf_op jit(solution)/shard_map/products/pallas_call | solution.py:142
  47.1 3.1 %products.13 = (f32[1,512,512]{2,1,0:T(8,128)S(1)}, f32[8,512]{1,0:T(8,128)S(1)}) custom-call(f32[16,40,128]{2,1,0:T(8,128)S(1)} %all_to_all.5.blocks_ref, bf16[2,512,1024]{2,1,0:T(8,128)(2,1)} %own_ref.17, bf16[2,512,1024]{2,1,0:T(8,128)(2,1)} %collective-permute-done.1.other_ref), custom_call_target="tpu_custom_call" | custom-call | flops 1073741824 | bytes 6291456 | tf_op jit(solution)/shard_map/products/pallas_call | solution.py:142
  50.2 1.3 %collective-permute-done.4.refs_0_ = bf16[528,512]{1,0:T(8,128)(2,1)S(1)} collective-permute-done((bf16[528,512]{1,0:T(8,128)(2,1)S(1)}, bf16[528,512]{1,0:T(8,128)(2,1)S(1)}, u32[]{:S(2)}, u32[]{:S(2)}) %collective-permute-start.4) | collective-permute-done | bytes 540704 | tf_op jit(solution)/shard_map/ppermute | solution.py:297
  51.5 0.1 add_on.6
  51.6 1.8 %collective-permute-start.5 = (bf16[528,512]{1,0:T(8,128)(2,1)S(1)}, bf16[528,512]{1,0:T(8,128)(2,1)S(1)}, u32[]{:S(2)}, u32[]{:S(2)}) collective-permute-start(bf16[528,512]{1,0:T(8,128)(2,1)S(1)} %add_on.6), channel_id=1, source_target_pairs={{0,2},{1,15},{2,4},{3,1},{4,6},{5,3},{6,8},{7,5},{8,10},{9,7},{10,... | collective-permute-start | bytes 1622024 | tf_op jit(solution)/shard_map/ppermute | solution.py:297
  53.4 3.7 %collective-permute-done.7.refs_0_ = bf16[512,512]{1,0:T(8,128)(2,1)S(1)} collective-permute-done((bf16[512,512]{1,0:T(8,128)(2,1)S(1)}, bf16[512,512]{1,0:T(8,128)(2,1)S(1)}, u32[]{:S(2)}, u32[]{:S(2)}) %collective-permute-start.7) | collective-permute-done | bytes 524320 | tf_op jit(solution)/shard_map/ppermute | solution.py:293
  57.2 0.1 add_on.8
  57.3 1.8 %collective-permute-start.8 = (bf16[512,512]{1,0:T(8,128)(2,1)S(1)}, bf16[512,512]{1,0:T(8,128)(2,1)S(1)}, u32[]{:S(2)}, u32[]{:S(2)}) collective-permute-start(bf16[512,512]{1,0:T(8,128)(2,1)S(1)} %add_on.8), channel_id=1, source_target_pairs={{0,2},{1,15},{2,4},{3,1},{4,6},{5,3},{6,8},{7,5},{8,10},{9,7},{10,... | collective-permute-start | bytes 1572872 | tf_op jit(solution)/shard_map/ppermute | solution.py:301
  59.0 3.0 %products.16 = (f32[1,512,512]{2,1,0:T(8,128)S(1)}, f32[8,512]{1,0:T(8,128)S(1)}) custom-call(f32[16,40,128]{2,1,0:T(8,128)S(1)} %all_to_all.5.blocks_ref, bf16[2,512,1024]{2,1,0:T(8,128)(2,1)} %own_ref.17, bf16[2,512,1024]{2,1,0:T(8,128)(2,1)} %collective-permute-done.1.other_ref), custom_call_target="tpu_custom_call" | custom-call | flops 1073741824 | bytes 6291456 | tf_op jit(solution)/shard_map/products/pallas_call | solution.py:142
  62.0 3.1 %products.15 = (f32[1,512,512]{2,1,0:T(8,128)S(1)}, f32[8,512]{1,0:T(8,128)S(1)}) custom-call(f32[16,40,128]{2,1,0:T(8,128)S(1)} %all_to_all.5.blocks_ref, bf16[2,512,1024]{2,1,0:T(8,128)(2,1)} %own_ref.17, bf16[2,512,1024]{2,1,0:T(8,128)(2,1)} %collective-permute-done.1.other_ref), custom_call_target="tpu_custom_call" | custom-call | flops 1073741824 | bytes 6291456 | tf_op jit(solution)/shard_map/products/pallas_call | solution.py:142
  65.2 0.0 collective-permute-done.5.refs_0_
  65.2 0.1 add_on.7
  65.3 4.0 %collective-permute-start.10 = (bf16[528,256]{1,0:T(8,128)(2,1)S(1)}, bf16[528,256]{1,0:T(8,128)(2,1)S(1)}, u32[]{:S(2)}, u32[]{:S(2)}) collective-permute-start(bf16[528,256]{1,0:T(8,128)(2,1)S(1)} %get-tuple-element.37), channel_id=1, source_target_pairs={{0,3},{1,14},{2,5},{3,0},{4,7},{5,2},{6,9},{7,4},{8,11},{9,6},{10,... | collective-permute-start | bytes 811016 | tf_op jit(solution)/shard_map/ppermute | solution.py:306
  69.3 0.0 collective-permute-start.6
  69.3 0.0 collective-permute-done.8.refs_0_
  69.3 0.1 add_on.9
  69.4 2.3 %collective-permute-start.11 = (bf16[512,256]{1,0:T(8,128)(2,1)S(1)}, bf16[512,256]{1,0:T(8,128)(2,1)S(1)}, u32[]{:S(2)}, u32[]{:S(2)}) collective-permute-start(bf16[512,256]{1,0:T(8,128)(2,1)S(1)} %get-tuple-element.38), channel_id=1, source_target_pairs={{0,3},{1,14},{2,5},{3,0},{4,7},{5,2},{6,9},{7,4},{8,11},{9,6},{10,... | collective-permute-start | bytes 786440 | tf_op jit(solution)/shard_map/ppermute | solution.py:302
  71.7 1.3 %collective-permute-start.9 = (bf16[512,256]{1,0:T(8,128)(2,1)S(1)}, bf16[512,256]{1,0:T(8,128)(2,1)S(1)}, u32[]{:S(2)}, u32[]{:S(2)}) collective-permute-start(bf16[512,256]{1,0:T(8,128)(2,1)S(1)} %get-tuple-element.36), channel_id=1, source_target_pairs={{0,2},{1,15},{2,4},{3,1},{4,6},{5,3},{6,8},{7,5},{8,10},{9,7},{10,... | collective-permute-start | bytes 786440 | tf_op jit(solution)/shard_map/ppermute | solution.py:301
  73.0 4.1 %products.17 = (f32[2,512,256]{2,1,0:T(8,128)S(1)}, f32[8,256]{1,0:T(8,128)S(1)}) custom-call(f32[16,40,128]{2,1,0:T(8,128)S(1)} %all_to_all.5.blocks_ref, bf16[2,512,1024]{2,1,0:T(8,128)(2,1)} %own_ref.17, bf16[2,512,1024]{2,1,0:T(8,128)(2,1)} %collective-permute-done.1.other_ref), custom_call_target="tpu_custom_call" | custom-call | flops 1073741824 | bytes 12582912 | tf_op jit(solution)/shard_map/products/pallas_call | solution.py:142
  77.1 2.0 %collective-permute-done.11.d_ref = bf16[512,256]{1,0:T(8,128)(2,1)S(1)} collective-permute-done((bf16[512,256]{1,0:T(8,128)(2,1)S(1)}, bf16[512,256]{1,0:T(8,128)(2,1)S(1)}, u32[]{:S(2)}, u32[]{:S(2)}) %collective-permute-start.11) | collective-permute-done | bytes 262176 | tf_op jit(solution)/shard_map/ppermute | solution.py:302
  79.1 2.1 %collective-permute-done.9.b_ref = bf16[512,256]{1,0:T(8,128)(2,1)S(1)} collective-permute-done((bf16[512,256]{1,0:T(8,128)(2,1)S(1)}, bf16[512,256]{1,0:T(8,128)(2,1)S(1)}, u32[]{:S(2)}, u32[]{:S(2)}) %collective-permute-start.9) | collective-permute-done | bytes 262176 | tf_op jit(solution)/shard_map/ppermute | solution.py:301
  81.2 0.0 collective-permute-done.10.c_ref
  81.2 0.0 collective-permute-done.6.a_ref
  81.2 1.1 %finish.1 = f32[2,512,256]{2,1,0:T(8,128)} custom-call(bf16[528,256]{1,0:T(8,128)(2,1)S(1)} %collective-permute-done.6.a_ref, bf16[512,256]{1,0:T(8,128)(2,1)S(1)} %collective-permute-done.9.b_ref, bf16[528,256]{1,0:T(8,128)(2,1)S(1)} %collective-permute-done.10.c_ref, bf16[512,256]{1,0:T(8,128)(2,1)S(1)} %collective-permute-done.11.d_ref, ...), custom_call_target="tpu_custom_call" | custom-call | flops 26214400 | bytes 4194304 | tf_op jit(solution)/shard_map/finish/pallas_call | solution.py:214
  (5 shorter events, 0.0 us)
Async XLA Ops:
  0.0 7.3 %collective-permute-start.1 = (bf16[2,512,1024]{2,1,0:T(8,128)(2,1)}, bf16[2,512,1024]{2,1,0:T(8,128)(2,1)}, u32[]{:S(2)}, u32[]{:S(2)}) collective-permute-start(bf16[2,512,1024]{2,1,0:T(8,128)(2,1)} %own_ref.17), channel_id=1, source_target_pairs={{0,1},{1,0},{2,3},{3,2},{4,5},{5,4},{6,7},{7,6},{8,9},{9,8},{10,11... | collective-permute-start | bytes 6291464 | tf_op jit(solution)/shard_map/ppermute | solution.py:274
  4.6 3.5 %collective-permute-start = (f32[24,128]{1,0:T(8,128)}, f32[24,128]{1,0:T(8,128)S(1)}, u32[]{:S(2)}, u32[]{:S(2)}) collective-permute-start(f32[24,128]{1,0:T(8,128)} %pack.1), channel_id=1, source_target_pairs={{0,0},{1,1},{2,2},{3,3},{4,4},{5,5},{6,6},{7,7},{8,8},{9,9},{10,10... | collective-permute-start | bytes 36872 | tf_op jit(solution)/shard_map/ppermute | solution.py:281
  29.6 13.3 %collective-permute-start.3 = (bf16[528,256]{1,0:T(8,128)(2,1)S(1)}, bf16[528,256]{1,0:T(8,128)(2,1)S(1)}, u32[]{:S(2)}, u32[]{:S(2)}) collective-permute-start(bf16[528,256]{1,0:T(8,128)(2,1)S(1)} %products.10), channel_id=1, source_target_pairs={{0,2},{1,15},{2,4},{3,1},{4,6},{5,3},{6,8},{7,5},{8,10},{9,7},{10,... | collective-permute-start | bytes 811016 | tf_op jit(solution)/shard_map/ppermute | solution.py:291
  36.6 6.3 %collective-permute-start.2 = (bf16[528,256]{1,0:T(8,128)(2,1)S(1)}, bf16[528,256]{1,0:T(8,128)(2,1)S(1)}, u32[]{:S(2)}, u32[]{:S(2)}) collective-permute-start(bf16[528,256]{1,0:T(8,128)(2,1)S(1)} %products.9), channel_id=1, source_target_pairs={{0,2},{1,15},{2,4},{3,1},{4,6},{5,3},{6,8},{7,5},{8,10},{9,7},{10,... | collective-permute-start | bytes 811016 | tf_op jit(solution)/shard_map/ppermute | solution.py:291
  43.0 8.6 %collective-permute-start.4 = (bf16[528,512]{1,0:T(8,128)(2,1)S(1)}, bf16[528,512]{1,0:T(8,128)(2,1)S(1)}, u32[]{:S(2)}, u32[]{:S(2)}) collective-permute-start(bf16[528,512]{1,0:T(8,128)(2,1)S(1)} %add_on.5), channel_id=1, source_target_pairs={{0,2},{1,15},{2,4},{3,1},{4,6},{5,3},{6,8},{7,5},{8,10},{9,7},{10,... | collective-permute-start | bytes 1622024 | tf_op jit(solution)/shard_map/ppermute | solution.py:297
  43.8 13.3 %collective-permute-start.7 = (bf16[512,512]{1,0:T(8,128)(2,1)S(1)}, bf16[512,512]{1,0:T(8,128)(2,1)S(1)}, u32[]{:S(2)}, u32[]{:S(2)}) collective-permute-start(bf16[512,512]{1,0:T(8,128)(2,1)S(1)} %get-tuple-element.33), channel_id=1, source_target_pairs={{0,2},{1,15},{2,4},{3,1},{4,6},{5,3},{6,8},{7,5},{8,10},{9,7},{10,... | collective-permute-start | bytes 1572872 | tf_op jit(solution)/shard_map/ppermute | solution.py:293
  51.6 13.5 %collective-permute-start.5 = (bf16[528,512]{1,0:T(8,128)(2,1)S(1)}, bf16[528,512]{1,0:T(8,128)(2,1)S(1)}, u32[]{:S(2)}, u32[]{:S(2)}) collective-permute-start(bf16[528,512]{1,0:T(8,128)(2,1)S(1)} %add_on.6), channel_id=1, source_target_pairs={{0,2},{1,15},{2,4},{3,1},{4,6},{5,3},{6,8},{7,5},{8,10},{9,7},{10,... | collective-permute-start | bytes 1622024 | tf_op jit(solution)/shard_map/ppermute | solution.py:297
  57.3 12.0 %collective-permute-start.8 = (bf16[512,512]{1,0:T(8,128)(2,1)S(1)}, bf16[512,512]{1,0:T(8,128)(2,1)S(1)}, u32[]{:S(2)}, u32[]{:S(2)}) collective-permute-start(bf16[512,512]{1,0:T(8,128)(2,1)S(1)} %add_on.8), channel_id=1, source_target_pairs={{0,2},{1,15},{2,4},{3,1},{4,6},{5,3},{6,8},{7,5},{8,10},{9,7},{10,... | collective-permute-start | bytes 1572872 | tf_op jit(solution)/shard_map/ppermute | solution.py:301
  65.3 15.9 %collective-permute-start.10 = (bf16[528,256]{1,0:T(8,128)(2,1)S(1)}, bf16[528,256]{1,0:T(8,128)(2,1)S(1)}, u32[]{:S(2)}, u32[]{:S(2)}) collective-permute-start(bf16[528,256]{1,0:T(8,128)(2,1)S(1)} %get-tuple-element.37), channel_id=1, source_target_pairs={{0,3},{1,14},{2,5},{3,0},{4,7},{5,2},{6,9},{7,4},{8,11},{9,6},{10,... | collective-permute-start | bytes 811016 | tf_op jit(solution)/shard_map/ppermute | solution.py:306
  69.3 11.9 %collective-permute-start.6 = (bf16[528,256]{1,0:T(8,128)(2,1)S(1)}, bf16[528,256]{1,0:T(8,128)(2,1)S(1)}, u32[]{:S(2)}, u32[]{:S(2)}) collective-permute-start(bf16[528,256]{1,0:T(8,128)(2,1)S(1)} %get-tuple-element.32), channel_id=1, source_target_pairs={{0,2},{1,15},{2,4},{3,1},{4,6},{5,3},{6,8},{7,5},{8,10},{9,7},{10,... | collective-permute-start | bytes 811016 | tf_op jit(solution)/shard_map/ppermute | solution.py:305
  69.4 9.7 %collective-permute-start.11 = (bf16[512,256]{1,0:T(8,128)(2,1)S(1)}, bf16[512,256]{1,0:T(8,128)(2,1)S(1)}, u32[]{:S(2)}, u32[]{:S(2)}) collective-permute-start(bf16[512,256]{1,0:T(8,128)(2,1)S(1)} %get-tuple-element.38), channel_id=1, source_target_pairs={{0,3},{1,14},{2,5},{3,0},{4,7},{5,2},{6,9},{7,4},{8,11},{9,6},{10,... | collective-permute-start | bytes 786440 | tf_op jit(solution)/shard_map/ppermute | solution.py:302
  71.7 9.5 %collective-permute-start.9 = (bf16[512,256]{1,0:T(8,128)(2,1)S(1)}, bf16[512,256]{1,0:T(8,128)(2,1)S(1)}, u32[]{:S(2)}, u32[]{:S(2)}) collective-permute-start(bf16[512,256]{1,0:T(8,128)(2,1)S(1)} %get-tuple-element.36), channel_id=1, source_target_pairs={{0,2},{1,15},{2,4},{3,1},{4,6},{5,3},{6,8},{7,5},{8,10},{9,7},{10,... | collective-permute-start | bytes 786440 | tf_op jit(solution)/shard_map/ppermute | solution.py:301

commit v3 on v2

--- a/solution.py
+++ b/solution.py
@@ -16,7 +16,7 @@
 BF16 = jnp.bfloat16
 
 
-def look_up(core, col, blocks_ref, low_ref, shift_ref, *, step, value_rows, first, count):
+def look_up(core, col, blocks_ref, low_ref, shift_ref, *, step, value_rows, count):
     places = blocks_ref.shape[0]
     table = blocks_ref[:, :value_rows, :].reshape(places * value_rows, LANES)
     high = table.astype(BF16)
@@ -44,7 +44,7 @@
     spots = jnp.transpose(rows)
     row_ids = lax.broadcasted_iota(jnp.int32, (LANES, places * value_rows), 1).astype(F32)
     lane_ids = lax.broadcasted_iota(jnp.int32, (LANES, LANES), 1).astype(F32)
-    for tile in range(first, first + count):
+    for tile in range(count):
         picks = [jnp.where(row_ids == spots[:, k + tile : k + tile + 1], 1.0, 0.0).astype(BF16) for k in (0, 8)]
         got = jnp.dot(jnp.concatenate(picks, axis=0), split, preferred_element_type=F32)
         got = (got[:, :LANES] + got[:, LANES : 2 * LANES]) + got[:, 2 * LANES :]
@@ -53,16 +53,21 @@
             for k, at in ((4, 0), (12, LANES))
         )
         shift = spots[:, 16 + tile : 17 + tile] * (upper - lower)
-        at = slice((tile - first) * LANES, (tile - first + 1) * LANES)
+        at = slice(tile * LANES, (tile + 1) * LANES)
         low_ref[at, :] = jnp.broadcast_to(lower, (LANES, LANES))
         shift_ref[at, :] = jnp.broadcast_to(shift, (LANES, LANES))
 
 
-def multiply(blocks_ref, own_ref, other_ref, *refs, step, which, first, sends, tall):
-    out_ref, norm_ref = refs[0], None if tall else refs[1]
-    low_ref, shift_ref, block_ref, square_ref, halves_ref, sems = refs[-6:]
+def multiply(blocks_ref, own_ref, other_ref, *refs, step, which, sends, tall, found):
+    block_ref, square_ref, halves_ref, sems = refs[-4:]
+    refs = refs[:-4]
+    if found:
+        low_ref, shift_ref, *outs = refs
+    else:
+        *outs, low_ref, shift_ref = refs
+    out_ref, norm_ref = outs[0], None if tall else outs[1]
     columns = low_ref.shape[0]
-    rows, width = halves_ref.shape[2:]
+    _, width = halves_ref.shape[2:]
     tiles = width // LANES
     value_rows = 2 * tiles
     core = lax.axis_index("depth").astype(jnp.int32)
@@ -78,9 +83,8 @@
     for pair in loads:
         for load in pair:
             load.start()
-    look_up(
-        core, col, blocks_ref, low_ref, shift_ref, step=step, value_rows=value_rows, first=first, count=columns // LANES
-    )
+    if not found:
+        look_up(core, col, blocks_ref, low_ref, shift_ref, step=step, value_rows=value_rows, count=columns // LANES)
     for u, half in enumerate(halves):
         values = [[blocks_ref[s, pl.ds(half * tiles + t, 1), :] for t in range(tiles)] for s in range(2)]
         edge = blocks_ref[jnp.where(half == 0, blocks_ref.shape[0] - 1, 0), value_rows + 8 :, :]
@@ -95,28 +99,38 @@
                     for tile in range(tiles):
                         cauchy = seams[source][tile] / ((values[source][tile] - low) - shift)
                         square = square + cauchy * cauchy
-                        block_ref[
-                            start : start + PIECE, source * width + tile * LANES : source * width + (tile + 1) * LANES
-                        ] = cauchy.astype(BF16)
+                        begin = source * width + tile * LANES
+                        block_ref[start : start + PIECE, begin : begin + LANES] = cauchy.astype(BF16)
                 square_ref[start : start + PIECE, :] = square
-            if part == 0:
+            if part == WAIT_AT[found] or part == columns // 256 - 1 and columns // 256 <= WAIT_AT[found]:
                 for load in loads[u]:
                     load.wait()
-            at = slice(part * 256, (part + 1) * 256)
-            nt = (((1,), (1,)), ((), ()))
-            product = lax.dot_general(halves_ref[u, 0], block_ref[at, :width], nt, preferred_element_type=F32)
-            product = product + lax.dot_general(halves_ref[u, 1], block_ref[at, width:], nt, preferred_element_type=F32)
-            norm = jnp.sum(jnp.transpose(square_ref[at, :]), axis=0, keepdims=True)
-            if sends:
-                out_ref[:rows, at] = product.astype(BF16)
-            else:
-                out_ref[u, :, at] = product
-            if tall:
-                put_norm(out_ref, rows, at, norm)
-            elif u == 0:
-                norm_ref[:, at] = jnp.broadcast_to(norm, (8, 256))
-            else:
-                norm_ref[:, at] += jnp.broadcast_to(norm, (8, 256))
+                for done in range(part):
+                    multiply_out(u, done, out_ref, norm_ref, block_ref, square_ref, halves_ref, sends, tall)
+            if part >= WAIT_AT[found] or columns // 256 <= WAIT_AT[found]:
+                multiply_out(u, part, out_ref, norm_ref, block_ref, square_ref, halves_ref, sends, tall)
+
+
+WAIT_AT = {False: 0, True: 1}
+
+
+def multiply_out(u, part, out_ref, norm_ref, block_ref, square_ref, halves_ref, sends, tall):
+    nt = (((1,), (1,)), ((), ()))
+    rows, width = halves_ref.shape[2:]
+    at = slice(part * 256, (part + 1) * 256)
+    product = lax.dot_general(halves_ref[u, 0], block_ref[at, :width], nt, preferred_element_type=F32)
+    product = product + lax.dot_general(halves_ref[u, 1], block_ref[at, width:], nt, preferred_element_type=F32)
+    norm = jnp.sum(jnp.transpose(square_ref[at, :]), axis=0, keepdims=True)
+    if sends:
+        out_ref[:rows, at] = product.astype(BF16)
+    else:
+        out_ref[u, :, at] = product
+    if tall:
+        put_norm(out_ref, rows, at, norm)
+    elif u == 0:
+        norm_ref[:, at] = jnp.broadcast_to(norm, (8, 256))
+    else:
+        norm_ref[:, at] += jnp.broadcast_to(norm, (8, 256))
 
 
 def put_norm(out_ref, rows, at, norm):
@@ -130,7 +144,7 @@
 HBM = pl.BlockSpec(memory_space=pl.ANY)
 
 
-def products(which, blocks, own, other, step, columns, first=0, sends=False, tall=False):
+def products(which, blocks, own, other, step, columns, sends=False, tall=False, found=()):
     n = len(which)
     rows, width = own.shape[1:]
     if sends:
@@ -139,25 +153,29 @@
         out_shape = [jax.ShapeDtypeStruct((n, rows, columns), F32)]
     if not tall:
         out_shape.append(jax.ShapeDtypeStruct((8, columns), F32))
+    scratch = [
+        pltpu.VMEM((columns, 2 * width), BF16),
+        pltpu.VMEM((columns, LANES), F32),
+        pltpu.VMEM((n, 2, rows, width), BF16),
+        pltpu.SemaphoreType.DMA((n, 2)),
+    ]
+    keeps = not found and not tall and n == 1
+    if keeps:
+        out_shape += [jax.ShapeDtypeStruct((columns, LANES), F32)] * 2
+    elif not found:
+        scratch = [pltpu.VMEM((columns, LANES), F32)] * 2 + scratch
     return pl.pallas_call(
-        functools.partial(multiply, step=step, which=which, first=first, sends=sends, tall=tall),
+        functools.partial(multiply, step=step, which=which, sends=sends, tall=tall, found=bool(found)),
         out_shape=out_shape,
-        in_specs=[VMEM, HBM, HBM],
+        in_specs=[VMEM, HBM, HBM] + [VMEM] * len(found),
         out_specs=[VMEM] * len(out_shape),
-        scratch_shapes=[
-            pltpu.VMEM((columns, LANES), F32),
-            pltpu.VMEM((columns, LANES), F32),
-            pltpu.VMEM((columns, 2 * width), BF16),
-            pltpu.VMEM((columns, LANES), F32),
-            pltpu.VMEM((n, 2, rows, width), BF16),
-            pltpu.SemaphoreType.DMA((n, 2)),
-        ],
+        scratch_shapes=scratch,
         compiler_params=pltpu.CompilerParams(vmem_limit_bytes=52 << 20),
         cost_estimate=pl.CostEstimate(
             flops=n * rows * columns * width * 4, bytes_accessed=n * 6 << 20, transcendentals=n * columns * width * 2
         ),
         name="products",
-    )(blocks, own, other)
+    )(blocks, own, other, *found)
 
 
 def add_on(*refs, pieces):
@@ -284,23 +302,21 @@
     parcel = jnp.concatenate([theirs] + edge, axis=0)
     blocks = lax.all_to_all(jnp.broadcast_to(parcel[None], (nrows,) + parcel.shape), ROW, 0, 0, tiled=True)
 
-    multiplied = functools.partial(products, blocks=blocks, own=halves, other=other)
-    a = []
-    for first in range(0, columns // LANES, 2):
-        (part,) = multiplied(("first",), step=reach, first=first, columns=2 * LANES, sends=True, tall=True)
-        a.append(lax.ppermute(part, ring, straight))
-    b, norm = multiplied(("second",), step=reach - 1, columns=columns, sends=True)
+    multiplied = functools.partial(products, blocks=blocks, own=halves, other=other, columns=columns)
+    (a,) = multiplied(("first",), step=reach, sends=True, tall=True)
+    a = lax.ppermute(a, ring, straight)
+    b, norm, *found = multiplied(("second",), step=reach - 1, sends=True)
     b = lax.ppermute(b, ring, straight)
-    product, more = multiplied(("first",), step=reach - 1, columns=columns)
-    (a,) = added(a, product, norm + more, 1)
+    product, more = multiplied(("first",), step=reach - 1, found=found)
+    (a,) = added([a], product, norm + more, 1)
     for step in range(reach - 2, 0, -1):
         a = lax.ppermute(a, ring, straight)
-        product, norm = multiplied(("second",), step=step, columns=columns)
+        product, norm, *found = multiplied(("second",), step=step)
         pieces = 1 if step > 1 else 2
         b, *b_across = added([b], product, norm, pieces)
         b = lax.ppermute(b, ring, straight)
         b_across = [lax.ppermute(x, ring, across) for x in b_across]
-        product, more = multiplied(("first",), step=step, columns=columns)
+        product, more = multiplied(("first",), step=step, found=found)
         a, *a_across = added([a], product, norm + more, pieces)
     a = lax.ppermute(a, ring, straight)
     a_across = [lax.ppermute(x, ring, across) for x in a_across]

time: 83.3 us -> 84.4 us (1.013)
  starting transfers between devices: 21.5 us -> 28.3 us
  waiting for transfers between devices: 9.83 us -> 6.95 us
  Pallas kernels: 30.1 us -> 27.6 us
    ppermute x3 -> x4, starting transfers between devices: 2.61 us -> 11.1 us  [body(): a = lax.ppermute(a, ring, straight)]
    ppermute x2 -> x0, starting transfers between devices: 4.75 us -> none  [body(): a.append(lax.ppermute(part, ring, straight))]
    ppermute x3, waiting for transfers between devices: 5.82 us -> 2.32 us  [body(): b = lax.ppermute(b, ring, straight)]
    pallas_call x9 -> x8, Pallas kernels: 27.2 us -> 24.7 us  [products(): pl.pallas_call(functools.partial(multiply, step=step, which=which, sends=...]
    ppermute x3, starting transfers between devices: 3.32 us -> 5.41 us  [body(): b = lax.ppermute(b, ring, straight)]
    ppermute x1, waiting for transfers between devices: 2.03 us -> 3.32 us  [body(): b_across = [lax.ppermute(x, ring, across) for x in b_across]]
    ppermute x1, starting transfers between devices: 2.3 us -> 3.41 us  [body(): b_across = [lax.ppermute(x, ring, across) for x in b_across]]
  transfers between devices with their start and end apart: 12 -> 11, of which waited for: 5 -> 5; matrix products, arithmetic and copies ran while one was open for 2% -> 2% of each run, Pallas kernels for 32% -> 28%
where the time goes in v3:
time: 84.4 us; the launch traced here: 83.8 us
  starting transfers between devices  28.3 us (34%)
  Pallas kernels  27.6 us (33%)
  blocking collectives  19.1 us (23%)
  waiting for transfers between devices  6.95 us (8%)
  other arithmetic  1.51 us (2%)
    pallas_call x8, Pallas kernels, products(): pl.pallas_call(functools.partial(multiply, step=step, which=which, sends=...  24.7 us
    all_to_all x1, blocking collectives, body(): lax.all_to_all(jnp.broadcast_to(parcel[None], (nrows,) + parcel.shape), R...  19.1 us
    ppermute x4, starting transfers between devices, body(): a = lax.ppermute(a, ring, straight)  11.1 us
    ppermute x3, starting transfers between devices, body(): b = lax.ppermute(b, ring, straight)  5.41 us
    ppermute x1, starting transfers between devices, body(): a_across = [lax.ppermute(x, ring, across) for x in a_across]  3.76 us
    ppermute x1, starting transfers between devices, body(): b_across = [lax.ppermute(x, ring, across) for x in b_across]  3.41 us
    ppermute x1, waiting for transfers between devices, body(): b_across = [lax.ppermute(x, ring, across) for x in b_across]  3.32 us
    ppermute x1, starting transfers between devices, body(): other = lax.ppermute(halves, 'depth', [(0, 1), (1, 0)])  3.2 us
  transfers between devices with their start and end apart: 11, of which 5 were waited for; matrix products, arithmetic and copies ran while one was open for 2% of the time, Pallas kernels for 28%

profile of v3, /device:TPU:1, one launch (start us, length us, event | category | flops | bytes accessed | tf_op | source)
XLA Modules:
  0.0 83.8 jit_solution(12395504917046261253)
XLA Ops:
  0.0 3.2 %collective-permute-start.1 = (bf16[2,512,1024]{2,1,0:T(8,128)(2,1)}, bf16[2,512,1024]{2,1,0:T(8,128)(2,1)}, u32[]{:S(2)}, u32[]{:S(2)}) collective-permute-start(bf16[2,512,1024]{2,1,0:T(8,128)(2,1)} %own_ref.15), channel_id=1, source_target_pairs={{0,1},{1,0},{2,3},{3,2},{4,5},{5,4},{6,7},{7,6},{8,9},{9,8},{10,11... | collective-permute-start | bytes 6291464 | tf_op jit(solution)/shard_map/ppermute | solution.py:292
  3.2 1.3 %pack.1 = f32[24,128]{1,0:T(8,128)} custom-call(f32[2,1024]{1,0:T(2,128)} %spectrum_ref.1, s32[1,512]{1,0:T(1,128)} %bitcast.6, f32[1,512]{1,0:T(1,128)} %bitcast.7), custom_call_target="tpu_custom_call" | custom-call | flops 1000 | bytes 400000 | tf_op jit(solution)/shard_map/pack/pallas_call | solution.py:265
  4.6 1.4 %collective-permute-start = (f32[24,128]{1,0:T(8,128)}, f32[24,128]{1,0:T(8,128)S(1)}, u32[]{:S(2)}, u32[]{:S(2)}) collective-permute-start(f32[24,128]{1,0:T(8,128)} %pack.1), channel_id=1, source_target_pairs={{0,0},{1,1},{2,2},{3,3},{4,4},{5,5},{6,6},{7,7},{8,8},{9,9},{10,10... | collective-permute-start | bytes 36872 | tf_op jit(solution)/shard_map/ppermute | solution.py:299
  5.9 0.7 fusion
  6.7 0.7 collective-permute-done.1.other_ref
  7.3 0.7 fusion.1
  8.1 0.0 collective-permute-done
  8.1 19.1 %all_to_all.5.blocks_ref = f32[16,40,128]{2,1,0:T(8,128)S(1)} all-to-all(f32[16,40,128]{2,1,0:T(8,128)S(1)} %broadcast_in_dim.2), channel_id=1, replica_groups=mesh['row_0'=4,'row_1'=4,'col'=8,'depth'=2] {'row_0','row_1'}, dimensions={0} | all-to-all | bytes 655360 | tf_op jit(solution)/shard_map/all_to_all | solution.py:303
  27.2 3.1 %products.8 = bf16[528,512]{1,0:T(8,128)(2,1)S(1)} custom-call(f32[16,40,128]{2,1,0:T(8,128)S(1)} %all_to_all.5.blocks_ref, bf16[2,512,1024]{2,1,0:T(8,128)(2,1)} %own_ref.15, bf16[2,512,1024]{2,1,0:T(8,128)(2,1)} %collective-permute-done.1.other_ref), custom_call_target="tpu_custom_call" | custom-call | flops 1073741824 | bytes 6291456 | tf_op jit(solution)/shard_map/products/pallas_call | solution.py:167
  30.3 4.7 %collective-permute-start.2 = (bf16[528,512]{1,0:T(8,128)(2,1)S(1)}, bf16[528,512]{1,0:T(8,128)(2,1)S(1)}, u32[]{:S(2)}, u32[]{:S(2)}) collective-permute-start(bf16[528,512]{1,0:T(8,128)(2,1)S(1)} %products.8), channel_id=1, source_target_pairs={{0,2},{1,15},{2,4},{3,1},{4,6},{5,3},{6,8},{7,5},{8,10},{9,7},{10,... | collective-permute-start | bytes 1622024 | tf_op jit(solution)/shard_map/ppermute | solution.py:307
  35.0 3.0 %products.9 = (bf16[512,512]{1,0:T(8,128)(2,1)S(1)}, f32[8,512]{1,0:T(8,128)S(1)}, f32[512,128]{1,0:T(8,128)S(1)}, f32[512,128]{1,0:T(8,128)S(1)}) custom-call(f32[16,40,128]{2,1,0:T(8,128)S(1)} %all_to_all.5.blocks_ref, bf16[2,512,1024]{2,1,0:T(8,128)(2,1)} %own_ref.15, bf16[2,512,1024]{2,1,0:T(8,128)(2,1)} %collective-permute-done.1.other_ref), custom_call_target="tpu_custom_call" | custom-call | flops 1073741824 | bytes 6291456 | tf_op jit(solution)/shard_map/products/pallas_call | solution.py:167
  37.9 2.9 %products.10 = (f32[1,512,512]{2,1,0:T(8,128)S(1)}, f32[8,512]{1,0:T(8,128)S(1)}) custom-call(f32[16,40,128]{2,1,0:T(8,128)S(1)} %all_to_all.5.blocks_ref, bf16[2,512,1024]{2,1,0:T(8,128)(2,1)} %own_ref.15, bf16[2,512,1024]{2,1,0:T(8,128)(2,1)} %collective-permute-done.1.other_ref, f32[512,128]{1,0:T(8,128)S(1)} %get-tuple-element.29.refs_0_, ...), custom_call_target="tpu_custom_call" | custom-call | flops 1073741824 | bytes 6291456 | tf_op jit(solution)/shard_map/products/pallas_call | solution.py:167
  40.8 0.5 collective-permute-done.2.refs_0_
  41.3 0.1 add_on.5
  41.4 3.2 %collective-permute-start.3 = (bf16[528,512]{1,0:T(8,128)(2,1)S(1)}, bf16[528,512]{1,0:T(8,128)(2,1)S(1)}, u32[]{:S(2)}, u32[]{:S(2)}) collective-permute-start(bf16[528,512]{1,0:T(8,128)(2,1)S(1)} %add_on.5), channel_id=1, source_target_pairs={{0,2},{1,15},{2,4},{3,1},{4,6},{5,3},{6,8},{7,5},{8,10},{9,7},{10,... | collective-permute-start | bytes 1622024 | tf_op jit(solution)/shard_map/ppermute | solution.py:313
  44.6 0.3 collective-permute-start.6
  44.8 3.0 %products.11 = (f32[1,512,512]{2,1,0:T(8,128)S(1)}, f32[8,512]{1,0:T(8,128)S(1)}, f32[512,128]{1,0:T(8,128)S(1)}, f32[512,128]{1,0:T(8,128)S(1)}) custom-call(f32[16,40,128]{2,1,0:T(8,128)S(1)} %all_to_all.5.blocks_ref, bf16[2,512,1024]{2,1,0:T(8,128)(2,1)} %own_ref.15, bf16[2,512,1024]{2,1,0:T(8,128)(2,1)} %collective-permute-done.1.other_ref), custom_call_target="tpu_custom_call" | custom-call | flops 1073741824 | bytes 6291456 | tf_op jit(solution)/shard_map/products/pallas_call | solution.py:167
  47.8 2.9 %products.12 = (f32[1,512,512]{2,1,0:T(8,128)S(1)}, f32[8,512]{1,0:T(8,128)S(1)}) custom-call(f32[16,40,128]{2,1,0:T(8,128)S(1)} %all_to_all.5.blocks_ref, bf16[2,512,1024]{2,1,0:T(8,128)(2,1)} %own_ref.15, bf16[2,512,1024]{2,1,0:T(8,128)(2,1)} %collective-permute-done.1.other_ref, f32[512,128]{1,0:T(8,128)S(1)} %get-tuple-element.34.refs_0_, ...), custom_call_target="tpu_custom_call" | custom-call | flops 1073741824 | bytes 6291456 | tf_op jit(solution)/shard_map/products/pallas_call | solution.py:167
  50.7 0.2 collective-permute-done.3.refs_0_
  50.9 0.1 add_on.6
  51.0 3.2 %collective-permute-start.4 = (bf16[528,512]{1,0:T(8,128)(2,1)S(1)}, bf16[528,512]{1,0:T(8,128)(2,1)S(1)}, u32[]{:S(2)}, u32[]{:S(2)}) collective-permute-start(bf16[528,512]{1,0:T(8,128)(2,1)S(1)} %add_on.6), channel_id=1, source_target_pairs={{0,2},{1,15},{2,4},{3,1},{4,6},{5,3},{6,8},{7,5},{8,10},{9,7},{10,... | collective-permute-start | bytes 1622024 | tf_op jit(solution)/shard_map/ppermute | solution.py:313
  54.2 2.3 %collective-permute-done.6.refs_0_ = bf16[512,512]{1,0:T(8,128)(2,1)S(1)} collective-permute-done((bf16[512,512]{1,0:T(8,128)(2,1)S(1)}, bf16[512,512]{1,0:T(8,128)(2,1)S(1)}, u32[]{:S(2)}, u32[]{:S(2)}) %collective-permute-start.6) | collective-permute-done | bytes 524320 | tf_op jit(solution)/shard_map/ppermute | solution.py:309
  56.5 0.1 add_on.8
  56.6 3.2 %collective-permute-start.7 = (bf16[512,512]{1,0:T(8,128)(2,1)S(1)}, bf16[512,512]{1,0:T(8,128)(2,1)S(1)}, u32[]{:S(2)}, u32[]{:S(2)}) collective-permute-start(bf16[512,512]{1,0:T(8,128)(2,1)S(1)} %add_on.8), channel_id=1, source_target_pairs={{0,2},{1,15},{2,4},{3,1},{4,6},{5,3},{6,8},{7,5},{8,10},{9,7},{10,... | collective-permute-start | bytes 1572872 | tf_op jit(solution)/shard_map/ppermute | solution.py:317
  59.8 3.0 %products.13 = (f32[1,512,512]{2,1,0:T(8,128)S(1)}, f32[8,512]{1,0:T(8,128)S(1)}, f32[512,128]{1,0:T(8,128)S(1)}, f32[512,128]{1,0:T(8,128)S(1)}) custom-call(f32[16,40,128]{2,1,0:T(8,128)S(1)} %all_to_all.5.blocks_ref, bf16[2,512,1024]{2,1,0:T(8,128)(2,1)} %own_ref.15, bf16[2,512,1024]{2,1,0:T(8,128)(2,1)} %collective-permute-done.1.other_ref), custom_call_target="tpu_custom_call" | custom-call | flops 1073741824 | bytes 6291456 | tf_op jit(solution)/shard_map/products/pallas_call | solution.py:167
  62.8 2.9 %products.14 = (f32[1,512,512]{2,1,0:T(8,128)S(1)}, f32[8,512]{1,0:T(8,128)S(1)}) custom-call(f32[16,40,128]{2,1,0:T(8,128)S(1)} %all_to_all.5.blocks_ref, bf16[2,512,1024]{2,1,0:T(8,128)(2,1)} %own_ref.15, bf16[2,512,1024]{2,1,0:T(8,128)(2,1)} %collective-permute-done.1.other_ref, f32[512,128]{1,0:T(8,128)S(1)} %get-tuple-element.39.refs_0_, ...), custom_call_target="tpu_custom_call" | custom-call | flops 1073741824 | bytes 6291456 | tf_op jit(solution)/shard_map/products/pallas_call | solution.py:167
  65.6 0.0 collective-permute-done.4.refs_0_
  65.6 0.1 add_on.7
  65.8 0.1 collective-permute-start.5
  65.9 3.8 %collective-permute-start.9 = (bf16[528,256]{1,0:T(8,128)(2,1)S(1)}, bf16[528,256]{1,0:T(8,128)(2,1)S(1)}, u32[]{:S(2)}, u32[]{:S(2)}) collective-permute-start(bf16[528,256]{1,0:T(8,128)(2,1)S(1)} %get-tuple-element.49), channel_id=1, source_target_pairs={{0,3},{1,14},{2,5},{3,0},{4,7},{5,2},{6,9},{7,4},{8,11},{9,6},{10,... | collective-permute-start | bytes 811016 | tf_op jit(solution)/shard_map/ppermute | solution.py:322
  69.6 0.0 collective-permute-done.7.refs_0_
  69.6 0.1 add_on.9
  69.8 1.9 %collective-permute-start.8 = (bf16[512,256]{1,0:T(8,128)(2,1)S(1)}, bf16[512,256]{1,0:T(8,128)(2,1)S(1)}, u32[]{:S(2)}, u32[]{:S(2)}) collective-permute-start(bf16[512,256]{1,0:T(8,128)(2,1)S(1)} %get-tuple-element.48), channel_id=1, source_target_pairs={{0,2},{1,15},{2,4},{3,1},{4,6},{5,3},{6,8},{7,5},{8,10},{9,7},{10,... | collective-permute-start | bytes 786440 | tf_op jit(solution)/shard_map/ppermute | solution.py:317
  71.7 3.4 %collective-permute-start.10 = (bf16[512,256]{1,0:T(8,128)(2,1)S(1)}, bf16[512,256]{1,0:T(8,128)(2,1)S(1)}, u32[]{:S(2)}, u32[]{:S(2)}) collective-permute-start(bf16[512,256]{1,0:T(8,128)(2,1)S(1)} %get-tuple-element.50), channel_id=1, source_target_pairs={{0,3},{1,14},{2,5},{3,0},{4,7},{5,2},{6,9},{7,4},{8,11},{9,6},{10,... | collective-permute-start | bytes 786440 | tf_op jit(solution)/shard_map/ppermute | solution.py:318
  75.1 4.1 %products.15 = (f32[2,512,256]{2,1,0:T(8,128)S(1)}, f32[8,256]{1,0:T(8,128)S(1)}) custom-call(f32[16,40,128]{2,1,0:T(8,128)S(1)} %all_to_all.5.blocks_ref, bf16[2,512,1024]{2,1,0:T(8,128)(2,1)} %own_ref.15, bf16[2,512,1024]{2,1,0:T(8,128)(2,1)} %collective-permute-done.1.other_ref), custom_call_target="tpu_custom_call" | custom-call | flops 1073741824 | bytes 12582912 | tf_op jit(solution)/shard_map/products/pallas_call | solution.py:167
  79.2 0.0 collective-permute-done.8.b_ref
  79.2 3.3 %collective-permute-done.10.d_ref = bf16[512,256]{1,0:T(8,128)(2,1)S(1)} collective-permute-done((bf16[512,256]{1,0:T(8,128)(2,1)S(1)}, bf16[512,256]{1,0:T(8,128)(2,1)S(1)}, u32[]{:S(2)}, u32[]{:S(2)}) %collective-permute-start.10) | collective-permute-done | bytes 262176 | tf_op jit(solution)/shard_map/ppermute | solution.py:318
  82.6 0.0 collective-permute-done.5.a_ref
  82.6 0.0 collective-permute-done.9.c_ref
  82.6 1.1 %finish.1 = f32[2,512,256]{2,1,0:T(8,128)} custom-call(bf16[528,256]{1,0:T(8,128)(2,1)S(1)} %collective-permute-done.5.a_ref, bf16[512,256]{1,0:T(8,128)(2,1)S(1)} %collective-permute-done.8.b_ref, bf16[528,256]{1,0:T(8,128)(2,1)S(1)} %collective-permute-done.9.c_ref, bf16[512,256]{1,0:T(8,128)(2,1)S(1)} %collective-permute-done.10.d_ref, ...), custom_call_target="tpu_custom_call" | custom-call | flops 26214400 | bytes 4194304 | tf_op jit(solution)/shard_map/finish/pallas_call | solution.py:232
  (5 shorter events, 0.0 us)
Async XLA Ops:
  0.0 7.3 %collective-permute-start.1 = (bf16[2,512,1024]{2,1,0:T(8,128)(2,1)}, bf16[2,512,1024]{2,1,0:T(8,128)(2,1)}, u32[]{:S(2)}, u32[]{:S(2)}) collective-permute-start(bf16[2,512,1024]{2,1,0:T(8,128)(2,1)} %own_ref.15), channel_id=1, source_target_pairs={{0,1},{1,0},{2,3},{3,2},{4,5},{5,4},{6,7},{7,6},{8,9},{9,8},{10,11... | collective-permute-start | bytes 6291464 | tf_op jit(solution)/shard_map/ppermute | solution.py:292
  4.6 3.5 %collective-permute-start = (f32[24,128]{1,0:T(8,128)}, f32[24,128]{1,0:T(8,128)S(1)}, u32[]{:S(2)}, u32[]{:S(2)}) collective-permute-start(f32[24,128]{1,0:T(8,128)} %pack.1), channel_id=1, source_target_pairs={{0,0},{1,1},{2,2},{3,3},{4,4},{5,5},{6,6},{7,7},{8,8},{9,9},{10,10... | collective-permute-start | bytes 36872 | tf_op jit(solution)/shard_map/ppermute | solution.py:299
  30.3 11.0 %collective-permute-start.2 = (bf16[528,512]{1,0:T(8,128)(2,1)S(1)}, bf16[528,512]{1,0:T(8,128)(2,1)S(1)}, u32[]{:S(2)}, u32[]{:S(2)}) collective-permute-start(bf16[528,512]{1,0:T(8,128)(2,1)S(1)} %products.8), channel_id=1, source_target_pairs={{0,2},{1,15},{2,4},{3,1},{4,6},{5,3},{6,8},{7,5},{8,10},{9,7},{10,... | collective-permute-start | bytes 1622024 | tf_op jit(solution)/shard_map/ppermute | solution.py:307
  41.4 9.5 %collective-permute-start.3 = (bf16[528,512]{1,0:T(8,128)(2,1)S(1)}, bf16[528,512]{1,0:T(8,128)(2,1)S(1)}, u32[]{:S(2)}, u32[]{:S(2)}) collective-permute-start(bf16[528,512]{1,0:T(8,128)(2,1)S(1)} %add_on.5), channel_id=1, source_target_pairs={{0,2},{1,15},{2,4},{3,1},{4,6},{5,3},{6,8},{7,5},{8,10},{9,7},{10,... | collective-permute-start | bytes 1622024 | tf_op jit(solution)/shard_map/ppermute | solution.py:313
  44.6 11.9 %collective-permute-start.6 = (bf16[512,512]{1,0:T(8,128)(2,1)S(1)}, bf16[512,512]{1,0:T(8,128)(2,1)S(1)}, u32[]{:S(2)}, u32[]{:S(2)}) collective-permute-start(bf16[512,512]{1,0:T(8,128)(2,1)S(1)} %get-tuple-element.45), channel_id=1, source_target_pairs={{0,2},{1,15},{2,4},{3,1},{4,6},{5,3},{6,8},{7,5},{8,10},{9,7},{10,... | collective-permute-start | bytes 1572872 | tf_op jit(solution)/shard_map/ppermute | solution.py:309
  51.0 14.7 %collective-permute-start.4 = (bf16[528,512]{1,0:T(8,128)(2,1)S(1)}, bf16[528,512]{1,0:T(8,128)(2,1)S(1)}, u32[]{:S(2)}, u32[]{:S(2)}) collective-permute-start(bf16[528,512]{1,0:T(8,128)(2,1)S(1)} %add_on.6), channel_id=1, source_target_pairs={{0,2},{1,15},{2,4},{3,1},{4,6},{5,3},{6,8},{7,5},{8,10},{9,7},{10,... | collective-permute-start | bytes 1622024 | tf_op jit(solution)/shard_map/ppermute | solution.py:313
  56.6 13.0 %collective-permute-start.7 = (bf16[512,512]{1,0:T(8,128)(2,1)S(1)}, bf16[512,512]{1,0:T(8,128)(2,1)S(1)}, u32[]{:S(2)}, u32[]{:S(2)}) collective-permute-start(bf16[512,512]{1,0:T(8,128)(2,1)S(1)} %add_on.8), channel_id=1, source_target_pairs={{0,2},{1,15},{2,4},{3,1},{4,6},{5,3},{6,8},{7,5},{8,10},{9,7},{10,... | collective-permute-start | bytes 1572872 | tf_op jit(solution)/shard_map/ppermute | solution.py:317
  65.8 16.8 %collective-permute-start.5 = (bf16[528,256]{1,0:T(8,128)(2,1)S(1)}, bf16[528,256]{1,0:T(8,128)(2,1)S(1)}, u32[]{:S(2)}, u32[]{:S(2)}) collective-permute-start(bf16[528,256]{1,0:T(8,128)(2,1)S(1)} %get-tuple-element.44), channel_id=1, source_target_pairs={{0,2},{1,15},{2,4},{3,1},{4,6},{5,3},{6,8},{7,5},{8,10},{9,7},{10,... | collective-permute-start | bytes 811016 | tf_op jit(solution)/shard_map/ppermute | solution.py:321
  65.9 16.7 %collective-permute-start.9 = (bf16[528,256]{1,0:T(8,128)(2,1)S(1)}, bf16[528,256]{1,0:T(8,128)(2,1)S(1)}, u32[]{:S(2)}, u32[]{:S(2)}) collective-permute-start(bf16[528,256]{1,0:T(8,128)(2,1)S(1)} %get-tuple-element.49), channel_id=1, source_target_pairs={{0,3},{1,14},{2,5},{3,0},{4,7},{5,2},{6,9},{7,4},{8,11},{9,6},{10,... | collective-permute-start | bytes 811016 | tf_op jit(solution)/shard_map/ppermute | solution.py:322
  69.8 9.5 %collective-permute-start.8 = (bf16[512,256]{1,0:T(8,128)(2,1)S(1)}, bf16[512,256]{1,0:T(8,128)(2,1)S(1)}, u32[]{:S(2)}, u32[]{:S(2)}) collective-permute-start(bf16[512,256]{1,0:T(8,128)(2,1)S(1)} %get-tuple-element.48), channel_id=1, source_target_pairs={{0,2},{1,15},{2,4},{3,1},{4,6},{5,3},{6,8},{7,5},{8,10},{9,7},{10,... | collective-permute-start | bytes 786440 | tf_op jit(solution)/shard_map/ppermute | solution.py:317
  71.7 10.9 %collective-permute-start.10 = (bf16[512,256]{1,0:T(8,128)(2,1)S(1)}, bf16[512,256]{1,0:T(8,128)(2,1)S(1)}, u32[]{:S(2)}, u32[]{:S(2)}) collective-permute-start(bf16[512,256]{1,0:T(8,128)(2,1)S(1)} %get-tuple-element.50), channel_id=1, source_target_pairs={{0,3},{1,14},{2,5},{3,0},{4,7},{5,2},{6,9},{7,4},{8,11},{9,6},{10,... | collective-permute-start | bytes 786440 | tf_op jit(solution)/shard_map/ppermute | solution.py:318

commit v4 on v3

--- a/solution.py
+++ b/solution.py
@@ -294,9 +294,11 @@
     for r in range(nrows):
         for k in range(ncols):
             for c in range(ndepth):
-                source = along(c, k, r // 2) * ndepth + (c ^ (r & 1))
+                source = along(c, k, (r or nrows - 1) // 2) * ndepth + (c ^ ((r or nrows - 1) & 1))
                 pairs.append((r * ncols * ndepth + source, r * ncols * ndepth + k * ndepth + c))
-    theirs = lax.ppermute(packed(spectrum, wanted, fraction), ROW + ring, pairs)
+    mine = packed(spectrum, wanted, fraction)
+    theirs = lax.ppermute(mine, ROW + ring, pairs)
+    theirs = jnp.where(lax.axis_index(ROW) == 0, mine, theirs)
     last = lax.axis_index(ROW) == nrows - 1
     edge = [jnp.where(last, h[0, rows - 1], h[1, 0]).astype(F32).reshape(-1, LANES) for h in (halves, other)]
     parcel = jnp.concatenate([theirs] + edge, axis=0)

time: 84.4 us -> 83.4 us (0.988)
  blocking collectives: 19.1 us -> 16.2 us
  waiting for transfers between devices: 6.95 us -> 8.84 us
    all_to_all x1, blocking collectives: 19.1 us -> 16.2 us  [body(): lax.all_to_all(jnp.broadcast_to(parcel[None], (nrows,) + parcel.shape), R...]
    ppermute x1, waiting for transfers between devices: 0.01 us -> 2.56 us  [body(): theirs = lax.ppermute(mine, ROW + ring, pairs)]
    ppermute x1, starting transfers between devices: 1.37 us -> 0.08 us  [body(): theirs = lax.ppermute(mine, ROW + ring, pairs)]
where the time goes in v4:
time: 83.4 us; the launch traced here: 82.8 us
  Pallas kernels  27.6 us (33%)
  starting transfers between devices  27.5 us (33%)
  blocking collectives  16.2 us (19%)
  waiting for transfers between devices  8.84 us (11%)
  other arithmetic  2.23 us (3%)
    pallas_call x8, Pallas kernels, products(): pl.pallas_call(functools.partial(multiply, step=step, which=which, sends=...  24.7 us
    all_to_all x1, blocking collectives, body(): lax.all_to_all(jnp.broadcast_to(parcel[None], (nrows,) + parcel.shape), R...  16.2 us
    ppermute x4, starting transfers between devices, body(): a = lax.ppermute(a, ring, straight)  11.6 us
    ppermute x3, starting transfers between devices, body(): b = lax.ppermute(b, ring, straight)  5.41 us
    ppermute x1, starting transfers between devices, body(): a_across = [lax.ppermute(x, ring, across) for x in a_across]  3.76 us
    ppermute x1, starting transfers between devices, body(): b_across = [lax.ppermute(x, ring, across) for x in b_across]  3.41 us
    ppermute x1, waiting for transfers between devices, body(): b_across = [lax.ppermute(x, ring, across) for x in b_across]  3.32 us
    ppermute x1, starting transfers between devices, body(): other = lax.ppermute(halves, 'depth', [(0, 1), (1, 0)])  3.2 us
  transfers between devices with their start and end apart: 11, of which 5 were waited for; matrix products, arithmetic and copies ran while one was open for 2% of the time, Pallas kernels for 28%

profile of v4, /device:TPU:1, one launch (start us, length us, event | category | flops | bytes accessed | tf_op | source)
XLA Modules:
  0.0 82.8 jit_solution(8844734129131806622)
XLA Ops:
  0.0 3.2 %collective-permute-start.1 = (bf16[2,512,1024]{2,1,0:T(8,128)(2,1)}, bf16[2,512,1024]{2,1,0:T(8,128)(2,1)}, u32[]{:S(2)}, u32[]{:S(2)}) collective-permute-start(bf16[2,512,1024]{2,1,0:T(8,128)(2,1)} %own_ref.15), channel_id=1, source_target_pairs={{0,1},{1,0},{2,3},{3,2},{4,5},{5,4},{6,7},{7,6},{8,9},{9,8},{10,11... | collective-permute-start | bytes 6291464 | tf_op jit(solution)/shard_map/ppermute | solution.py:292
  3.2 1.3 %pack.1 = f32[24,128]{1,0:T(8,128)} custom-call(f32[2,1024]{1,0:T(2,128)} %spectrum_ref.1, s32[1,512]{1,0:T(1,128)} %bitcast.6, f32[1,512]{1,0:T(1,128)} %bitcast.7), custom_call_target="tpu_custom_call" | custom-call | flops 1000 | bytes 400000 | tf_op jit(solution)/shard_map/pack/pallas_call | solution.py:265
  4.6 0.1 collective-permute-start
  4.7 0.7 fusion
  5.4 2.6 %collective-permute-done = f32[24,128]{1,0:T(8,128)S(1)} collective-permute-done((f32[24,128]{1,0:T(8,128)}, f32[24,128]{1,0:T(8,128)S(1)}, u32[]{:S(2)}, u32[]{:S(2)}) %collective-permute-start) | collective-permute-done | bytes 12320 | tf_op jit(solution)/shard_map/ppermute | solution.py:300
  8.0 0.7 broadcast_select_fusion.2
  8.7 0.0 collective-permute-done.1.other_ref
  8.7 0.7 fusion.1
  9.5 16.2 %all_to_all.5.blocks_ref = f32[16,40,128]{2,1,0:T(8,128)S(1)} all-to-all(f32[16,40,128]{2,1,0:T(8,128)S(1)} %broadcast_in_dim.2), channel_id=1, replica_groups=mesh['row_0'=4,'row_1'=4,'col'=8,'depth'=2] {'row_0','row_1'}, dimensions={0} | all-to-all | bytes 655360 | tf_op jit(solution)/shard_map/all_to_all | solution.py:305
  25.7 3.1 %products.8 = bf16[528,512]{1,0:T(8,128)(2,1)S(1)} custom-call(f32[16,40,128]{2,1,0:T(8,128)S(1)} %all_to_all.5.blocks_ref, bf16[2,512,1024]{2,1,0:T(8,128)(2,1)} %own_ref.15, bf16[2,512,1024]{2,1,0:T(8,128)(2,1)} %collective-permute-done.1.other_ref), custom_call_target="tpu_custom_call" | custom-call | flops 1073741824 | bytes 6291456 | tf_op jit(solution)/shard_map/products/pallas_call | solution.py:167
  28.8 5.1 %collective-permute-start.2 = (bf16[528,512]{1,0:T(8,128)(2,1)S(1)}, bf16[528,512]{1,0:T(8,128)(2,1)S(1)}, u32[]{:S(2)}, u32[]{:S(2)}) collective-permute-start(bf16[528,512]{1,0:T(8,128)(2,1)S(1)} %products.8), channel_id=1, source_target_pairs={{0,2},{1,15},{2,4},{3,1},{4,6},{5,3},{6,8},{7,5},{8,10},{9,7},{10,... | collective-permute-start | bytes 1622024 | tf_op jit(solution)/shard_map/ppermute | solution.py:309
  33.9 3.0 %products.9 = (bf16[512,512]{1,0:T(8,128)(2,1)S(1)}, f32[8,512]{1,0:T(8,128)S(1)}, f32[512,128]{1,0:T(8,128)S(1)}, f32[512,128]{1,0:T(8,128)S(1)}) custom-call(f32[16,40,128]{2,1,0:T(8,128)S(1)} %all_to_all.5.blocks_ref, bf16[2,512,1024]{2,1,0:T(8,128)(2,1)} %own_ref.15, bf16[2,512,1024]{2,1,0:T(8,128)(2,1)} %collective-permute-done.1.other_ref), custom_call_target="tpu_custom_call" | custom-call | flops 1073741824 | bytes 6291456 | tf_op jit(solution)/shard_map/products/pallas_call | solution.py:167
  36.9 2.9 %products.10 = (f32[1,512,512]{2,1,0:T(8,128)S(1)}, f32[8,512]{1,0:T(8,128)S(1)}) custom-call(f32[16,40,128]{2,1,0:T(8,128)S(1)} %all_to_all.5.blocks_ref, bf16[2,512,1024]{2,1,0:T(8,128)(2,1)} %own_ref.15, bf16[2,512,1024]{2,1,0:T(8,128)(2,1)} %collective-permute-done.1.other_ref, f32[512,128]{1,0:T(8,128)S(1)} %get-tuple-element.29.refs_0_, ...), custom_call_target="tpu_custom_call" | custom-call | flops 1073741824 | bytes 6291456 | tf_op jit(solution)/shard_map/products/pallas_call | solution.py:167
  39.7 0.5 collective-permute-done.2.refs_0_
  40.2 0.1 add_on.5
  40.3 3.2 %collective-permute-start.3 = (bf16[528,512]{1,0:T(8,128)(2,1)S(1)}, bf16[528,512]{1,0:T(8,128)(2,1)S(1)}, u32[]{:S(2)}, u32[]{:S(2)}) collective-permute-start(bf16[528,512]{1,0:T(8,128)(2,1)S(1)} %add_on.5), channel_id=1, source_target_pairs={{0,2},{1,15},{2,4},{3,1},{4,6},{5,3},{6,8},{7,5},{8,10},{9,7},{10,... | collective-permute-start | bytes 1622024 | tf_op jit(solution)/shard_map/ppermute | solution.py:315
  43.5 0.3 collective-permute-start.6
  43.8 3.0 %products.11 = (f32[1,512,512]{2,1,0:T(8,128)S(1)}, f32[8,512]{1,0:T(8,128)S(1)}, f32[512,128]{1,0:T(8,128)S(1)}, f32[512,128]{1,0:T(8,128)S(1)}) custom-call(f32[16,40,128]{2,1,0:T(8,128)S(1)} %all_to_all.5.blocks_ref, bf16[2,512,1024]{2,1,0:T(8,128)(2,1)} %own_ref.15, bf16[2,512,1024]{2,1,0:T(8,128)(2,1)} %collective-permute-done.1.other_ref), custom_call_target="tpu_custom_call" | custom-call | flops 1073741824 | bytes 6291456 | tf_op jit(solution)/shard_map/products/pallas_call | solution.py:167
  46.8 2.9 %products.12 = (f32[1,512,512]{2,1,0:T(8,128)S(1)}, f32[8,512]{1,0:T(8,128)S(1)}) custom-call(f32[16,40,128]{2,1,0:T(8,128)S(1)} %all_to_all.5.blocks_ref, bf16[2,512,1024]{2,1,0:T(8,128)(2,1)} %own_ref.15, bf16[2,512,1024]{2,1,0:T(8,128)(2,1)} %collective-permute-done.1.other_ref, f32[512,128]{1,0:T(8,128)S(1)} %get-tuple-element.34.refs_0_, ...), custom_call_target="tpu_custom_call" | custom-call | flops 1073741824 | bytes 6291456 | tf_op jit(solution)/shard_map/products/pallas_call | solution.py:167
  49.6 0.2 collective-permute-done.3.refs_0_
  49.8 0.1 add_on.6
  49.9 3.2 %collective-permute-start.4 = (bf16[528,512]{1,0:T(8,128)(2,1)S(1)}, bf16[528,512]{1,0:T(8,128)(2,1)S(1)}, u32[]{:S(2)}, u32[]{:S(2)}) collective-permute-start(bf16[528,512]{1,0:T(8,128)(2,1)S(1)} %add_on.6), channel_id=1, source_target_pairs={{0,2},{1,15},{2,4},{3,1},{4,6},{5,3},{6,8},{7,5},{8,10},{9,7},{10,... | collective-permute-start | bytes 1622024 | tf_op jit(solution)/shard_map/ppermute | solution.py:315
  53.1 2.3 %collective-permute-done.6.refs_0_ = bf16[512,512]{1,0:T(8,128)(2,1)S(1)} collective-permute-done((bf16[512,512]{1,0:T(8,128)(2,1)S(1)}, bf16[512,512]{1,0:T(8,128)(2,1)S(1)}, u32[]{:S(2)}, u32[]{:S(2)}) %collective-permute-start.6) | collective-permute-done | bytes 524320 | tf_op jit(solution)/shard_map/ppermute | solution.py:311
  55.4 0.1 add_on.8
  55.5 3.2 %collective-permute-start.7 = (bf16[512,512]{1,0:T(8,128)(2,1)S(1)}, bf16[512,512]{1,0:T(8,128)(2,1)S(1)}, u32[]{:S(2)}, u32[]{:S(2)}) collective-permute-start(bf16[512,512]{1,0:T(8,128)(2,1)S(1)} %add_on.8), channel_id=1, source_target_pairs={{0,2},{1,15},{2,4},{3,1},{4,6},{5,3},{6,8},{7,5},{8,10},{9,7},{10,... | collective-permute-start | bytes 1572872 | tf_op jit(solution)/shard_map/ppermute | solution.py:319
  58.7 3.0 %products.13 = (f32[1,512,512]{2,1,0:T(8,128)S(1)}, f32[8,512]{1,0:T(8,128)S(1)}, f32[512,128]{1,0:T(8,128)S(1)}, f32[512,128]{1,0:T(8,128)S(1)}) custom-call(f32[16,40,128]{2,1,0:T(8,128)S(1)} %all_to_all.5.blocks_ref, bf16[2,512,1024]{2,1,0:T(8,128)(2,1)} %own_ref.15, bf16[2,512,1024]{2,1,0:T(8,128)(2,1)} %collective-permute-done.1.other_ref), custom_call_target="tpu_custom_call" | custom-call | flops 1073741824 | bytes 6291456 | tf_op jit(solution)/shard_map/products/pallas_call | solution.py:167
  61.7 2.9 %products.14 = (f32[1,512,512]{2,1,0:T(8,128)S(1)}, f32[8,512]{1,0:T(8,128)S(1)}) custom-call(f32[16,40,128]{2,1,0:T(8,128)S(1)} %all_to_all.5.blocks_ref, bf16[2,512,1024]{2,1,0:T(8,128)(2,1)} %own_ref.15, bf16[2,512,1024]{2,1,0:T(8,128)(2,1)} %collective-permute-done.1.other_ref, f32[512,128]{1,0:T(8,128)S(1)} %get-tuple-element.39.refs_0_, ...), custom_call_target="tpu_custom_call" | custom-call | flops 1073741824 | bytes 6291456 | tf_op jit(solution)/shard_map/products/pallas_call | solution.py:167
  64.6 0.0 collective-permute-done.4.refs_0_
  64.6 0.1 add_on.7
  64.7 0.1 collective-permute-start.5
  64.8 3.8 %collective-permute-start.9 = (bf16[528,256]{1,0:T(8,128)(2,1)S(1)}, bf16[528,256]{1,0:T(8,128)(2,1)S(1)}, u32[]{:S(2)}, u32[]{:S(2)}) collective-permute-start(bf16[528,256]{1,0:T(8,128)(2,1)S(1)} %get-tuple-element.49), channel_id=1, source_target_pairs={{0,3},{1,14},{2,5},{3,0},{4,7},{5,2},{6,9},{7,4},{8,11},{9,6},{10,... | collective-permute-start | bytes 811016 | tf_op jit(solution)/shard_map/ppermute | solution.py:324
  68.6 0.0 collective-permute-done.7.refs_0_
  68.6 0.1 add_on.9
  68.7 1.9 %collective-permute-start.8 = (bf16[512,256]{1,0:T(8,128)(2,1)S(1)}, bf16[512,256]{1,0:T(8,128)(2,1)S(1)}, u32[]{:S(2)}, u32[]{:S(2)}) collective-permute-start(bf16[512,256]{1,0:T(8,128)(2,1)S(1)} %get-tuple-element.48), channel_id=1, source_target_pairs={{0,2},{1,15},{2,4},{3,1},{4,6},{5,3},{6,8},{7,5},{8,10},{9,7},{10,... | collective-permute-start | bytes 786440 | tf_op jit(solution)/shard_map/ppermute | solution.py:319
  70.6 3.4 %collective-permute-start.10 = (bf16[512,256]{1,0:T(8,128)(2,1)S(1)}, bf16[512,256]{1,0:T(8,128)(2,1)S(1)}, u32[]{:S(2)}, u32[]{:S(2)}) collective-permute-start(bf16[512,256]{1,0:T(8,128)(2,1)S(1)} %get-tuple-element.50), channel_id=1, source_target_pairs={{0,3},{1,14},{2,5},{3,0},{4,7},{5,2},{6,9},{7,4},{8,11},{9,6},{10,... | collective-permute-start | bytes 786440 | tf_op jit(solution)/shard_map/ppermute | solution.py:320
  74.1 4.1 %products.15 = (f32[2,512,256]{2,1,0:T(8,128)S(1)}, f32[8,256]{1,0:T(8,128)S(1)}) custom-call(f32[16,40,128]{2,1,0:T(8,128)S(1)} %all_to_all.5.blocks_ref, bf16[2,512,1024]{2,1,0:T(8,128)(2,1)} %own_ref.15, bf16[2,512,1024]{2,1,0:T(8,128)(2,1)} %collective-permute-done.1.other_ref), custom_call_target="tpu_custom_call" | custom-call | flops 1073741824 | bytes 12582912 | tf_op jit(solution)/shard_map/products/pallas_call | solution.py:167
  78.2 0.0 collective-permute-done.8.b_ref
  78.2 3.3 %collective-permute-done.10.d_ref = bf16[512,256]{1,0:T(8,128)(2,1)S(1)} collective-permute-done((bf16[512,256]{1,0:T(8,128)(2,1)S(1)}, bf16[512,256]{1,0:T(8,128)(2,1)S(1)}, u32[]{:S(2)}, u32[]{:S(2)}) %collective-permute-start.10) | collective-permute-done | bytes 262176 | tf_op jit(solution)/shard_map/ppermute | solution.py:320
  81.5 0.0 collective-permute-done.5.a_ref
  81.5 0.0 collective-permute-done.9.c_ref
  81.5 1.1 %finish.1 = f32[2,512,256]{2,1,0:T(8,128)} custom-call(bf16[528,256]{1,0:T(8,128)(2,1)S(1)} %collective-permute-done.5.a_ref, bf16[512,256]{1,0:T(8,128)(2,1)S(1)} %collective-permute-done.8.b_ref, bf16[528,256]{1,0:T(8,128)(2,1)S(1)} %collective-permute-done.9.c_ref, bf16[512,256]{1,0:T(8,128)(2,1)S(1)} %collective-permute-done.10.d_ref, ...), custom_call_target="tpu_custom_call" | custom-call | flops 26214400 | bytes 4194304 | tf_op jit(solution)/shard_map/finish/pallas_call | solution.py:232
  (5 shorter events, 0.0 us)
Async XLA Ops:
  0.0 8.7 %collective-permute-start.1 = (bf16[2,512,1024]{2,1,0:T(8,128)(2,1)}, bf16[2,512,1024]{2,1,0:T(8,128)(2,1)}, u32[]{:S(2)}, u32[]{:S(2)}) collective-permute-start(bf16[2,512,1024]{2,1,0:T(8,128)(2,1)} %own_ref.15), channel_id=1, source_target_pairs={{0,1},{1,0},{2,3},{3,2},{4,5},{5,4},{6,7},{7,6},{8,9},{9,8},{10,11... | collective-permute-start | bytes 6291464 | tf_op jit(solution)/shard_map/ppermute | solution.py:292
  4.6 3.4 %collective-permute-start = (f32[24,128]{1,0:T(8,128)}, f32[24,128]{1,0:T(8,128)S(1)}, u32[]{:S(2)}, u32[]{:S(2)}) collective-permute-start(f32[24,128]{1,0:T(8,128)} %pack.1), channel_id=1, source_target_pairs={{15,0},{2,1},{1,2},{4,3},{3,4},{6,5},{5,6},{8,7},{7,8},{10,9},{9,1... | collective-permute-start | bytes 36872 | tf_op jit(solution)/shard_map/ppermute | solution.py:300
  28.8 11.4 %collective-permute-start.2 = (bf16[528,512]{1,0:T(8,128)(2,1)S(1)}, bf16[528,512]{1,0:T(8,128)(2,1)S(1)}, u32[]{:S(2)}, u32[]{:S(2)}) collective-permute-start(bf16[528,512]{1,0:T(8,128)(2,1)S(1)} %products.8), channel_id=1, source_target_pairs={{0,2},{1,15},{2,4},{3,1},{4,6},{5,3},{6,8},{7,5},{8,10},{9,7},{10,... | collective-permute-start | bytes 1622024 | tf_op jit(solution)/shard_map/ppermute | solution.py:309
  40.3 9.5 %collective-permute-start.3 = (bf16[528,512]{1,0:T(8,128)(2,1)S(1)}, bf16[528,512]{1,0:T(8,128)(2,1)S(1)}, u32[]{:S(2)}, u32[]{:S(2)}) collective-permute-start(bf16[528,512]{1,0:T(8,128)(2,1)S(1)} %add_on.5), channel_id=1, source_target_pairs={{0,2},{1,15},{2,4},{3,1},{4,6},{5,3},{6,8},{7,5},{8,10},{9,7},{10,... | collective-permute-start | bytes 1622024 | tf_op jit(solution)/shard_map/ppermute | solution.py:315
  43.5 11.9 %collective-permute-start.6 = (bf16[512,512]{1,0:T(8,128)(2,1)S(1)}, bf16[512,512]{1,0:T(8,128)(2,1)S(1)}, u32[]{:S(2)}, u32[]{:S(2)}) collective-permute-start(bf16[512,512]{1,0:T(8,128)(2,1)S(1)} %get-tuple-element.45), channel_id=1, source_target_pairs={{0,2},{1,15},{2,4},{3,1},{4,6},{5,3},{6,8},{7,5},{8,10},{9,7},{10,... | collective-permute-start | bytes 1572872 | tf_op jit(solution)/shard_map/ppermute | solution.py:311
  49.9 14.7 %collective-permute-start.4 = (bf16[528,512]{1,0:T(8,128)(2,1)S(1)}, bf16[528,512]{1,0:T(8,128)(2,1)S(1)}, u32[]{:S(2)}, u32[]{:S(2)}) collective-permute-start(bf16[528,512]{1,0:T(8,128)(2,1)S(1)} %add_on.6), channel_id=1, source_target_pairs={{0,2},{1,15},{2,4},{3,1},{4,6},{5,3},{6,8},{7,5},{8,10},{9,7},{10,... | collective-permute-start | bytes 1622024 | tf_op jit(solution)/shard_map/ppermute | solution.py:315
  55.5 13.0 %collective-permute-start.7 = (bf16[512,512]{1,0:T(8,128)(2,1)S(1)}, bf16[512,512]{1,0:T(8,128)(2,1)S(1)}, u32[]{:S(2)}, u32[]{:S(2)}) collective-permute-start(bf16[512,512]{1,0:T(8,128)(2,1)S(1)} %add_on.8), channel_id=1, source_target_pairs={{0,2},{1,15},{2,4},{3,1},{4,6},{5,3},{6,8},{7,5},{8,10},{9,7},{10,... | collective-permute-start | bytes 1572872 | tf_op jit(solution)/shard_map/ppermute | solution.py:319
  64.7 16.8 %collective-permute-start.5 = (bf16[528,256]{1,0:T(8,128)(2,1)S(1)}, bf16[528,256]{1,0:T(8,128)(2,1)S(1)}, u32[]{:S(2)}, u32[]{:S(2)}) collective-permute-start(bf16[528,256]{1,0:T(8,128)(2,1)S(1)} %get-tuple-element.44), channel_id=1, source_target_pairs={{0,2},{1,15},{2,4},{3,1},{4,6},{5,3},{6,8},{7,5},{8,10},{9,7},{10,... | collective-permute-start | bytes 811016 | tf_op jit(solution)/shard_map/ppermute | solution.py:323
  64.8 16.7 %collective-permute-start.9 = (bf16[528,256]{1,0:T(8,128)(2,1)S(1)}, bf16[528,256]{1,0:T(8,128)(2,1)S(1)}, u32[]{:S(2)}, u32[]{:S(2)}) collective-permute-start(bf16[528,256]{1,0:T(8,128)(2,1)S(1)} %get-tuple-element.49), channel_id=1, source_target_pairs={{0,3},{1,14},{2,5},{3,0},{4,7},{5,2},{6,9},{7,4},{8,11},{9,6},{10,... | collective-permute-start | bytes 811016 | tf_op jit(solution)/shard_map/ppermute | solution.py:324
  68.7 9.5 %collective-permute-start.8 = (bf16[512,256]{1,0:T(8,128)(2,1)S(1)}, bf16[512,256]{1,0:T(8,128)(2,1)S(1)}, u32[]{:S(2)}, u32[]{:S(2)}) collective-permute-start(bf16[512,256]{1,0:T(8,128)(2,1)S(1)} %get-tuple-element.48), channel_id=1, source_target_pairs={{0,2},{1,15},{2,4},{3,1},{4,6},{5,3},{6,8},{7,5},{8,10},{9,7},{10,... | collective-permute-start | bytes 786440 | tf_op jit(solution)/shard_map/ppermute | solution.py:319
  70.6 10.9 %collective-permute-start.10 = (bf16[512,256]{1,0:T(8,128)(2,1)S(1)}, bf16[512,256]{1,0:T(8,128)(2,1)S(1)}, u32[]{:S(2)}, u32[]{:S(2)}) collective-permute-start(bf16[512,256]{1,0:T(8,128)(2,1)S(1)} %get-tuple-element.50), channel_id=1, source_target_pairs={{0,3},{1,14},{2,5},{3,0},{4,7},{5,2},{6,9},{7,4},{8,11},{9,6},{10,... | collective-permute-start | bytes 786440 | tf_op jit(solution)/shard_map/ppermute | solution.py:320

commit v5 on v4

--- a/solution.py
+++ b/solution.py
@@ -18,7 +18,7 @@
 
 def look_up(core, col, blocks_ref, low_ref, shift_ref, *, step, value_rows, count):
     places = blocks_ref.shape[0]
-    table = blocks_ref[:, :value_rows, :].reshape(places * value_rows, LANES)
+    table = blocks_ref[:, :value_rows, :].reshape(places * value_rows, LANES) * 0.25
     high = table.astype(BF16)
     rest = table - high.astype(F32)
     middle = rest.astype(BF16)
@@ -47,7 +47,7 @@
     for tile in range(count):
         picks = [jnp.where(row_ids == spots[:, k + tile : k + tile + 1], 1.0, 0.0).astype(BF16) for k in (0, 8)]
         got = jnp.dot(jnp.concatenate(picks, axis=0), split, preferred_element_type=F32)
-        got = (got[:, :LANES] + got[:, LANES : 2 * LANES]) + got[:, 2 * LANES :]
+        got = ((got[:, :LANES] + got[:, LANES : 2 * LANES]) + got[:, 2 * LANES :]) * 4.0
         lower, upper = (
             jnp.sum(jnp.where(lane_ids == spots[:, k + tile : k + tile + 1], got[at : at + LANES], 0.0), axis=1, keepdims=True)
             for k, at in ((4, 0), (12, LANES))
@@ -264,7 +264,7 @@
     rows = sum(x.size for x in arrays) // LANES
     return pl.pallas_call(
         pack,
-        out_shape=jax.ShapeDtypeStruct((rows, LANES), F32),
+        out_shape=pltpu.VMEM((rows, LANES), F32),
         in_specs=[HBM] * 3,
         out_specs=VMEM,
         scratch_shapes=[pltpu.VMEM(x.shape, x.dtype) for x in arrays] + [pltpu.SemaphoreType.DMA((3,))],

time: 83.4 us -> 82.4 us (0.988)
  transfers between devices with their start and end apart: 11 -> 11, of which waited for: 5 -> 6; matrix products, arithmetic and copies ran while one was open for 2% -> 1% of each run, Pallas kernels for 28% -> 28%
where the time goes in v5:
time: 82.4 us; the launch traced here: 81.9 us
  starting transfers between devices  27.5 us (33%)
  Pallas kernels  27 us (33%)
  blocking collectives  16.7 us (20%)
  waiting for transfers between devices  8.81 us (11%)
  other arithmetic  1.52 us (2%)
    pallas_call x8, Pallas kernels, products(): pl.pallas_call(functools.partial(multiply, step=step, which=which, sends=...  24.6 us
    all_to_all x1, blocking collectives, body(): lax.all_to_all(jnp.broadcast_to(parcel[None], (nrows,) + parcel.shape), R...  16.7 us
    ppermute x4, starting transfers between devices, body(): a = lax.ppermute(a, ring, straight)  11.6 us
    ppermute x3, starting transfers between devices, body(): b = lax.ppermute(b, ring, straight)  5.41 us
    ppermute x1, starting transfers between devices, body(): a_across = [lax.ppermute(x, ring, across) for x in a_across]  3.77 us
    ppermute x1, starting transfers between devices, body(): b_across = [lax.ppermute(x, ring, across) for x in b_across]  3.4 us
    ppermute x1, waiting for transfers between devices, body(): b_across = [lax.ppermute(x, ring, across) for x in b_across]  3.32 us
    ppermute x1, starting transfers between devices, body(): other = lax.ppermute(halves, 'depth', [(0, 1), (1, 0)])  3.2 us
  transfers between devices with their start and end apart: 11, of which 6 were waited for; matrix products, arithmetic and copies ran while one was open for 1% of the time, Pallas kernels for 28%

profile of v5, /device:TPU:1, one launch (start us, length us, event | category | flops | bytes accessed | tf_op | source)
XLA Modules:
  0.0 81.9 jit_solution(1805558617636104524)
XLA Ops:
  0.0 3.2 %collective-permute-start.1 = (bf16[2,512,1024]{2,1,0:T(8,128)(2,1)}, bf16[2,512,1024]{2,1,0:T(8,128)(2,1)}, u32[]{:S(2)}, u32[]{:S(2)}) collective-permute-start(bf16[2,512,1024]{2,1,0:T(8,128)(2,1)} %own_ref.15), channel_id=1, source_target_pairs={{0,1},{1,0},{2,3},{3,2},{4,5},{5,4},{6,7},{7,6},{8,9},{9,8},{10,11... | collective-permute-start | bytes 6291464 | tf_op jit(solution)/shard_map/ppermute | solution.py:292
  3.2 0.7 pack.1
  4.0 0.1 collective-permute-start
  4.1 0.7 fusion
  4.8 2.3 %collective-permute-done = f32[24,128]{1,0:T(8,128)S(1)} collective-permute-done((f32[24,128]{1,0:T(8,128)S(1)}, f32[24,128]{1,0:T(8,128)S(1)}, u32[]{:S(2)}, u32[]{:S(2)}) %collective-permute-start) | collective-permute-done | bytes 12320 | tf_op jit(solution)/shard_map/ppermute | solution.py:300
  7.2 0.2 collective-permute-done.1.other_ref
  7.3 0.7 fusion.1
  8.1 16.7 %all_to_all.5.blocks_ref = f32[16,40,128]{2,1,0:T(8,128)S(1)} all-to-all(f32[16,40,128]{2,1,0:T(8,128)S(1)} %broadcast_in_dim.2), channel_id=1, replica_groups=mesh['row_0'=4,'row_1'=4,'col'=8,'depth'=2] {'row_0','row_1'}, dimensions={0} | all-to-all | bytes 655360 | tf_op jit(solution)/shard_map/all_to_all | solution.py:305
  24.9 3.1 %products.8 = bf16[528,512]{1,0:T(8,128)(2,1)S(1)} custom-call(f32[16,40,128]{2,1,0:T(8,128)S(1)} %all_to_all.5.blocks_ref, bf16[2,512,1024]{2,1,0:T(8,128)(2,1)} %own_ref.15, bf16[2,512,1024]{2,1,0:T(8,128)(2,1)} %collective-permute-done.1.other_ref), custom_call_target="tpu_custom_call" | custom-call | flops 1073741824 | bytes 6291456 | tf_op jit(solution)/shard_map/products/pallas_call | solution.py:167
  27.9 5.1 %collective-permute-start.2 = (bf16[528,512]{1,0:T(8,128)(2,1)S(1)}, bf16[528,512]{1,0:T(8,128)(2,1)S(1)}, u32[]{:S(2)}, u32[]{:S(2)}) collective-permute-start(bf16[528,512]{1,0:T(8,128)(2,1)S(1)} %products.8), channel_id=1, source_target_pairs={{0,2},{1,15},{2,4},{3,1},{4,6},{5,3},{6,8},{7,5},{8,10},{9,7},{10,... | collective-permute-start | bytes 1622024 | tf_op jit(solution)/shard_map/ppermute | solution.py:309
  33.0 3.0 %products.9 = (bf16[512,512]{1,0:T(8,128)(2,1)S(1)}, f32[8,512]{1,0:T(8,128)S(1)}, f32[512,128]{1,0:T(8,128)S(1)}, f32[512,128]{1,0:T(8,128)S(1)}) custom-call(f32[16,40,128]{2,1,0:T(8,128)S(1)} %all_to_all.5.blocks_ref, bf16[2,512,1024]{2,1,0:T(8,128)(2,1)} %own_ref.15, bf16[2,512,1024]{2,1,0:T(8,128)(2,1)} %collective-permute-done.1.other_ref), custom_call_target="tpu_custom_call" | custom-call | flops 1073741824 | bytes 6291456 | tf_op jit(solution)/shard_map/products/pallas_call | solution.py:167
  36.0 2.8 %products.10 = (f32[1,512,512]{2,1,0:T(8,128)S(1)}, f32[8,512]{1,0:T(8,128)S(1)}) custom-call(f32[16,40,128]{2,1,0:T(8,128)S(1)} %all_to_all.5.blocks_ref, bf16[2,512,1024]{2,1,0:T(8,128)(2,1)} %own_ref.15, bf16[2,512,1024]{2,1,0:T(8,128)(2,1)} %collective-permute-done.1.other_ref, f32[512,128]{1,0:T(8,128)S(1)} %get-tuple-element.29.refs_0_, ...), custom_call_target="tpu_custom_call" | custom-call | flops 1073741824 | bytes 6291456 | tf_op jit(solution)/shard_map/products/pallas_call | solution.py:167
  38.9 0.5 collective-permute-done.2.refs_0_
  39.3 0.1 add_on.5
  39.5 3.2 %collective-permute-start.3 = (bf16[528,512]{1,0:T(8,128)(2,1)S(1)}, bf16[528,512]{1,0:T(8,128)(2,1)S(1)}, u32[]{:S(2)}, u32[]{:S(2)}) collective-permute-start(bf16[528,512]{1,0:T(8,128)(2,1)S(1)} %add_on.5), channel_id=1, source_target_pairs={{0,2},{1,15},{2,4},{3,1},{4,6},{5,3},{6,8},{7,5},{8,10},{9,7},{10,... | collective-permute-start | bytes 1622024 | tf_op jit(solution)/shard_map/ppermute | solution.py:315
  42.6 0.3 collective-permute-start.6
  42.9 3.0 %products.11 = (f32[1,512,512]{2,1,0:T(8,128)S(1)}, f32[8,512]{1,0:T(8,128)S(1)}, f32[512,128]{1,0:T(8,128)S(1)}, f32[512,128]{1,0:T(8,128)S(1)}) custom-call(f32[16,40,128]{2,1,0:T(8,128)S(1)} %all_to_all.5.blocks_ref, bf16[2,512,1024]{2,1,0:T(8,128)(2,1)} %own_ref.15, bf16[2,512,1024]{2,1,0:T(8,128)(2,1)} %collective-permute-done.1.other_ref), custom_call_target="tpu_custom_call" | custom-call | flops 1073741824 | bytes 6291456 | tf_op jit(solution)/shard_map/products/pallas_call | solution.py:167
  45.9 2.8 %products.12 = (f32[1,512,512]{2,1,0:T(8,128)S(1)}, f32[8,512]{1,0:T(8,128)S(1)}) custom-call(f32[16,40,128]{2,1,0:T(8,128)S(1)} %all_to_all.5.blocks_ref, bf16[2,512,1024]{2,1,0:T(8,128)(2,1)} %own_ref.15, bf16[2,512,1024]{2,1,0:T(8,128)(2,1)} %collective-permute-done.1.other_ref, f32[512,128]{1,0:T(8,128)S(1)} %get-tuple-element.34.refs_0_, ...), custom_call_target="tpu_custom_call" | custom-call | flops 1073741824 | bytes 6291456 | tf_op jit(solution)/shard_map/products/pallas_call | solution.py:167
  48.8 0.2 collective-permute-done.3.refs_0_
  48.9 0.1 add_on.6
  49.1 3.2 %collective-permute-start.4 = (bf16[528,512]{1,0:T(8,128)(2,1)S(1)}, bf16[528,512]{1,0:T(8,128)(2,1)S(1)}, u32[]{:S(2)}, u32[]{:S(2)}) collective-permute-start(bf16[528,512]{1,0:T(8,128)(2,1)S(1)} %add_on.6), channel_id=1, source_target_pairs={{0,2},{1,15},{2,4},{3,1},{4,6},{5,3},{6,8},{7,5},{8,10},{9,7},{10,... | collective-permute-start | bytes 1622024 | tf_op jit(solution)/shard_map/ppermute | solution.py:315
  52.2 2.3 %collective-permute-done.6.refs_0_ = bf16[512,512]{1,0:T(8,128)(2,1)S(1)} collective-permute-done((bf16[512,512]{1,0:T(8,128)(2,1)S(1)}, bf16[512,512]{1,0:T(8,128)(2,1)S(1)}, u32[]{:S(2)}, u32[]{:S(2)}) %collective-permute-start.6) | collective-permute-done | bytes 524320 | tf_op jit(solution)/shard_map/ppermute | solution.py:311
  54.6 0.1 add_on.8
  54.7 3.2 %collective-permute-start.7 = (bf16[512,512]{1,0:T(8,128)(2,1)S(1)}, bf16[512,512]{1,0:T(8,128)(2,1)S(1)}, u32[]{:S(2)}, u32[]{:S(2)}) collective-permute-start(bf16[512,512]{1,0:T(8,128)(2,1)S(1)} %add_on.8), channel_id=1, source_target_pairs={{0,2},{1,15},{2,4},{3,1},{4,6},{5,3},{6,8},{7,5},{8,10},{9,7},{10,... | collective-permute-start | bytes 1572872 | tf_op jit(solution)/shard_map/ppermute | solution.py:319
  57.9 3.0 %products.13 = (f32[1,512,512]{2,1,0:T(8,128)S(1)}, f32[8,512]{1,0:T(8,128)S(1)}, f32[512,128]{1,0:T(8,128)S(1)}, f32[512,128]{1,0:T(8,128)S(1)}) custom-call(f32[16,40,128]{2,1,0:T(8,128)S(1)} %all_to_all.5.blocks_ref, bf16[2,512,1024]{2,1,0:T(8,128)(2,1)} %own_ref.15, bf16[2,512,1024]{2,1,0:T(8,128)(2,1)} %collective-permute-done.1.other_ref), custom_call_target="tpu_custom_call" | custom-call | flops 1073741824 | bytes 6291456 | tf_op jit(solution)/shard_map/products/pallas_call | solution.py:167
  60.9 2.8 %products.14 = (f32[1,512,512]{2,1,0:T(8,128)S(1)}, f32[8,512]{1,0:T(8,128)S(1)}) custom-call(f32[16,40,128]{2,1,0:T(8,128)S(1)} %all_to_all.5.blocks_ref, bf16[2,512,1024]{2,1,0:T(8,128)(2,1)} %own_ref.15, bf16[2,512,1024]{2,1,0:T(8,128)(2,1)} %collective-permute-done.1.other_ref, f32[512,128]{1,0:T(8,128)S(1)} %get-tuple-element.39.refs_0_, ...), custom_call_target="tpu_custom_call" | custom-call | flops 1073741824 | bytes 6291456 | tf_op jit(solution)/shard_map/products/pallas_call | solution.py:167
  63.7 0.0 collective-permute-done.4.refs_0_
  63.7 0.1 add_on.7
  63.9 0.1 collective-permute-start.5
  64.0 3.8 %collective-permute-start.9 = (bf16[528,256]{1,0:T(8,128)(2,1)S(1)}, bf16[528,256]{1,0:T(8,128)(2,1)S(1)}, u32[]{:S(2)}, u32[]{:S(2)}) collective-permute-start(bf16[528,256]{1,0:T(8,128)(2,1)S(1)} %get-tuple-element.49), channel_id=1, source_target_pairs={{0,3},{1,14},{2,5},{3,0},{4,7},{5,2},{6,9},{7,4},{8,11},{9,6},{10,... | collective-permute-start | bytes 811016 | tf_op jit(solution)/shard_map/ppermute | solution.py:324
  67.7 0.0 collective-permute-done.7.refs_0_
  67.7 0.1 add_on.9
  67.9 1.9 %collective-permute-start.8 = (bf16[512,256]{1,0:T(8,128)(2,1)S(1)}, bf16[512,256]{1,0:T(8,128)(2,1)S(1)}, u32[]{:S(2)}, u32[]{:S(2)}) collective-permute-start(bf16[512,256]{1,0:T(8,128)(2,1)S(1)} %get-tuple-element.48), channel_id=1, source_target_pairs={{0,2},{1,15},{2,4},{3,1},{4,6},{5,3},{6,8},{7,5},{8,10},{9,7},{10,... | collective-permute-start | bytes 786440 | tf_op jit(solution)/shard_map/ppermute | solution.py:319
  69.8 3.4 %collective-permute-start.10 = (bf16[512,256]{1,0:T(8,128)(2,1)S(1)}, bf16[512,256]{1,0:T(8,128)(2,1)S(1)}, u32[]{:S(2)}, u32[]{:S(2)}) collective-permute-start(bf16[512,256]{1,0:T(8,128)(2,1)S(1)} %get-tuple-element.50), channel_id=1, source_target_pairs={{0,3},{1,14},{2,5},{3,0},{4,7},{5,2},{6,9},{7,4},{8,11},{9,6},{10,... | collective-permute-start | bytes 786440 | tf_op jit(solution)/shard_map/ppermute | solution.py:320
  73.2 4.1 %products.15 = (f32[2,512,256]{2,1,0:T(8,128)S(1)}, f32[8,256]{1,0:T(8,128)S(1)}) custom-call(f32[16,40,128]{2,1,0:T(8,128)S(1)} %all_to_all.5.blocks_ref, bf16[2,512,1024]{2,1,0:T(8,128)(2,1)} %own_ref.15, bf16[2,512,1024]{2,1,0:T(8,128)(2,1)} %collective-permute-done.1.other_ref), custom_call_target="tpu_custom_call" | custom-call | flops 1073741824 | bytes 12582912 | tf_op jit(solution)/shard_map/products/pallas_call | solution.py:167
  77.3 0.0 collective-permute-done.8.b_ref
  77.3 3.3 %collective-permute-done.10.d_ref = bf16[512,256]{1,0:T(8,128)(2,1)S(1)} collective-permute-done((bf16[512,256]{1,0:T(8,128)(2,1)S(1)}, bf16[512,256]{1,0:T(8,128)(2,1)S(1)}, u32[]{:S(2)}, u32[]{:S(2)}) %collective-permute-start.10) | collective-permute-done | bytes 262176 | tf_op jit(solution)/shard_map/ppermute | solution.py:320
  80.7 0.0 collective-permute-done.5.a_ref
  80.7 0.0 collective-permute-done.9.c_ref
  80.7 1.1 %finish.1 = f32[2,512,256]{2,1,0:T(8,128)} custom-call(bf16[528,256]{1,0:T(8,128)(2,1)S(1)} %collective-permute-done.5.a_ref, bf16[512,256]{1,0:T(8,128)(2,1)S(1)} %collective-permute-done.8.b_ref, bf16[528,256]{1,0:T(8,128)(2,1)S(1)} %collective-permute-done.9.c_ref, bf16[512,256]{1,0:T(8,128)(2,1)S(1)} %collective-permute-done.10.d_ref, ...), custom_call_target="tpu_custom_call" | custom-call | flops 26214400 | bytes 4194304 | tf_op jit(solution)/shard_map/finish/pallas_call | solution.py:232
  (6 shorter events, 0.0 us)
Async XLA Ops:
  0.0 7.3 %collective-permute-start.1 = (bf16[2,512,1024]{2,1,0:T(8,128)(2,1)}, bf16[2,512,1024]{2,1,0:T(8,128)(2,1)}, u32[]{:S(2)}, u32[]{:S(2)}) collective-permute-start(bf16[2,512,1024]{2,1,0:T(8,128)(2,1)} %own_ref.15), channel_id=1, source_target_pairs={{0,1},{1,0},{2,3},{3,2},{4,5},{5,4},{6,7},{7,6},{8,9},{9,8},{10,11... | collective-permute-start | bytes 6291464 | tf_op jit(solution)/shard_map/ppermute | solution.py:292
  4.0 3.2 %collective-permute-start = (f32[24,128]{1,0:T(8,128)S(1)}, f32[24,128]{1,0:T(8,128)S(1)}, u32[]{:S(2)}, u32[]{:S(2)}) collective-permute-start(f32[24,128]{1,0:T(8,128)S(1)} %pack.1), channel_id=1, source_target_pairs={{15,0},{2,1},{1,2},{4,3},{3,4},{6,5},{5,6},{8,7},{7,8},{10,9},{9,1... | collective-permute-start | bytes 36872 | tf_op jit(solution)/shard_map/ppermute | solution.py:300
  27.9 11.4 %collective-permute-start.2 = (bf16[528,512]{1,0:T(8,128)(2,1)S(1)}, bf16[528,512]{1,0:T(8,128)(2,1)S(1)}, u32[]{:S(2)}, u32[]{:S(2)}) collective-permute-start(bf16[528,512]{1,0:T(8,128)(2,1)S(1)} %products.8), channel_id=1, source_target_pairs={{0,2},{1,15},{2,4},{3,1},{4,6},{5,3},{6,8},{7,5},{8,10},{9,7},{10,... | collective-permute-start | bytes 1622024 | tf_op jit(solution)/shard_map/ppermute | solution.py:309
  39.5 9.5 %collective-permute-start.3 = (bf16[528,512]{1,0:T(8,128)(2,1)S(1)}, bf16[528,512]{1,0:T(8,128)(2,1)S(1)}, u32[]{:S(2)}, u32[]{:S(2)}) collective-permute-start(bf16[528,512]{1,0:T(8,128)(2,1)S(1)} %add_on.5), channel_id=1, source_target_pairs={{0,2},{1,15},{2,4},{3,1},{4,6},{5,3},{6,8},{7,5},{8,10},{9,7},{10,... | collective-permute-start | bytes 1622024 | tf_op jit(solution)/shard_map/ppermute | solution.py:315
  42.6 11.9 %collective-permute-start.6 = (bf16[512,512]{1,0:T(8,128)(2,1)S(1)}, bf16[512,512]{1,0:T(8,128)(2,1)S(1)}, u32[]{:S(2)}, u32[]{:S(2)}) collective-permute-start(bf16[512,512]{1,0:T(8,128)(2,1)S(1)} %get-tuple-element.45), channel_id=1, source_target_pairs={{0,2},{1,15},{2,4},{3,1},{4,6},{5,3},{6,8},{7,5},{8,10},{9,7},{10,... | collective-permute-start | bytes 1572872 | tf_op jit(solution)/shard_map/ppermute | solution.py:311
  49.1 14.7 %collective-permute-start.4 = (bf16[528,512]{1,0:T(8,128)(2,1)S(1)}, bf16[528,512]{1,0:T(8,128)(2,1)S(1)}, u32[]{:S(2)}, u32[]{:S(2)}) collective-permute-start(bf16[528,512]{1,0:T(8,128)(2,1)S(1)} %add_on.6), channel_id=1, source_target_pairs={{0,2},{1,15},{2,4},{3,1},{4,6},{5,3},{6,8},{7,5},{8,10},{9,7},{10,... | collective-permute-start | bytes 1622024 | tf_op jit(solution)/shard_map/ppermute | solution.py:315
  54.7 13.0 %collective-permute-start.7 = (bf16[512,512]{1,0:T(8,128)(2,1)S(1)}, bf16[512,512]{1,0:T(8,128)(2,1)S(1)}, u32[]{:S(2)}, u32[]{:S(2)}) collective-permute-start(bf16[512,512]{1,0:T(8,128)(2,1)S(1)} %add_on.8), channel_id=1, source_target_pairs={{0,2},{1,15},{2,4},{3,1},{4,6},{5,3},{6,8},{7,5},{8,10},{9,7},{10,... | collective-permute-start | bytes 1572872 | tf_op jit(solution)/shard_map/ppermute | solution.py:319
  63.9 16.8 %collective-permute-start.5 = (bf16[528,256]{1,0:T(8,128)(2,1)S(1)}, bf16[528,256]{1,0:T(8,128)(2,1)S(1)}, u32[]{:S(2)}, u32[]{:S(2)}) collective-permute-start(bf16[528,256]{1,0:T(8,128)(2,1)S(1)} %get-tuple-element.44), channel_id=1, source_target_pairs={{0,2},{1,15},{2,4},{3,1},{4,6},{5,3},{6,8},{7,5},{8,10},{9,7},{10,... | collective-permute-start | bytes 811016 | tf_op jit(solution)/shard_map/ppermute | solution.py:323
  64.0 16.7 %collective-permute-start.9 = (bf16[528,256]{1,0:T(8,128)(2,1)S(1)}, bf16[528,256]{1,0:T(8,128)(2,1)S(1)}, u32[]{:S(2)}, u32[]{:S(2)}) collective-permute-start(bf16[528,256]{1,0:T(8,128)(2,1)S(1)} %get-tuple-element.49), channel_id=1, source_target_pairs={{0,3},{1,14},{2,5},{3,0},{4,7},{5,2},{6,9},{7,4},{8,11},{9,6},{10,... | collective-permute-start | bytes 811016 | tf_op jit(solution)/shard_map/ppermute | solution.py:324
  67.9 9.5 %collective-permute-start.8 = (bf16[512,256]{1,0:T(8,128)(2,1)S(1)}, bf16[512,256]{1,0:T(8,128)(2,1)S(1)}, u32[]{:S(2)}, u32[]{:S(2)}) collective-permute-start(bf16[512,256]{1,0:T(8,128)(2,1)S(1)} %get-tuple-element.48), channel_id=1, source_target_pairs={{0,2},{1,15},{2,4},{3,1},{4,6},{5,3},{6,8},{7,5},{8,10},{9,7},{10,... | collective-permute-start | bytes 786440 | tf_op jit(solution)/shard_map/ppermute | solution.py:319
  69.8 10.9 %collective-permute-start.10 = (bf16[512,256]{1,0:T(8,128)(2,1)S(1)}, bf16[512,256]{1,0:T(8,128)(2,1)S(1)}, u32[]{:S(2)}, u32[]{:S(2)}) collective-permute-start(bf16[512,256]{1,0:T(8,128)(2,1)S(1)} %get-tuple-element.50), channel_id=1, source_target_pairs={{0,3},{1,14},{2,5},{3,0},{4,7},{5,2},{6,9},{7,4},{8,11},{9,6},{10,... | collective-permute-start | bytes 786440 | tf_op jit(solution)/shard_map/ppermute | solution.py:320
